TPU v7x, 32 devices: a whole 2x2x4 slice. The times are simulated.
32 devices in a mesh: fsdp: 32 (over z, y, x, core).
Axes of the slice: x: 2, y: 2, z: 4, core: 2. Of those that a mesh axis runs over, the one named last changes fastest.
Arguments:
- token_ids: int32 [128, 384], P('fsdp')
- tok_table: bfloat16 [501248, 768], P('fsdp')
- pos_table: bfloat16 [512, 768], replicated
- type_row: bfloat16 [768], replicated
- emb_gain: float32 [768], P('fsdp')
- emb_bias: float32 [768], P('fsdp')
- w_qkv: bfloat16 [768, 2304], P(None, 'fsdp')
- b_qkv: float32 [2304], P('fsdp')
- w_out: bfloat16 [12, 64, 768], P(None, None, 'fsdp')
- b_out: float32 [768], P('fsdp')
- ln1_gain: float32 [768], P('fsdp')
- ln1_bias: float32 [768], P('fsdp')
- w_ffn_in: bfloat16 [768, 3072], P(None, 'fsdp')
- b_ffn_in: float32 [3072], P('fsdp')
- w_ffn_out: bfloat16 [3072, 768], P('fsdp')
- b_ffn_out: float32 [768], P('fsdp')
- ln2_gain: float32 [768], P('fsdp')
- ln2_bias: float32 [768], P('fsdp')
Outputs:
- output: bfloat16 [128, 384, 768], P('fsdp')
All inputs are finite; a program needn't handle non-finite values.
Results may differ from a plain program's by a relative error of at most 0.00883599.
Values are sent between devices in bfloat16 or wider.
A program may use at most 1 GiB of HBM per device.

v0:
```python
import jax
import jax.numpy as jnp
from jax import lax
from jax.sharding import PartitionSpec as P

PAD_ID = 1
LN_EPS = 1e-5


def layer_norm(values, ln_gain, ln_shift):
    row_mean = jnp.mean(values, axis=-1, keepdims=True)
    centered = values - row_mean
    row_var = jnp.mean(centered * centered, axis=-1, keepdims=True)
    return centered * lax.rsqrt(row_var + LN_EPS) * ln_gain + ln_shift


def attention(qkv_heads, keep_mask, head_dim):
    scores = jnp.einsum('bqhd,bkhd->bhqk', qkv_heads[:, :, 0], qkv_heads[:, :, 1],
                        preferred_element_type=jnp.float32) * head_dim ** -0.5
    scores = jnp.where(keep_mask[:, None, None, :], scores, -1e30)
    attn_probs = jax.nn.softmax(scores, axis=-1).astype(jnp.bfloat16)
    return jnp.einsum('bhqk,bkhd->bqhd', attn_probs, qkv_heads[:, :, 2],
                      preferred_element_type=jnp.float32).astype(jnp.bfloat16)


def gather_full(shard_part, axis_pos):
    return lax.all_gather(shard_part, 'fsdp', axis=axis_pos, tiled=True)


def solution(mesh):
    def local_step(token_ids, tok_shard, pos_table, type_row, emb_gain, emb_bias, w_qkv, b_qkv, w_out, b_out,
                   ln1_gain, ln1_bias, w_ffn_in, b_ffn_in, w_ffn_out, b_ffn_out, ln2_gain, ln2_bias):
        batch_dev, seq_len = token_ids.shape
        shard_rows = tok_shard.shape[0]
        num_heads, head_dim = w_out.shape[0], w_out.shape[1]
        all_ids = lax.all_gather(token_ids, 'fsdp', axis=0, tiled=True)
        local_index = all_ids - lax.axis_index('fsdp') * shard_rows
        owned_mask = (local_index >= 0) & (local_index < shard_rows)
        found_rows = jnp.take(tok_shard, jnp.clip(local_index, 0, shard_rows - 1), axis=0)
        found_rows = jnp.where(owned_mask[:, :, None], found_rows, jnp.zeros((), found_rows.dtype))
        tok_rows = lax.psum_scatter(found_rows, 'fsdp', scatter_dimension=0, tiled=True)
        keep_mask = token_ids != PAD_ID
        keep_int = keep_mask.astype(jnp.int32)
        positions = jnp.cumsum(keep_int, axis=1) * keep_int + 1
        embedded = (tok_rows.astype(jnp.float32) + jnp.take(pos_table, positions, axis=0).astype(jnp.float32)
                    + type_row.astype(jnp.float32))
        x_embed = layer_norm(embedded, gather_full(emb_gain, 0), gather_full(emb_bias, 0)).astype(jnp.bfloat16)
        w_qkv_full = gather_full(w_qkv, 1)
        b_qkv_full = gather_full(b_qkv, 0)
        qkv_rows = (jnp.einsum('btd,de->bte', x_embed, w_qkv_full, preferred_element_type=jnp.float32)
                    + b_qkv_full).astype(jnp.bfloat16)
        qkv_heads = qkv_rows.reshape(batch_dev, seq_len, 3, num_heads, head_dim)
        context = attention(qkv_heads, keep_mask, head_dim)
        w_out_full = gather_full(w_out, 2)
        attn_out = (jnp.einsum('bqhd,hde->bqe', context, w_out_full, preferred_element_type=jnp.float32)
                    + gather_full(b_out, 0)).astype(jnp.bfloat16)
        x_attn = layer_norm(x_embed.astype(jnp.float32) + attn_out.astype(jnp.float32),
                            gather_full(ln1_gain, 0), gather_full(ln1_bias, 0)).astype(jnp.bfloat16)
        w_in_full = gather_full(w_ffn_in, 1)
        hidden = jax.nn.gelu(jnp.einsum('btd,df->btf', x_attn, w_in_full, preferred_element_type=jnp.float32)
                             + gather_full(b_ffn_in, 0), approximate=False).astype(jnp.bfloat16)
        w_back_full = gather_full(w_ffn_out, 0)
        ffn_out = (jnp.einsum('btf,fd->btd', hidden, w_back_full, preferred_element_type=jnp.float32)
                   + gather_full(b_ffn_out, 0))
        return layer_norm(x_attn.astype(jnp.float32) + ffn_out, gather_full(ln2_gain, 0),
                          gather_full(ln2_bias, 0)).astype(jnp.bfloat16)

    vec_spec = P('fsdp')
    in_specs = (P('fsdp', None), P('fsdp', None), P(None, None), P(None), vec_spec, vec_spec,
                P(None, 'fsdp'), vec_spec, P(None, None, 'fsdp'), vec_spec, vec_spec, vec_spec,
                P(None, 'fsdp'), vec_spec, P('fsdp', None), vec_spec, vec_spec, vec_spec)
    return jax.shard_map(local_step, mesh=mesh, in_specs=in_specs, out_specs=P('fsdp', None, None),
                         check_vma=False)
```

profile of v0, /device:TPU:0, one launch (start us, length us, event | category | flops | bytes accessed | tf_op | source)
XLA Modules:
  0.0 1293.0 jit_solution(7060616107319489077)
XLA Ops:
  6.5 43.9 %all-gather = s32[32,4,384]{2,1,0:T(4,128)S(1)} all-gather(s32[1,4,384]{2,1,0:T(4,128)} %bitcast.94), channel_id=1, replica_groups=mesh['fsdp'=32] {'fsdp'}, dimensions={0}, use_global_device_ids=true | all-gather | bytes 202752 | tf_op jit(solution)/shard_map/all_gather | solution.py:36
  50.5 0.1 subtract_clamp_fusion
  50.5 0.1 reshape.129
  50.6 0.7 compare_and_fusion.1
  51.3 0.1 compare_and_fusion
  51.5 0.7 reshape.130
  52.1 228.1 %gather_fusion = bf16[49152,768]{1,0:T(8,128)(2,1)} fusion(bf16[15664,768]{1,0:T(8,128)(2,1)} %param.19, s32[49152]{0:T(1024)S(1)} %broadcast_clamp_fusion), kind=kCustom, calls=%fused_computation | custom fusion | bytes 151191552 | tf_op jit(solution)/shard_map/jit(_take)/gather | solution.py:39
  280.3 50.3 %select_select_fusion = bf16[128,384,768]{2,1,0:T(8,128)(2,1)} fusion(bf16[128,384,768]{2,1,0:T(8,128)(2,1)} %bitcast.1, pred[128,384]{1,0:T(8,128)(4,1)S(1)} %copy-done.5, pred[128,384]{1,0:T(8,128)(4,1)S(1)} %copy-done.4), kind=kLoop, calls=%fused_computation.3 | loop fusion | flops 75497472 | bytes 151093248 | tf_op jit(solution)/shard_map/jit(_where)/select_n | solution.py:40
  330.7 0.0 all-gather.6.cloned.1.call-start
  330.7 0.7 all-gather.6.cloned.1.call-update
  331.4 0.0 all-gather.8.cloned.1.call-start
  331.5 0.7 all-gather.8.cloned.1.call-update
  332.2 0.5 all-gather.10.cloned.1.call-update
  332.7 0.0 all-gather.12.cloned.1.call-start
  332.8 0.5 all-gather.12.cloned.1.call-update
  333.4 1.2 reduce-window.6
  334.6 0.2 slice_reduce_fusion
  334.8 0.2 reduce-window.9
  335.0 0.1 add_bitcast_fusion
  335.1 0.2 dynamic-update-slice
  335.4 0.2 dynamic-update-slice.1
  335.6 0.2 dynamic-update-slice.3
  335.9 0.2 dynamic-update-slice.4
  336.1 0.2 dynamic-update-slice.5
  336.3 0.2 dynamic-update-slice.7
  336.5 0.2 dynamic-update-slice.8
  336.8 0.2 dynamic-update-slice.9
  337.0 5.0 gather_fusion.1
  342.0 0.3 dynamic-update-slice.2
  342.3 0.3 dynamic-update-slice.6
  342.5 38.2 %all-reduce.10 = (f32[768]{0:T(1024)S(1)}, f32[768]{0:T(1024)S(1)}, f32[768]{0:T(1024)S(1)}, f32[2304]{0:T(1024)S(1)}, f32[768]{0:T(1024)S(1)}, /*index=5*/f32[7...) all-reduce(f32[768]{0:T(1024)S(1)} %dynamic-update-slice.3, ...), channel_id=1, replica_groups=mesh['fsdp'=32] {'fsdp'}, use_global_device_ids=true, to_apply=%add.3 | all-reduce | flops 11520 | bytes 92160
  380.7 597.8 %reduce-scatter.2.cloned.1.call-done = bf16[4,384,768]{2,1,0:T(8,128)(2,1)} async-done(((bf16[128,384,768]{2,1,0:T(8,128)(2,1)}), bf16[4,384,768]{2,1,0:T(8,128)(2,1)}) %reduce-scatter.2.cloned.1.call-update) | async-done | bytes 2359312 | tf_op jit(solution)/shard_map/reduce_scatter | solution.py:41
  978.5 2.8 fusion.25
  981.4 3.0 multiply_reduce_fusion.2
  984.4 2.7 add_convert_fusion.3
  987.2 54.3 %all-gather.6.cloned.1.call-done = bf16[768,2304]{0,1:T(8,128)(2,1)} async-done(((bf16[768,72]{0,1:T(8,128)(2,1)}), bf16[768,2304]{0,1:T(8,128)(2,1)}) %all-gather.6.cloned.1.call-update) | async-done | bytes 3538960 | tf_op jit(solution)/shard_map/all_gather | solution.py:27
  1041.5 10.1 add_convert_fusion
  1051.5 10.3 copy.26
  1061.8 18.1 %fusion.77 = (f32[4,12,384]{2,1,0:T(8,128)S(1)}, f32[4,12,384,384]{2,3,1,0:T(8,128)}) fusion(pred[4,384]{1,0:T(4,128)(4,1)S(1)} %get-tuple-element.20, bf16[4,384,3,12,64]{1,4,3,2,0:T(8,128)(2,1)} %bitcast.92), kind=kOutput, calls=%fused_computation.120 | convolution fusion | flops 934281600 | bytes 33105408 | tf_op jit(solution)/shard_map/sub | solution.py:21
  1079.9 17.5 %all-gather.8.cloned.1.call-done = bf16[12,64,768]{1,2,0:T(8,128)(2,1)} async-done(((bf16[12,64,24]{1,2,0:T(8,128)(2,1)}), bf16[12,64,768]{1,2,0:T(8,128)(2,1)}) %all-gather.8.cloned.1.call-update) | async-done | bytes 1179664 | tf_op jit(solution)/shard_map/all_gather | solution.py:27
  1097.4 15.3 %fusion.24 = (f32[4,384]{1,0:T(4,128)S(1)}, bf16[4,384,768]{2,1,0:T(8,128)(2,1)}) fusion(bf16[4,384,768]{2,1,0:T(8,128)(2,1)S(1)} %copy-done.3, f32[768]{0:T(1024)S(1)} %get-tuple-element.7, bf16[12,64,768]{1,2,0:T(8,128)(2,1)} %all-gather.8.cloned.1.call-done, f32[4,12,384,384]{2,3,1,0:T(8,128)} %get-tuple-element.22, ...), kind=kOutput, calls=%fused_computation.53 | convolution fusion | flops 2740320768 | bytes 37831680 | tf_op jit(solution)/shard_map/bqhd,hde->bqe/dot_general | solution.py:55
  1112.7 2.8 multiply_reduce_fusion.1
  1115.5 48.3 %all-gather.10.cloned.1.call-done = bf16[768,3072]{0,1:T(8,128)(2,1)} async-done(((bf16[768,96]{0,1:T(8,128)(2,1)}), bf16[768,3072]{0,1:T(8,128)(2,1)}) %all-gather.10.cloned.1.call-update) | async-done | bytes 4718608 | tf_op jit(solution)/shard_map/all_gather | solution.py:27
  1163.7 21.1 %fusion.22 = (u8[384,3072]{1,0:T(8,128)(4,1)}, u8[384,3072]{1,0:T(8,128)(4,1)}, f32[4,384,3072]{2,1,0:T(8,128)}) fusion(f32[3072]{0:T(1024)S(1)} %get-tuple-element.13, bf16[768,3072]{0,1:T(8,128)(2,1)} %all-gather.10.cloned.1.call-done, bf16[4,384,768]{2,1,0:T(8,128)(2,1)} %get-tuple-element.24, bf16[4,384,768]{2,1,0:T(8,128)(2,1)S(1)} %copy-done.3, ...), kind=kOutput, calls=%fused_computation.51 | convolution fusion | flops 7320895488 | bytes 30701568 | tf_op jit(solution)/shard_map/btd,df->btf/dot_general | solution.py:60
  1184.9 43.9 %all-gather.12.cloned.1.call-done = bf16[3072,768]{1,0:T(8,128)(2,1)} async-done(((bf16[96,768]{1,0:T(8,128)(2,1)}), bf16[3072,768]{1,0:T(8,128)(2,1)}) %all-gather.12.cloned.1.call-update) | async-done | bytes 4718608 | tf_op jit(solution)/shard_map/all_gather | solution.py:27
  1228.8 54.8 %fusion.78 = (f32[4,384]{1,0:T(4,128)S(1)}, f32[4,384,768]{2,1,0:T(8,128)S(1)}) fusion(f32[768]{0:T(1024)S(1)} %get-tuple-element.14, bf16[3072,768]{1,0:T(8,128)(2,1)} %all-gather.12.cloned.1.call-done, f32[4,384,3072]{2,1,0:T(8,128)} %get-tuple-element.25, f32[3072]{0:T(1024)S(1)} %get-tuple-element.13, u8[384,3072]{1,0:T(8,128)(4,1)} %get-tuple-element.6, ...), kind=kOutput, calls=%fused_computation.121 | convolution fusion | flops 7596931584 | bytes 35429376 | tf_op jit(solution)/shard_map/btf,fd->btd/dot_general | solution.py:63
  1283.6 0.7 multiply_reduce_fusion
  1284.3 1.9 add_convert_fusion.1
  (68 shorter events, 0.3 us)
Async XLA Ops:
  6.5 330.4 %copy-start = (bf16[512,768]{1,0:T(8,128)(2,1)S(1)}, bf16[512,768]{1,0:T(8,128)(2,1)}, u32[]{:S(2)}) copy-start(bf16[512,768]{1,0:T(8,128)(2,1)} %param.20) | copy-start | bytes 2359300
  6.5 972.0 %reduce-scatter.2.cloned.1.call-start = ((), (), s32[]{:S(2)}) async-start(), calls=%async_computation.1 | async-start | bytes 77856768 | tf_op jit(solution)/shard_map/reduce_scatter | solution.py:41
  52.1 228.1 %copy-start.4 = (pred[128,384]{1,0:T(8,128)(4,1)S(1)}, pred[128,384]{1,0:T(8,128)(4,1)}, u32[]{:S(2)}) copy-start(pred[128,384]{1,0:T(8,128)(4,1)} %reshape.130) | copy-start | bytes 147460
  52.1 228.1 %copy-start.5 = (pred[128,384]{1,0:T(8,128)(4,1)S(1)}, pred[128,384]{1,0:T(8,128)(4,1)}, u32[]{:S(2)}) copy-start(pred[128,384]{1,0:T(8,128)(4,1)} %compare_and_fusion.1) | copy-start | bytes 147460
  330.5 2.8 copy-start.6
  330.5 4.6 copy-start.9
  330.5 4.6 copy-start.10
  330.5 4.9 copy-start.11
  330.6 5.1 copy-start.12
  330.6 5.3 copy-start.13
  330.6 5.5 copy-start.14
  330.6 5.7 copy-start.15
  330.6 5.9 copy-start.16
  330.6 6.1 copy-start.17
  330.7 710.8 %all-gather.6.cloned.1.call-start = ((), (), s32[]{:S(2)}) async-start(), calls=%async_computation.2 | async-start | bytes 3649536 | tf_op jit(solution)/shard_map/all_gather | solution.py:27
  331.4 766.0 %all-gather.8.cloned.1.call-start = ((), (), s32[]{:S(2)}) async-start(), calls=%async_computation.3 | async-start | bytes 2433024 | tf_op jit(solution)/shard_map/all_gather | solution.py:27
  332.1 831.6 %all-gather.10.cloned.1.call-start = ((), (), s32[]{:S(2)}) async-start(), calls=%async_computation.4 | async-start | bytes 4866048 | tf_op jit(solution)/shard_map/all_gather | solution.py:27
  332.7 896.1 %all-gather.12.cloned.1.call-start = ((), (), s32[]{:S(2)}) async-start(), calls=%async_computation.5 | async-start | bytes 4866048 | tf_op jit(solution)/shard_map/all_gather | solution.py:27
  337.0 5.0 copy-start.18
  337.0 5.3 copy-start.19
  978.5 5.9 copy-start.2
  1061.8 35.6 %copy-start.3 = (bf16[4,384,768]{2,1,0:T(8,128)(2,1)S(1)}, bf16[4,384,768]{2,1,0:T(8,128)(2,1)}, u32[]{:S(2)}) copy-start(bf16[4,384,768]{2,1,0:T(8,128)(2,1)} %add_convert_fusion.3) | copy-start | bytes 7077892
  1228.8 55.5 %copy-start.7 = (f32[768]{0:T(1024)S(1)}, f32[768]{0:T(1024)}, u32[]{:S(2)}) copy-start(f32[768]{0:T(1024)} %get-tuple-element.15) | copy-start | bytes 9220
  1228.8 55.5 %copy-start.8 = (f32[768]{0:T(1024)S(1)}, f32[768]{0:T(1024)}, u32[]{:S(2)}) copy-start(f32[768]{0:T(1024)} %get-tuple-element.16) | copy-start | bytes 9220
  1228.8 57.5 %copy-start.1 = (bf16[512,768]{1,0:T(8,128)(2,1)S(1)}, bf16[512,768]{1,0:T(8,128)(2,1)}, u32[]{:S(2)}) copy-start(bf16[512,768]{1,0:T(8,128)(2,1)} %param.20) | copy-start | bytes 2359300
Sparse Core Ops, SparseCore 0:
  330.8 647.7 reduce-scatter.1
  981.4 59.9 all-gather.5
  1044.3 53.0 all-gather.7
  1100.1 63.5 all-gather.9
  1166.5 62.2 all-gather.11
where the time goes:
time: 1300 us; the launch traced here: 1290 us
  waiting for transfers between devices  764 us (59%)
  local copies, waits for them, and re-layouts  247 us (19%)
  matrix products  119 us (9%)
  blocking collectives  82.1 us (6%)
  other arithmetic  66.6 us (5%)
  between operations  13.6 us (1%)
    reduce_scatter x1, waiting for transfers between devices, local_step(): lax.psum_scatter(found_rows, 'fsdp', scatter_dimension=0, tiled=True)  598 us
    gather x1, local copies, waits for them, and re-layouts, local_step(): jnp.take(tok_shard, jnp.clip(local_index, 0, shard_rows - 1), axis=0)  228 us
    all_gather x4, waiting for transfers between devices, gather_full(): return lax.all_gather(shard_part, 'fsdp', axis=axis_pos, tiled=True)  164 us
    dot_general x1, matrix products, local_step(): jnp.einsum('btf,fd->btd', hidden, w_back_full, preferred_element_type=jnp...  54.8 us
    select_n x1, other arithmetic, local_step(): jnp.where(owned_mask[:, :, None], found_rows, jnp.zeros((), found_rows.dt...  50.3 us
    all_gather x1, blocking collectives, local_step(): all_ids = lax.all_gather(token_ids, 'fsdp', axis=0, tiled=True)  43.9 us
    unnamed x1, blocking collectives  38.2 us
  transfers between devices with their start and end apart: 5, of which 5 were waited for; matrix products, arithmetic and copies ran while one was open for 7% of the time, Pallas kernels for 0%

commit v1 on v0

v1 whole, which is shorter than its diff:
```python
import jax
import jax.numpy as jnp
from jax import lax
from jax.experimental import pallas as pl
from jax.experimental.pallas import tpu as pltpu
from jax.sharding import PartitionSpec as P

PAD_ID = 1
LN_EPS = 1e-5


def layer_norm(values, ln_gain, ln_shift):
    row_mean = jnp.mean(values, axis=-1, keepdims=True)
    centered = values - row_mean
    row_var = jnp.mean(centered * centered, axis=-1, keepdims=True)
    return centered * lax.rsqrt(row_var + LN_EPS) * ln_gain + ln_shift


def attention(qkv_heads, keep_mask, head_dim):
    scores = jnp.einsum('bqhd,bkhd->bhqk', qkv_heads[:, :, 0], qkv_heads[:, :, 1],
                        preferred_element_type=jnp.float32) * head_dim ** -0.5
    scores = jnp.where(keep_mask[:, None, None, :], scores, -1e30)
    attn_probs = jax.nn.softmax(scores, axis=-1).astype(jnp.bfloat16)
    return jnp.einsum('bhqk,bkhd->bqhd', attn_probs, qkv_heads[:, :, 2],
                      preferred_element_type=jnp.float32).astype(jnp.bfloat16)


HEAD = 2048
CAPS = ((0, 1, 184), (1, 2, 96), (2, 4, 72), (4, 32, 48))
EXTRA = 48
MESH = pl.DeviceIdType.MESH


def others(n, me, one):
    def body(k, carry):
        one(k, lax.rem(me + k, n))
        return carry

    lax.fori_loop(1, n, body, 0)


def meet(n, me):
    barrier = pltpu.get_barrier_semaphore()
    others(n, me, lambda k, dev: pl.semaphore_signal(barrier, inc=1, device_id=(dev,), device_id_type=MESH))
    pl.semaphore_wait(barrier, n - 1)


def tell_kernel(n, part, msg_ref, table_ref, told_ref, piece_ref, send_sem, recv_sem, out_sem, in_sem, own_sem):
    me = lax.axis_index('fsdp')
    meet(n, me)

    def note(k, dev, slot):
        return pltpu.make_async_remote_copy(msg_ref, told_ref.at[slot], send_sem.at[k], recv_sem.at[slot],
                                            device_id=(dev,), device_id_type=MESH)

    def head(dev):
        return pltpu.make_async_remote_copy(table_ref.at[pl.ds(pl.multiple_of(dev * part, 8), part)], piece_ref,
                                            out_sem.at[dev], in_sem, device_id=(dev,), device_id_type=MESH)

    def own():
        return pltpu.make_async_copy(table_ref.at[pl.ds(0, part)], piece_ref, own_sem)

    others(n, me, lambda k, dev: note(k, dev, me).start())

    @pl.when(me == 0)
    def _():
        others(n, me, lambda k, dev: head(dev).start())
        own().start()

    told_ref[me] = msg_ref[...]
    others(n, me, lambda k, dev: note(k, dev, dev).wait_recv())
    others(n, me, lambda k, dev: note(k, dev, me).wait_send())

    @pl.when(me == 0)
    def _():
        own().wait()
        others(n, me, lambda k, dev: head(dev).wait_send())

    @pl.when(me != 0)
    def _():
        head(me).wait_recv()


def tell(n, msg, table):
    part = HEAD // n
    return pl.pallas_call(
        lambda *refs: tell_kernel(n, part, *refs),
        out_shape=(jax.ShapeDtypeStruct((n,) + msg.shape, msg.dtype),
                   jax.ShapeDtypeStruct((part, table.shape[1]), table.dtype)),
        in_specs=[pl.BlockSpec(memory_space=pltpu.VMEM), pl.BlockSpec(memory_space=pl.ANY)],
        out_specs=(pl.BlockSpec(memory_space=pltpu.VMEM), pl.BlockSpec(memory_space=pltpu.VMEM)),
        scratch_shapes=[pltpu.SemaphoreType.DMA((n,)), pltpu.SemaphoreType.DMA((n,)), pltpu.SemaphoreType.DMA((n,)),
                        pltpu.SemaphoreType.DMA, pltpu.SemaphoreType.DMA],
        compiler_params=pltpu.CompilerParams(collective_id=0, has_side_effects=True))(msg, table)


def bases():
    out, at = [], 0
    for lo, hi, cap in CAPS:
        out.append(at)
        at += (hi - lo) * cap
    return out, at


def swap_kernel(n, send_ref, recv_ref, send_sem, recv_sem, own_sem):
    me = lax.axis_index('fsdp')
    meet(n, me)
    starts, _ = bases()

    def spot(c, dev):
        lo, _, cap = CAPS[c]
        return recv_ref.at[pl.ds(pl.multiple_of(starts[c] + (dev - lo) * cap, 8), cap)]

    def row(c, k, dev, owner):
        return pltpu.make_async_remote_copy(send_ref.at[dev, pl.ds(0, CAPS[c][2])], spot(c, owner), send_sem.at[k],
                                            recv_sem.at[owner], device_id=(dev,), device_id_type=MESH)

    def own(c):
        return pltpu.make_async_copy(send_ref.at[me, pl.ds(0, CAPS[c][2])], spot(c, me), own_sem)

    for c, (lo, hi, cap) in enumerate(CAPS):
        @pl.when((me >= lo) & (me < hi))
        def _(c=c):
            others(n, me, lambda k, dev: row(c, k, dev, me).start())
            own(c).start()

    for c, (lo, hi, cap) in enumerate(CAPS):
        def one(dev, carry, c=c):
            @pl.when(dev != me)
            def _():
                row(c, 0, dev, dev).wait_recv()

            return carry

        lax.fori_loop(lo, hi, one, 0)

    for c, (lo, hi, cap) in enumerate(CAPS):
        @pl.when((me >= lo) & (me < hi))
        def _(c=c):
            others(n, me, lambda k, dev: row(c, k, dev, me).wait_send())
            own(c).wait()


def swap(n, rows):
    return pl.pallas_call(
        lambda *refs: swap_kernel(n, *refs),
        out_shape=jax.ShapeDtypeStruct((bases()[1], rows.shape[2]), rows.dtype),
        in_specs=[pl.BlockSpec(memory_space=pl.ANY)], out_specs=pl.BlockSpec(memory_space=pl.ANY),
        scratch_shapes=[pltpu.SemaphoreType.DMA((n,)), pltpu.SemaphoreType.DMA((n,)), pltpu.SemaphoreType.DMA],
        compiler_params=pltpu.CompilerParams(collective_id=1, has_side_effects=True))(rows)


def solution(mesh):
    def local_step(token_ids, tok_shard, pos_table, type_row, emb_gain, emb_bias, w_qkv, b_qkv, w_out, b_out,
                   ln1_gain, ln1_bias, w_ffn_in, b_ffn_in, w_ffn_out, b_ffn_out, ln2_gain, ln2_bias):
        n_dev = mesh.shape['fsdp']
        me = lax.axis_index('fsdp')
        batch_dev, seq_len = token_ids.shape
        n_tok = batch_dev * seq_len
        shard_rows, width = tok_shard.shape
        num_heads, head_dim = w_out.shape[0], w_out.shape[1]
        pieces = [w_qkv.T, w_out.reshape(num_heads * head_dim, -1).T, w_ffn_in.T, w_ffn_out]
        sizes = [p.shape[0] for p in pieces]
        weights = lax.all_gather(jnp.concatenate(pieces, axis=0), 'fsdp', axis=0, tiled=False)
        full, at = [], 0
        for size in sizes:
            full.append(weights[:, at:at + size].reshape(n_dev * size, width))
            at += size
        w_qkv_t, w_out_t, w_in_t, w_back = full

        ids = token_ids.reshape(n_tok)
        keep = ids != PAD_ID
        asks = keep & (ids >= HEAD)
        owner = jnp.where(asks, ids // shard_rows, n_dev)
        place = jnp.arange(n_tok, dtype=jnp.int32)
        lanes = jnp.arange(128, dtype=jnp.int32)
        mine = (owner[:, None] == lanes[None, :]) & (lanes < n_dev)[None, :]
        before = (place[None, :] < place[:, None]).astype(jnp.bfloat16)
        ranks = jnp.dot(before, mine.astype(jnp.bfloat16), preferred_element_type=jnp.float32)
        count = jnp.sum(mine.astype(jnp.float32), axis=0)
        rank = jnp.sum(jnp.where(mine, ranks, 0.0), axis=1).astype(jnp.int32)
        starts, slots = bases()
        cap, base = jnp.zeros_like(owner), jnp.zeros_like(owner)
        for (lo, hi, c), b in zip(CAPS, starts):
            inside = (owner >= lo) & (owner < hi)
            cap = jnp.where(inside, c, cap)
            base = jnp.where(inside, b + (owner - lo) * c, base)
        fits = rank < cap
        slot = jnp.where(fits, base + rank, -1)
        wide = slots + -slots % 128
        slotted = jnp.sum(jnp.where(slot[:, None] == jnp.arange(wide, dtype=jnp.int32)[None, :],
                                    ids.astype(jnp.float32)[:, None], 0.0), axis=0)

        small = [emb_gain, emb_bias, ln1_gain, ln1_bias, ln2_gain, ln2_bias, b_out, b_ffn_out, b_qkv, b_ffn_in]
        message = jnp.concatenate([slotted, count] + small)
        message = jnp.pad(message, (0, -message.shape[0] % 1024))
        told, piece = tell(n_dev, message.reshape(-1, 128), tok_shard)
        told = told.reshape(n_dev, -1)
        head = lax.all_gather(piece, 'fsdp', axis=0, tiled=True)
        at = wide + 128
        vectors = []
        for v in small:
            vectors.append(told[:, at:at + v.shape[0]].reshape(-1))
            at += v.shape[0]
        emb_g, emb_b, ln1_g, ln1_b, ln2_g, ln2_b, b_out_f, b_back_f, b_qkv_f, b_in_f = vectors

        my_base = jnp.int32(0)
        for (lo, hi, c), b in zip(CAPS, starts):
            my_base = jnp.where((me >= lo) & (me < hi), b + (me - lo) * c, my_base)
        most = max(c for _, _, c in CAPS)
        wanted = lax.dynamic_slice(told, (0, my_base), (n_dev, most)).astype(jnp.int32) - me * shard_rows
        wanted = jnp.clip(wanted, 0, shard_rows - 1)
        rows = jnp.take(tok_shard, wanted.reshape(-1), axis=0, mode='clip').reshape(n_dev, most, width)
        got = swap(n_dev, rows)
        spot = jnp.where(ids < HEAD, ids, HEAD + jnp.maximum(slot, 0))
        tok_rows = jnp.take(jnp.concatenate([head, got], axis=0), spot, axis=0, mode='clip')

        caps = jnp.concatenate([jnp.full((hi - lo,), c, jnp.float32) for lo, hi, c in CAPS])
        left = jnp.max(told[:, wide:wide + n_dev] - caps[None, :])
        rounds = (jnp.maximum(left, 0.0).astype(jnp.int32) + EXTRA - 1) // EXTRA

        def again(state):
            r, rows_now = state
            extra = rank - cap - r * EXTRA
            live = asks & (extra >= 0) & (extra < EXTRA)
            at_slot = jnp.where(live, owner * EXTRA + extra, n_dev * EXTRA)
            ask = jnp.zeros((n_dev * EXTRA + 1,), jnp.int32).at[at_slot].set(ids)[:-1]
            asked = lax.all_to_all(ask.reshape(n_dev, EXTRA), 'fsdp', 0, 0, tiled=True)
            asked = jnp.clip(asked - me * shard_rows, 0, shard_rows - 1)
            found = jnp.take(tok_shard, asked.reshape(-1), axis=0, mode='clip').reshape(n_dev, EXTRA, width)
            back = lax.all_to_all(found, 'fsdp', 0, 0, tiled=True).reshape(n_dev * EXTRA, width)
            new = jnp.take(back, jnp.where(live, at_slot, 0), axis=0, mode='clip')
            return r + 1, jnp.where(live[:, None], new, rows_now)

        _, tok_rows = lax.while_loop(lambda state: state[0] < rounds, again, (jnp.int32(0), tok_rows))
        tok_rows = tok_rows.reshape(batch_dev, seq_len, width)

        keep_mask = token_ids != PAD_ID
        keep_int = keep_mask.astype(jnp.int32)
        positions = jnp.cumsum(keep_int, axis=1) * keep_int + 1
        embedded = (tok_rows.astype(jnp.float32) + jnp.take(pos_table, positions, axis=0).astype(jnp.float32)
                    + type_row.astype(jnp.float32))
        x_embed = layer_norm(embedded, emb_g, emb_b).astype(jnp.bfloat16)
        qkv_rows = (jnp.einsum('btd,ed->bte', x_embed, w_qkv_t, preferred_element_type=jnp.float32)
                    + b_qkv_f).astype(jnp.bfloat16)
        qkv_heads = qkv_rows.reshape(batch_dev, seq_len, 3, num_heads, head_dim)
        context = attention(qkv_heads, keep_mask, head_dim).reshape(batch_dev, seq_len, width)
        attn_out = (jnp.einsum('bqc,ec->bqe', context, w_out_t, preferred_element_type=jnp.float32)
                    + b_out_f).astype(jnp.bfloat16)
        x_attn = layer_norm(x_embed.astype(jnp.float32) + attn_out.astype(jnp.float32), ln1_g, ln1_b).astype(jnp.bfloat16)
        hidden = jax.nn.gelu(jnp.einsum('btd,fd->btf', x_attn, w_in_t, preferred_element_type=jnp.float32)
                             + b_in_f, approximate=False).astype(jnp.bfloat16)
        ffn_out = jnp.einsum('btf,fd->btd', hidden, w_back, preferred_element_type=jnp.float32) + b_back_f
        return layer_norm(x_attn.astype(jnp.float32) + ffn_out, ln2_g, ln2_b).astype(jnp.bfloat16)

    vec_spec = P('fsdp')
    in_specs = (P('fsdp', None), P('fsdp', None), P(None, None), P(None), vec_spec, vec_spec,
                P(None, 'fsdp'), vec_spec, P(None, None, 'fsdp'), vec_spec, vec_spec, vec_spec,
                P(None, 'fsdp'), vec_spec, P('fsdp', None), vec_spec, vec_spec, vec_spec)
    return jax.shard_map(local_step, mesh=mesh, in_specs=in_specs, out_specs=P('fsdp', None, None),
                         check_vma=False)
```

time: 1300 us -> 465 us (0.36)
  waiting for transfers between devices: 764 us -> 11.2 us
  Pallas kernels: 0 us -> 194 us
  local copies, waits for them, and re-layouts: 247 us -> 83 us
  blocking collectives: 82.1 us -> 0 us
  other arithmetic: 66.6 us -> 24.4 us
    reduce_scatter x1 -> x0, waiting for transfers between devices: 598 us -> none  [local_step(): lax.psum_scatter(found_rows, 'fsdp', scatter_dimension=0, tiled=True)]
    pallas_call x0 -> x2, Pallas kernels: none -> 194 us  [the longest x1 152 us: swap(): pl.pallas_call(lambda *refs: swap_kernel(n, *refs), out_shape=jax.ShapeDt...]
    gather x1 -> x2, local copies, waits for them, and re-layouts: 228 us -> 43 us  [the longest x1 33 us: local_step(): jnp.take(tok_shard, wanted.reshape(-1), axis=0, mode='clip')]
    all_gather x4 -> x2, waiting for transfers between devices: 164 us -> 11.2 us  [the longest x1 11.1 us: local_step(): lax.all_gather(jnp.concatenate(pieces, axis=0), 'fsdp', axis=0, tiled=False)]
    select_n x2 -> x3, other arithmetic: 50.3 us -> 0.12 us  [the longest x1 0.07 us: local_step(): spot = jnp.where(ids < HEAD, ids, HEAD + jnp.maximum(slot, 0))]
    all_gather x1 -> x0, blocking collectives: 43.9 us -> none  [local_step(): all_ids = lax.all_gather(token_ids, 'fsdp', axis=0, tiled=True)]
    unnamed x1 -> x0, blocking collectives: 38.2 us -> none
    slice x1 -> x7, local copies, waits for them, and re-layouts: 0.22 us -> 13.4 us  [the longest x3 12.9 us: local_step(): full.append(weights[:, at:at + size].reshape(n_dev * size, width))]
  transfers between devices with their start and end apart: 5 -> 2, of which waited for: 5 -> 1; matrix products, arithmetic and copies ran while one was open for 7% -> 17% of each run, Pallas kernels for 0% -> 33%
where the time goes in v1:
time: 465 us; the launch traced here: 456 us
  Pallas kernels  194 us (42%)
  matrix products  120 us (26%)
  local copies, waits for them, and re-layouts  83 us (18%)
  other arithmetic  24.4 us (5%)
  between operations  15.2 us (3%)
  waiting for transfers between devices  11.2 us (2%)
  loops' own time  8.73 us (2%)
    pallas_call x1, Pallas kernels, swap(): pl.pallas_call(lambda *refs: swap_kernel(n, *refs), out_shape=jax.ShapeDt...  152 us
    dot_general x1, matrix products, local_step(): jnp.einsum('btf,fd->btd', hidden, w_back, preferred_element_type=jnp.floa...  54.8 us
    pallas_call x1, Pallas kernels, tell(): pl.pallas_call(lambda *refs: tell_kernel(n, part, *refs), out_shape=(jax....  41.6 us
    gather x1, local copies, waits for them, and re-layouts, local_step(): jnp.take(tok_shard, wanted.reshape(-1), axis=0, mode='clip')  33 us
    dot_general x1, matrix products, local_step(): jnp.einsum('btd,fd->btf', x_attn, w_in_t, preferred_element_type=jnp.floa...  21.5 us
    dot_general x1, matrix products, attention(): jnp.einsum('bhqk,bkhd->bqhd', attn_probs, qkv_heads[:, :, 2], preferred_e...  16.3 us
    slice x3, local copies, waits for them, and re-layouts, local_step(): full.append(weights[:, at:at + size].reshape(n_dev * size, width))  12.9 us
    sub x1, matrix products, attention(): attn_probs = jax.nn.softmax(scores, axis=-1).astype(jnp.bfloat16)  12.2 us
  transfers between devices with their start and end apart: 2, of which 1 were waited for; matrix products, arithmetic and copies ran while one was open for 17% of the time, Pallas kernels for 33%

profile of v1, /device:TPU:0, one launch (start us, length us, event | category | flops | bytes accessed | tf_op | source)
XLA Modules:
  0.0 456.2 jit_solution(7804434085920562868)
XLA Ops:
  6.7 0.8 reshape.539
  7.5 0.3 convert_reduce_fusion
  7.8 1.3 fusion.40
  9.1 1.5 select_reduce_fusion.1
  10.8 0.6 pad_bitcast_fusion.refs_0_
  11.4 41.6 %shard_map.172 = (f32[32,24,128]{2,1,0:T(8,128)}, bf16[64,768]{1,0:T(8,128)(2,1)}) custom-call(f32[24,128]{1,0:T(8,128)} %pad_bitcast_fusion.refs_0_, bf16[15664,768]{1,0:T(8,128)(2,1)} %refs_1_.1), custom_call_target="tpu_custom_call" | custom-call | tf_op jit(solution)/shard_map/pallas_call | solution.py:86
  53.1 0.1 reshape.546
  53.3 0.8 pad_maximum_fusion.1
  54.1 1.1 copy.54
  55.2 0.6 fusion.46
  56.7 1.2 reduce-window.6
  57.9 0.2 slice_reduce_fusion
  58.1 0.2 reduce-window.9
  58.5 0.7 add.368
  59.1 0.7 add.379
  59.9 0.1 reshape.573
  60.0 0.1 fusion.91
  60.1 0.7 mul.247
  60.8 0.7 add.376
  61.5 0.7 mul.236
  62.2 0.7 mul.224
  62.9 0.7 add.387
  63.6 0.7 add.382
  64.2 0.7 add.371
  64.9 33.0 %gather_fusion.2 = bf16[5888,768]{1,0:T(8,128)(2,1)} fusion(bf16[15664,768]{1,0:T(8,128)(2,1)} %refs_1_.1, s32[6144]{0:T(1024)S(1)} %pad_clamp_fusion.2), kind=kCustom, calls=%fused_computation.2 | custom fusion | bytes 18111488 | tf_op jit(solution)/shard_map/jit(_take)/gather | solution.py:213
  97.9 152.2 %shard_map.173 = bf16[1768,768]{1,0:T(8,128)(2,1)} custom-call(bf16[32,184,768]{2,1,0:T(8,128)(2,1)} %bitcast.109), custom_call_target="tpu_custom_call" | custom-call | tf_op jit(solution)/shard_map/pallas_call | solution.py:145
  250.1 5.6 %gather_fusion.4 = bf16[1536,768]{1,0:T(8,128)(2,1)} fusion(bf16[512,768]{1,0:T(8,128)(2,1)S(1)} %copy-done, s32[2048]{0:T(1024)S(1)} %pad_clamp_fusion.3), kind=kCustom, calls=%fused_computation.4 | custom fusion | bytes 4724736 | tf_op jit(solution)/shard_map/jit(_take)/gather | solution.py:241
  255.9 4.7 %pad_maximum_fusion = bf16[3816,768]{1,0:T(8,128)(2,1)} fusion(bf16[1768,768]{1,0:T(8,128)(2,1)S(1)} %copy-done.3, bf16[2048,768]{1,0:T(8,128)(2,1)} %all-gather.4.cloned.1.call-done), kind=kLoop, calls=%fused_computation.59 | loop fusion | flops 11722752 | bytes 11722752 | tf_op jit(solution)/shard_map/concatenate | solution.py:216
  260.7 10.1 %gather_fusion.3 = bf16[1536,768]{1,0:T(8,128)(2,1)} fusion(bf16[3816,768]{1,0:T(8,128)(2,1)} %pad_maximum_fusion, s32[2048]{0:T(1024)S(1)} %pad_clamp_fusion.4), kind=kCustom, calls=%fused_computation.3 | custom fusion | bytes 4724736 | tf_op jit(solution)/shard_map/jit(_take)/gather | solution.py:216
  270.7 8.7 %while.13 = (s32[]{:T(128)}, bf16[1536,768]{1,0:T(8,128)(2,1)}, s32[]{:T(128)}, s32[1536,1]{0,1:T(1,128)S(1)}, pred[1536]{0:T(1024)(128)(4,1)S(1)}, /*index=5*/s...) while((s32[]{:T(128)}, bf16[1536,768]{1,0:T(8,128)(2,1)}, ...), condition=%wide.region_6.7_spmd, body=%wide.region_4.6_spmd.sunk | while | flops 1212931 | bytes 23744692 | solution.py:235
  279.5 3.6 fusion.41
  283.1 3.1 multiply_reduce_fusion.2
  286.3 4.2 add_convert_fusion.4
  290.4 11.1 %all-gather.6.cloned.1.call-done = bf16[9216,768]{1,0:T(8,128)(2,1)} async-done(((bf16[288,768]{1,0:T(8,128)(2,1)}), bf16[9216,768]{1,0:T(8,128)(2,1)}) %all-gather.6.cloned.1.call-update) | async-done | bytes 14155792 | tf_op jit(solution)/shard_map/all_gather | solution.py:164
  301.6 2.4 slice.106
  304.0 2.2 slice.101
  306.2 8.3 %fusion.90 = (bf16[32,96,768]{2,1,0:T(8,128)(2,1)}, bf16[32,96,768]{2,1,0:T(8,128)(2,1)}) fusion(bf16[32,288,768]{2,1,0:T(8,128)(2,1)} %bitcast.112), kind=kLoop, calls=%fused_computation.171 | loop fusion | bytes 18874368 | tf_op jit(solution)/shard_map/slice | solution.py:167
  314.5 7.8 %add_convert_fusion = bf16[4,384,2304]{2,1,0:T(8,128)(2,1)} fusion(bf16[4,384,768]{2,1,0:T(8,128)(2,1)S(1)} %bitcast.118, bf16[2304,768,1]{1,0,2:T(8,128)(2,1)S(1)} %bitcast.117, f32[2304]{0:T(1024)S(1)} %copy-done.17), kind=kOutput, calls=%fused_computation.51 | convolution fusion | flops 5442895872 | bytes 12985344 | tf_op jit(solution)/shard_map/btd,ed->bte/dot_general | solution.py:244
  322.3 10.3 %copy.35 = bf16[4,384,2304]{1,2,0:T(8,128)(2,1)} copy(bf16[4,384,2304]{2,1,0:T(8,128)(2,1)} %add_convert_fusion) | data formatting | bytes 14155776 | tf_op jit(solution)/shard_map/convert_element_type | solution.py:245
  332.6 12.2 %fusion.92 = f32[4,12,384]{2,1,0:T(8,128)S(1)} fusion(pred[4,384]{1,0:T(4,128)(4,1)S(1)} %copy-done.19, bf16[4,384,3,12,64]{1,4,3,2,0:T(8,128)(2,1)} %bitcast.113), kind=kOutput, calls=%fused_computation.173 | convolution fusion | flops 934281600 | bytes 4793856 | tf_op jit(solution)/shard_map/sub | solution.py:23
  344.8 16.3 %fusion.36 = bf16[4,12,64,384]{3,2,1,0:T(8,128)(2,1)} fusion(f32[4,12,384]{2,1,0:T(8,128)S(1)} %fusion.92, pred[4,384]{1,0:T(4,128)(4,1)S(1)} %copy-done.19, bf16[4,384,3,12,64]{1,4,3,2,0:T(8,128)(2,1)} %bitcast.114), kind=kOutput, calls=%fused_computation.82 | convolution fusion | flops 1848527232 | bytes 9512448 | tf_op jit(solution)/shard_map/bhqk,bkhd->bqhd/dot_general | solution.py:24
  361.1 6.2 %fusion.24 = (f32[4,384]{1,0:T(4,128)S(1)}, bf16[4,384,768]{2,1,0:T(8,128)(2,1)S(1)}, bf16[4,384,768]{2,1,0:T(8,128)(2,1)S(1)}) fusion(f32[768]{0:T(1024)S(1)} %add.363, f32[768]{0:T(1024)S(1)} %copy-done.15, f32[4,384]{1,0:T(4,128)S(1)} %rsqrt.29, f32[4,384]{1,0:T(4,128)S(1)} %div.60, f32[768]{0:T(1024)S(1)} %convert_element_type.112, ...), kind=kOutput, calls=%fused_computation.74 | convolution fusion | flops 1830812160 | bytes 13008384 | tf_op jit(solution)/shard_map/bqc,ec->bqe/dot_general | solution.py:248
  367.3 1.5 copy-done.4
  368.8 1.1 multiply_reduce_fusion.1
  370.0 21.5 %fusion.22 = (u8[384,3072]{1,0:T(8,128)(4,1)}, u8[384,3072]{1,0:T(8,128)(4,1)}, f32[4,384,3072]{2,1,0:T(8,128)}) fusion(f32[3072]{0:T(1024)S(1)} %copy-done.16, bf16[3072,768,1]{1,0,2:T(8,128)(2,1)} %bitcast.116, bf16[4,384,768]{2,1,0:T(8,128)(2,1)} %copy-done.6, bf16[4,384,768]{2,1,0:T(8,128)(2,1)} %copy-done.4, f32[768]{0:T(1024)S(1)} %copy-done.22, ...), kind=kOutput, calls=%fused_computation.72 | convolution fusion | flops 7320895488 | bytes 30701568 | tf_op jit(solution)/shard_map/btd,fd->btf/dot_general | solution.py:251
  391.5 54.8 %fusion.93 = (f32[4,384]{1,0:T(4,128)S(1)}, f32[4,384,768]{2,1,0:T(8,128)S(1)}) fusion(f32[768]{0:T(1024)S(1)} %copy-done.24, bf16[3072,768,1]{1,0,2:T(8,128)(2,1)} %bitcast.115, f32[4,384,3072]{2,1,0:T(8,128)} %get-tuple-element.204, f32[3072]{0:T(1024)S(1)} %copy-done.16, u8[384,3072]{1,0:T(8,128)(4,1)} %get-tuple-element.163, ...), kind=kOutput, calls=%fused_computation.174 | convolution fusion | flops 7596931584 | bytes 35429376 | tf_op jit(solution)/shard_map/btf,fd->btd/dot_general | solution.py:253
  446.4 0.7 multiply_reduce_fusion
  447.0 1.9 add_convert_fusion.1
  (112 shorter events, 1.1 us)
Async XLA Ops:
  6.5 243.5 %copy-start = (bf16[512,768]{1,0:T(8,128)(2,1)S(1)}, bf16[512,768]{1,0:T(8,128)(2,1)}, u32[]{:S(2)}) copy-start(bf16[512,768]{1,0:T(8,128)(2,1)} %param.22) | copy-start | bytes 2359300
  6.5 4.0 copy-start.32
  6.5 4.0 copy-start.31
  6.5 4.1 copy-start.34
  6.5 4.1 copy-start.36
  6.5 4.1 copy-start.30
  6.6 4.1 copy-start.29
  6.6 4.1 copy-start.33
  6.6 4.1 copy-start.35
  6.6 4.1 copy-start.28
  6.6 4.1 copy-start.27
  6.6 249.3 %all-gather.4.cloned.1.call-start = ((), (), s32[]{:S(2)}) async-start(), calls=%async_computation.2 | async-start | bytes 3244032 | tf_op jit(solution)/shard_map/all_gather | solution.py:199
  11.4 41.7 %copy-start.11 = (bf16[12,64,24]{1,2,0:T(8,128)(2,1)S(1)}, bf16[12,64,24]{1,2,0:T(8,128)(2,1)}, u32[]{:S(2)}) copy-start(bf16[12,64,24]{1,2,0:T(8,128)(2,1)} %param.28) | copy-start | bytes 110596
  11.4 41.9 %copy-start.8 = (bf16[96,768]{1,0:T(8,128)(2,1)S(1)}, bf16[96,768]{1,0:T(8,128)(2,1)}, u32[]{:S(2)}) copy-start(bf16[96,768]{1,0:T(8,128)(2,1)} %param.34) | copy-start | bytes 442372
  11.4 41.9 %copy-start.9 = (bf16[768,96]{0,1:T(8,128)(2,1)S(1)}, bf16[768,96]{0,1:T(8,128)(2,1)}, u32[]{:S(2)}) copy-start(bf16[768,96]{0,1:T(8,128)(2,1)} %param.32) | copy-start | bytes 442372
  11.4 41.9 %copy-start.10 = (bf16[768,72]{0,1:T(8,128)(2,1)S(1)}, bf16[768,72]{0,1:T(8,128)(2,1)}, u32[]{:S(2)}) copy-start(bf16[768,72]{0,1:T(8,128)(2,1)} %param.26) | copy-start | bytes 331780
  11.4 43.8 %copy-start.37 = (f32[32]{0:T(128)S(1)}, f32[32]{0:T(128)}, u32[]{:S(2)}) copy-start(f32[32]{0:T(128)} %constant.97.clone.1) | copy-start | bytes 388
  11.4 45.2 %copy-start.26 = (bf16[768]{0:T(1024)(128)(2,1)S(1)}, bf16[768]{0:T(1024)(128)(2,1)}, u32[]{:S(2)}) copy-start(bf16[768]{0:T(1024)(128)(2,1)} %param.23) | copy-start | bytes 4612
  11.4 45.2 %copy-start.12 = (s32[4,384]{1,0:T(4,128)S(1)}, s32[4,384]{1,0:T(4,128)}, u32[]{:S(2)}) copy-start(s32[4,384]{1,0:T(4,128)} %param.20) | copy-start | bytes 18436
  53.0 248.5 %all-gather.6.cloned.1.call-start = ((), (), s32[]{:S(2)}) async-start(), calls=%async_computation.3 | async-start | bytes 14598144 | tf_op jit(solution)/shard_map/all_gather | solution.py:164
  56.7 3.1 copy-start.18
  58.4 1.4 copy-start.20
  250.1 5.8 %copy-start.3 = (bf16[1768,768]{1,0:T(8,128)(2,1)S(1)}, bf16[1768,768]{1,0:T(8,128)(2,1)}, u32[]{:S(2)}) copy-start(bf16[1768,768]{1,0:T(8,128)(2,1)} %shard_map.173) | copy-start | bytes 8146948
  279.5 3.6 copy-start.2
  279.5 6.8 %copy-start.15 = (f32[768]{0:T(1024)S(1)}, f32[768]{0:T(1024)}, u32[]{:S(2)}) copy-start(f32[768]{0:T(1024)} %mul.224) | copy-start | bytes 9220
  306.2 8.3 %copy-start.7 = (bf16[1536,768]{1,0:T(8,128)(2,1)S(1)}, bf16[1536,768]{1,0:T(8,128)(2,1)}, u32[]{:S(2)}) copy-start(bf16[1536,768]{1,0:T(8,128)(2,1)} %add_convert_fusion.4) | copy-start | bytes 7077892
  306.2 8.3 %copy-start.17 = (f32[2304]{0:T(1024)S(1)}, f32[2304]{0:T(1024)}, u32[]{:S(2)}) copy-start(f32[2304]{0:T(1024)} %add.368) | copy-start | bytes 27652
  322.3 10.3 %copy-start.19 = (pred[4,384]{1,0:T(4,128)(4,1)S(1)}, pred[4,384]{1,0:T(4,128)(4,1)}, u32[]{:S(2)}) copy-start(pred[4,384]{1,0:T(4,128)(4,1)} %copy-done.18) | copy-start | bytes 4612
  344.8 16.3 %copy-start.21 = (pred[4,384]{1,0:T(4,128)(4,1)S(1)}, pred[4,384]{1,0:T(4,128)(4,1)}, u32[]{:S(2)}) copy-start(pred[4,384]{1,0:T(4,128)(4,1)} %copy-done.20) | copy-start | bytes 4612
  344.8 16.3 %copy-start.25 = (f32[768]{0:T(1024)S(1)}, f32[768]{0:T(1024)}, u32[]{:S(2)}) copy-start(f32[768]{0:T(1024)} %add.371) | copy-start | bytes 9220
  367.3 1.5 copy-start.4
  367.3 2.7 copy-start.6
  367.3 2.7 copy-start.16
  367.3 2.7 copy-start.22
  367.3 2.7 copy-start.23
  370.0 21.5 %copy-start.5 = (bf16[4,384,768]{2,1,0:T(8,128)(2,1)S(1)}, bf16[4,384,768]{2,1,0:T(8,128)(2,1)}, u32[]{:S(2)}) copy-start(bf16[4,384,768]{2,1,0:T(8,128)(2,1)} %copy-done.4) | copy-start | bytes 7077892
  370.0 21.5 %copy-start.24 = (f32[768]{0:T(1024)S(1)}, f32[768]{0:T(1024)}, u32[]{:S(2)}) copy-start(f32[768]{0:T(1024)} %add.382) | copy-start | bytes 9220
  446.3 0.7 copy-start.13
  446.3 0.7 copy-start.14
  446.3 2.6 copy-start.1
Sparse Core Ops, SparseCore 0:
  53.1 82.6 all-gather.3
  138.7 162.7 all-gather.5

commit v2 on v1

--- a/solution.py
+++ b/solution.py
@@ -1,3 +1,5 @@
+import functools
+
 import jax
 import jax.numpy as jnp
 from jax import lax
@@ -5,28 +7,118 @@
 from jax.experimental.pallas import tpu as pltpu
 from jax.sharding import PartitionSpec as P
 
+
 PAD_ID = 1
 LN_EPS = 1e-5
 
 
-def layer_norm(values, ln_gain, ln_shift):
-    row_mean = jnp.mean(values, axis=-1, keepdims=True)
-    centered = values - row_mean
-    row_var = jnp.mean(centered * centered, axis=-1, keepdims=True)
-    return centered * lax.rsqrt(row_var + LN_EPS) * ln_gain + ln_shift
-
-
-def attention(qkv_heads, keep_mask, head_dim):
-    scores = jnp.einsum('bqhd,bkhd->bhqk', qkv_heads[:, :, 0], qkv_heads[:, :, 1],
-                        preferred_element_type=jnp.float32) * head_dim ** -0.5
-    scores = jnp.where(keep_mask[:, None, None, :], scores, -1e30)
-    attn_probs = jax.nn.softmax(scores, axis=-1).astype(jnp.bfloat16)
-    return jnp.einsum('bhqk,bkhd->bqhd', attn_probs, qkv_heads[:, :, 2],
-                      preferred_element_type=jnp.float32).astype(jnp.bfloat16)
+SQRT_HALF = 0.5 ** 0.5
+FFN_PART = 768
+
+
+def norm(z, gain, shift):
+    centered = z - jnp.mean(z, axis=-1, keepdims=True)
+    var = jnp.mean(centered * centered, axis=-1, keepdims=True)
+    return centered * lax.rsqrt(var + LN_EPS) * gain + shift
+
+
+def times(a, b):
+    return jnp.dot(a, b, preferred_element_type=jnp.float32)
+
+
+def times_t(a, b):
+    return lax.dot_general(a, b, (((1,), (1,)), ((), ())), preferred_element_type=jnp.float32)
+
+
+def layer_kernel(dims, spot_ref, keep_col_ref, keep_row_ref, head_ref, got_ref, pos_ref, type_ref, vec_ref, b_qkv_ref, b_in_ref,
+                 w_qkv_ref, w_out_ref, w_in_ref, w_back_ref, out_ref, qkv_ref, ctx_ref, x_ref):
+    heads, size = dims
+    seq, width = out_ref.shape[1:]
+    w_qkv_ref, w_out_ref, w_in_ref, w_back_ref = (
+        r.reshape(r.shape[0] * r.shape[1], width) for r in (w_qkv_ref, w_out_ref, w_in_ref, w_back_ref))
+    spot = spot_ref[0]
+    total = jnp.zeros((seq, width), jnp.float32)
+    step = 256
+    for ref, first in ((head_ref, 0), (got_ref, head_ref.shape[0])):
+        for at in range(0, ref.shape[0], step):
+            hit = spot == lax.broadcasted_iota(jnp.int32, (seq, step), 1) + (first + at)
+            total += times(jnp.where(hit, 1.0, 0.0).astype(jnp.bfloat16), ref[at:at + step, :])
+    kept = keep_col_ref[0] > 0
+    pos = jnp.where(kept, pos_ref[8:8 + seq, :].astype(jnp.float32), pos_ref[0:1, :].astype(jnp.float32))
+    embedded = total + pos + type_ref[...].astype(jnp.float32)
+    x_ref[...] = norm(embedded, vec_ref[0:1, :], vec_ref[1:2, :]).astype(jnp.bfloat16)
+
+    part = 2 * width // 2
+    for at in range(0, 3 * width, part):
+        qkv_ref[:, at:at + part] = (times_t(x_ref[...], w_qkv_ref[at:at + part, :])
+                                    + b_qkv_ref[:, at:at + part]).astype(jnp.bfloat16)
+
+    masked = jnp.where(keep_row_ref[0] > 0, 0.0, -1e30)
+    low = lax.broadcasted_iota(jnp.int32, (1, 2 * size), 1) < size
+    for pair in range(heads // 2):
+        at = pair * 2 * size
+        q = qkv_ref[:, at:at + 2 * size]
+        k = qkv_ref[:, width + at:width + at + 2 * size]
+        v = qkv_ref[:, 2 * width + at:2 * width + at + 2 * size]
+        zero = jnp.zeros_like(q)
+        mixed = []
+        for mine in (low, ~low):
+            s = times_t(jnp.where(mine, q, zero), k) * size ** -0.5 + masked
+            p = jnp.exp(s - jnp.max(s, axis=-1, keepdims=True))
+            p = p * (1.0 / jnp.sum(p, axis=-1, keepdims=True))
+            mixed.append(times(p.astype(jnp.bfloat16), v))
+        ctx_ref[:, at:at + 2 * size] = jnp.where(low, mixed[0], mixed[1]).astype(jnp.bfloat16)
+
+    a = (times_t(ctx_ref[...], w_out_ref[...]) + vec_ref[6:7, :]).astype(jnp.bfloat16)
+    z = x_ref[...].astype(jnp.float32) + a.astype(jnp.float32)
+    x_ref[...] = norm(z, vec_ref[2:3, :], vec_ref[3:4, :]).astype(jnp.bfloat16)
+
+    total = jnp.zeros((seq, width), jnp.float32)
+    for at in range(0, b_in_ref.shape[1], FFN_PART):
+        h = times_t(x_ref[...], w_in_ref[at:at + FFN_PART, :]) + b_in_ref[:, at:at + FFN_PART]
+        h = (0.5 * h * (1.0 + lax.erf(h * SQRT_HALF))).astype(jnp.bfloat16)
+        total += times(h, w_back_ref[at:at + FFN_PART, :])
+    z = x_ref[...].astype(jnp.float32) + (total + vec_ref[7:8, :])
+    out_ref[0] = norm(z, vec_ref[4:5, :], vec_ref[5:6, :]).astype(jnp.bfloat16)
+
+
+def layer(heads, size, spot, keep, head, got, pos_table, type_row, vecs, b_qkv, b_in, weights, sizes):
+    batch, seq = keep.shape
+    width = head.shape[1]
+    ffn = b_in.shape[0]
+    pos = jnp.concatenate([jnp.broadcast_to(pos_table[1:2], (8, width)), pos_table[2:2 + seq]], axis=0)
+    keep = keep.astype(jnp.float32)
+    n_dev = weights.shape[0]
+
+    def whole(*shape):
+        return pl.BlockSpec(shape, lambda b: (0,) * len(shape), pipeline_mode=pl.Buffered(1))
+
+    def each(*shape):
+        return pl.BlockSpec((1,) + shape, lambda b: (b,) + (0,) * len(shape))
+
+    pieces, at = [], 0
+    for rows in sizes:
+        pieces.append(pl.BlockSpec((n_dev, rows, width), functools.partial(lambda i, b: (0, i, 0), at // rows),
+                                   pipeline_mode=pl.Buffered(1)))
+        at += rows
+
+    return pl.pallas_call(
+        functools.partial(layer_kernel, (heads, size)),
+        out_shape=jax.ShapeDtypeStruct((batch, seq, width), jnp.bfloat16),
+        grid=(batch,),
+        in_specs=[each(seq, 1), each(seq, 1), each(1, seq), whole(*head.shape), whole(*got.shape), whole(*pos.shape),
+                  whole(1, width), whole(8, width), whole(1, 3 * width), whole(1, ffn)] + pieces,
+        out_specs=each(seq, width),
+        scratch_shapes=[pltpu.VMEM((seq, 3 * width), jnp.bfloat16), pltpu.VMEM((seq, width), jnp.bfloat16),
+                        pltpu.VMEM((seq, width), jnp.bfloat16)],
+        compiler_params=pltpu.CompilerParams(vmem_limit_bytes=60 << 20),
+        cost_estimate=pl.CostEstimate(flops=40 * 10 ** 9, bytes_accessed=30 * 10 ** 6, transcendentals=10 ** 7))(
+            spot.reshape(batch, seq, 1), keep[:, :, None], keep[:, None, :], head, got, pos, type_row[None, :], vecs,
+            b_qkv[None, :], b_in[None, :], *([weights] * len(sizes)))
 
 
 HEAD = 2048
-CAPS = ((0, 1, 184), (1, 2, 96), (2, 4, 72), (4, 32, 48))
+CAPS = ((0, 1, 192), (1, 2, 96), (2, 4, 80), (4, 32, 48))
 EXTRA = 48
 MESH = pl.DeviceIdType.MESH
 
@@ -162,11 +254,6 @@
         pieces = [w_qkv.T, w_out.reshape(num_heads * head_dim, -1).T, w_ffn_in.T, w_ffn_out]
         sizes = [p.shape[0] for p in pieces]
         weights = lax.all_gather(jnp.concatenate(pieces, axis=0), 'fsdp', axis=0, tiled=False)
-        full, at = [], 0
-        for size in sizes:
-            full.append(weights[:, at:at + size].reshape(n_dev * size, width))
-            at += size
-        w_qkv_t, w_out_t, w_in_t, w_back = full
 
         ids = token_ids.reshape(n_tok)
         keep = ids != PAD_ID
@@ -213,7 +300,6 @@
         rows = jnp.take(tok_shard, wanted.reshape(-1), axis=0, mode='clip').reshape(n_dev, most, width)
         got = swap(n_dev, rows)
         spot = jnp.where(ids < HEAD, ids, HEAD + jnp.maximum(slot, 0))
-        tok_rows = jnp.take(jnp.concatenate([head, got], axis=0), spot, axis=0, mode='clip')
 
         caps = jnp.concatenate([jnp.full((hi - lo,), c, jnp.float32) for lo, hi, c in CAPS])
         left = jnp.max(told[:, wide:wide + n_dev] - caps[None, :])
@@ -232,30 +318,18 @@
             new = jnp.take(back, jnp.where(live, at_slot, 0), axis=0, mode='clip')
             return r + 1, jnp.where(live[:, None], new, rows_now)
 
-        _, tok_rows = lax.while_loop(lambda state: state[0] < rounds, again, (jnp.int32(0), tok_rows))
-        tok_rows = tok_rows.reshape(batch_dev, seq_len, width)
-
-        keep_mask = token_ids != PAD_ID
-        keep_int = keep_mask.astype(jnp.int32)
-        positions = jnp.cumsum(keep_int, axis=1) * keep_int + 1
-        embedded = (tok_rows.astype(jnp.float32) + jnp.take(pos_table, positions, axis=0).astype(jnp.float32)
-                    + type_row.astype(jnp.float32))
-        x_embed = layer_norm(embedded, emb_g, emb_b).astype(jnp.bfloat16)
-        qkv_rows = (jnp.einsum('btd,ed->bte', x_embed, w_qkv_t, preferred_element_type=jnp.float32)
-                    + b_qkv_f).astype(jnp.bfloat16)
-        qkv_heads = qkv_rows.reshape(batch_dev, seq_len, 3, num_heads, head_dim)
-        context = attention(qkv_heads, keep_mask, head_dim).reshape(batch_dev, seq_len, width)
-        attn_out = (jnp.einsum('bqc,ec->bqe', context, w_out_t, preferred_element_type=jnp.float32)
-                    + b_out_f).astype(jnp.bfloat16)
-        x_attn = layer_norm(x_embed.astype(jnp.float32) + attn_out.astype(jnp.float32), ln1_g, ln1_b).astype(jnp.bfloat16)
-        hidden = jax.nn.gelu(jnp.einsum('btd,fd->btf', x_attn, w_in_t, preferred_element_type=jnp.float32)
-                             + b_in_f, approximate=False).astype(jnp.bfloat16)
-        ffn_out = jnp.einsum('btf,fd->btd', hidden, w_back, preferred_element_type=jnp.float32) + b_back_f
-        return layer_norm(x_attn.astype(jnp.float32) + ffn_out, ln2_g, ln2_b).astype(jnp.bfloat16)
+        def slow(got_now, spot_now):
+            rows_now = jnp.take(jnp.concatenate([head, got_now], axis=0), spot_now, axis=0, mode='clip')
+            _, rows_now = lax.while_loop(lambda state: state[0] < rounds, again, (jnp.int32(0), rows_now))
+            return jnp.pad(rows_now, ((0, slots - n_tok), (0, 0))), HEAD + place
+
+        got, spot = lax.cond(rounds > 0, slow, lambda g, p: (g, p), got, spot)
+        vecs = jnp.stack([emb_g, emb_b, ln1_g, ln1_b, ln2_g, ln2_b, b_out_f, b_back_f])
+        return layer(num_heads, head_dim, spot, token_ids != PAD_ID, head, got, pos_table, type_row, vecs, b_qkv_f, b_in_f,
+                     weights, sizes)
 
     vec_spec = P('fsdp')
     in_specs = (P('fsdp', None), P('fsdp', None), P(None, None), P(None), vec_spec, vec_spec,
                 P(None, 'fsdp'), vec_spec, P(None, None, 'fsdp'), vec_spec, vec_spec, vec_spec,
                 P(None, 'fsdp'), vec_spec, P('fsdp', None), vec_spec, vec_spec, vec_spec)
-    return jax.shard_map(local_step, mesh=mesh, in_specs=in_specs, out_specs=P('fsdp', None, None),
-                         check_vma=False)
+    return jax.shard_map(local_step, mesh=mesh, in_specs=in_specs, out_specs=P('fsdp', None, None), check_vma=False)

time: 465 us -> 380 us (0.82); the launches traced: 456 us -> 380 us
  matrix products: 120 us -> 1.26 us
  Pallas kernels: 194 us -> 309 us
  local copies, waits for them, and re-layouts: 83 us -> 50.8 us
  other arithmetic: 24.4 us -> 4.23 us
  waiting for transfers between devices: 11.2 us -> 0.04 us
  loops' own time: 8.73 us -> 0.23 us
    dot_general x5 -> x0, matrix products: 107 us -> none  [the longest x1 54.8 us: local_step(): jnp.einsum('btf,fd->btd', hidden, w_back, preferred_element_type=jnp.floa...]
    pallas_call x0 -> x1, Pallas kernels: none -> 72.7 us  [layer(): pl.pallas_call(functools.partial(layer_kernel, (heads, size)), out_shape=...]
    pallas_call x1, Pallas kernels: 152 us -> 194 us  [swap(): pl.pallas_call(lambda *refs: swap_kernel(n, *refs), out_shape=jax.ShapeDt...]
    gather x2 -> x0, local copies, waits for them, and re-layouts: 15.7 us -> none  [the longest x1 10.1 us: local_step(): jnp.take(jnp.concatenate([head, got], axis=0), spot, axis=0, mode='clip')]
    sub x1 -> x0, matrix products: 12.2 us -> none  [attention(): attn_probs = jax.nn.softmax(scores, axis=-1).astype(jnp.bfloat16)]
    slice x4 -> x2, local copies, waits for them, and re-layouts: 13.2 us -> 1.93 us  [the longest x1 1.2 us: layer(): pos_table[2:2 + seq]]
    all_gather x1, waiting for transfers between devices: 11.1 us -> 0.01 us  [local_step(): lax.all_gather(jnp.concatenate(pieces, axis=0), 'fsdp', axis=0, tiled=False)]
    convert_element_type x1 -> x0, local copies, waits for them, and re-layouts: 10.3 us -> none  [local_step(): qkv_rows = (jnp.einsum('btd,ed->bte', x_embed, w_qkv_t, preferred_element...]
  transfers between devices with their start and end apart: 2 -> 2, of which waited for: 1 -> 0; matrix products, arithmetic and copies ran while one was open for 17% -> 14% of each run, Pallas kernels for 33% -> 51%
where the time goes in v2:
time: 380 us
  Pallas kernels  309 us (81%)
  local copies, waits for them, and re-layouts  50.8 us (13%)
  between operations  14.5 us (4%)
  other arithmetic  4.23 us (1%)
    pallas_call x1, Pallas kernels, swap(): pl.pallas_call(lambda *refs: swap_kernel(n, *refs), out_shape=jax.ShapeDt...  194 us
    pallas_call x1, Pallas kernels, layer(): pl.pallas_call(functools.partial(layer_kernel, (heads, size)), out_shape=...  72.7 us
    pallas_call x1, Pallas kernels, tell(): pl.pallas_call(lambda *refs: tell_kernel(n, part, *refs), out_shape=(jax....  41.7 us
    gather x1, local copies, waits for them, and re-layouts, local_step(): jnp.take(tok_shard, wanted.reshape(-1), axis=0, mode='clip')  39.2 us
  transfers between devices with their start and end apart: 2, of which 0 were waited for; matrix products, arithmetic and copies ran while one was open for 14% of the time, Pallas kernels for 51%

profile of v2, /device:TPU:0, one launch (start us, length us, event | category | flops | bytes accessed | tf_op | source)
XLA Modules:
  0.0 379.7 jit_solution(1980259041253006152)
XLA Ops:
  6.5 0.7 reshape.264
  7.3 0.0 copy-start.6
  7.3 0.0 copy-start.7
  7.3 0.0 copy-start.8
  7.3 0.0 copy-start.11
  7.3 0.0 copy-start.12
  7.4 0.0 copy-start.15
  7.4 1.3 fusion.5
  8.7 0.3 convert_reduce_fusion
  9.0 1.5 select_reduce_fusion.1
  10.6 0.1 concatenate.12
  10.7 0.6 pad_bitcast_fusion.refs_0_
  11.3 0.0 copy-start.16
  11.3 41.7 %shard_map.172 = (f32[32,24,128]{2,1,0:T(8,128)}, bf16[64,768]{1,0:T(8,128)(2,1)}) custom-call(f32[24,128]{1,0:T(8,128)} %pad_bitcast_fusion.refs_0_, bf16[15664,768]{1,0:T(8,128)(2,1)} %refs_1_.1), custom_call_target="tpu_custom_call" | custom-call | tf_op jit(solution)/shard_map/pallas_call | solution.py:178
  53.0 0.0 all-gather.4.cloned.1.call-update
  53.0 0.0 all-gather.6.cloned.1.call-start
  53.1 0.1 reshape.268
  53.2 0.8 pad_maximum_fusion.2
  54.0 0.0 all-gather.6.cloned.1.call-update
  54.1 1.1 copy.29
  55.1 0.6 fusion.10
  56.4 0.1 slice.77
  56.5 0.1 slice.76
  56.6 0.1 subtract_clamp_fusion
  56.7 0.1 reshape.295
  56.8 39.2 %gather_fusion.3 = bf16[6144,768]{1,0:T(8,128)(2,1)} fusion(bf16[15664,768]{1,0:T(8,128)(2,1)} %refs_1_.1, s32[6144]{0:T(1024)S(1)} %broadcast_clamp_fusion), kind=kCustom, calls=%fused_computation.3 | custom fusion | bytes 18898944 | tf_op jit(solution)/shard_map/jit(_take)/gather | solution.py:300
  96.0 194.4 %shard_map.173 = bf16[1792,768]{1,0:T(8,128)(2,1)S(1)} custom-call(bf16[32,192,768]{2,1,0:T(8,128)(2,1)} %bitcast.26), custom_call_target="tpu_custom_call" | custom-call | tf_op jit(solution)/shard_map/pallas_call | solution.py:237
  290.4 0.1 fusion.15
  290.5 0.1 stack_reshape.24
  290.6 0.1 stack_reshape.25
  290.7 0.1 stack_reshape.26
  290.8 0.1 stack_reshape.27
  290.9 0.1 stack_reshape.28
  291.0 0.1 stack_reshape.29
  291.1 0.1 stack_reshape.30
  291.1 0.1 stack_reshape.31
  291.2 0.7 broadcast_in_dim_reshape.7.b_in_ref
  291.9 0.7 broadcast_in_dim_reshape.6.b_qkv_ref
  292.6 1.2 copy.26.keep_col_ref
  293.8 0.6 broadcast_in_dim.99.keep_row_ref
  294.4 1.2 slice.47
  295.6 0.6 broadcast_in_dim.102.type_ref
  296.2 0.6 stack.3.vec_ref
  296.9 0.7 slice_reduce_fusion
  297.6 0.9 pad_maximum_fusion.1.pos_ref
  298.5 0.2 conditional.1
  298.7 1.5 reshape.314.spot_ref
  300.2 72.7 %shard_map.174 = bf16[4,384,768]{2,1,0:T(8,128)(2,1)} custom-call(s32[4,384,1]{2,1,0:T(8,128)} %reshape.314.spot_ref, f32[4,384,1]{2,1,0:T(8,128)} %copy.26.keep_col_ref, f32[4,1,384]{2,1,0:T(1,128)} %broadcast_in_dim.99.keep_row_ref, bf16[2048,768]{1,0:T(8,128)(2,1)} %all-gather.4.cloned.1.call-done.head_ref, ...), custom_call_target="tpu_custom_call" | custom-call | flops 40000000000 | bytes 30000000 | tf_op jit(solution)/shard_map/pallas_call | solution.py:105
  (40 shorter events, 0.2 us)
Async XLA Ops:
  6.5 291.9 %all-gather.4.cloned.1.call-start = ((), (), s32[]{:S(2)}) async-start(), calls=%async_computation.2 | async-start | bytes 3244032 | tf_op jit(solution)/shard_map/all_gather | solution.py:286
  7.3 3.2 copy-start.6
  7.3 3.2 copy-start.7
  7.3 3.2 copy-start.8
  7.3 3.2 copy-start.9
  7.3 3.2 copy-start.10
  7.3 3.2 copy-start.11
  7.3 3.2 copy-start.12
  7.4 3.2 copy-start.13
  7.4 3.2 copy-start.14
  7.4 3.2 copy-start.15
  11.3 41.8 %copy-start.3 = (bf16[12,64,24]{1,2,0:T(8,128)(2,1)S(1)}, bf16[12,64,24]{1,2,0:T(8,128)(2,1)}, u32[]{:S(2)}) copy-start(bf16[12,64,24]{1,2,0:T(8,128)(2,1)} %param.30) | copy-start | bytes 110596
  11.3 41.9 %copy-start = (bf16[96,768]{1,0:T(8,128)(2,1)S(1)}, bf16[96,768]{1,0:T(8,128)(2,1)}, u32[]{:S(2)}) copy-start(bf16[96,768]{1,0:T(8,128)(2,1)} %param.36) | copy-start | bytes 442372
  11.3 41.9 %copy-start.1 = (bf16[768,96]{0,1:T(8,128)(2,1)S(1)}, bf16[768,96]{0,1:T(8,128)(2,1)}, u32[]{:S(2)}) copy-start(bf16[768,96]{0,1:T(8,128)(2,1)} %param.34) | copy-start | bytes 442372
  11.3 41.9 %copy-start.2 = (bf16[768,72]{0,1:T(8,128)(2,1)S(1)}, bf16[768,72]{0,1:T(8,128)(2,1)}, u32[]{:S(2)}) copy-start(bf16[768,72]{0,1:T(8,128)(2,1)} %param.28) | copy-start | bytes 331780
  11.3 43.8 %copy-start.16 = (f32[32]{0:T(128)S(1)}, f32[32]{0:T(128)}, u32[]{:S(2)}) copy-start(f32[32]{0:T(128)} %constant.119.clone.1) | copy-start | bytes 388
  53.0 247.2 %all-gather.6.cloned.1.call-start = ((), (), s32[]{:S(2)}) async-start(), calls=%async_computation.3 | async-start | bytes 14598144 | tf_op jit(solution)/shard_map/all_gather | solution.py:256
  96.0 196.6 %copy-start.4 = (s32[4,384]{1,0:T(4,128)S(1)}, s32[4,384]{1,0:T(4,128)}, u32[]{:S(2)}) copy-start(s32[4,384]{1,0:T(4,128)} %param.22) | copy-start | bytes 18436
  96.0 199.6 %copy-start.5 = (bf16[768]{0:T(1024)(128)(2,1)S(1)}, bf16[768]{0:T(1024)(128)(2,1)}, u32[]{:S(2)}) copy-start(bf16[768]{0:T(1024)(128)(2,1)} %param.25) | copy-start | bytes 4612
Sparse Core Ops, SparseCore 0:
  53.1 86.2 all-gather.3
  142.3 141.6 all-gather.5

commit v3 on v2

--- a/solution.py
+++ b/solution.py
@@ -30,7 +30,7 @@
     return lax.dot_general(a, b, (((1,), (1,)), ((), ())), preferred_element_type=jnp.float32)
 
 
-def layer_kernel(dims, spot_ref, keep_col_ref, keep_row_ref, head_ref, got_ref, pos_ref, type_ref, vec_ref, b_qkv_ref, b_in_ref,
+def layer_kernel(dims, spot_ref, spot_row_ref, head_ref, got_ref, pos_ref, type_ref, vec_ref, b_qkv_ref, b_in_ref,
                  w_qkv_ref, w_out_ref, w_in_ref, w_back_ref, out_ref, qkv_ref, ctx_ref, x_ref):
     heads, size = dims
     seq, width = out_ref.shape[1:]
@@ -43,8 +43,7 @@
         for at in range(0, ref.shape[0], step):
             hit = spot == lax.broadcasted_iota(jnp.int32, (seq, step), 1) + (first + at)
             total += times(jnp.where(hit, 1.0, 0.0).astype(jnp.bfloat16), ref[at:at + step, :])
-    kept = keep_col_ref[0] > 0
-    pos = jnp.where(kept, pos_ref[8:8 + seq, :].astype(jnp.float32), pos_ref[0:1, :].astype(jnp.float32))
+    pos = jnp.where(spot != PAD_ID, pos_ref[2:2 + seq, :].astype(jnp.float32), pos_ref[1:2, :].astype(jnp.float32))
     embedded = total + pos + type_ref[...].astype(jnp.float32)
     x_ref[...] = norm(embedded, vec_ref[0:1, :], vec_ref[1:2, :]).astype(jnp.bfloat16)
 
@@ -53,7 +52,7 @@
         qkv_ref[:, at:at + part] = (times_t(x_ref[...], w_qkv_ref[at:at + part, :])
                                     + b_qkv_ref[:, at:at + part]).astype(jnp.bfloat16)
 
-    masked = jnp.where(keep_row_ref[0] > 0, 0.0, -1e30)
+    masked = jnp.where(spot_row_ref[0] != PAD_ID, 0.0, -1e30)
     low = lax.broadcasted_iota(jnp.int32, (1, 2 * size), 1) < size
     for pair in range(heads // 2):
         at = pair * 2 * size
@@ -82,12 +81,10 @@
     out_ref[0] = norm(z, vec_ref[4:5, :], vec_ref[5:6, :]).astype(jnp.bfloat16)
 
 
-def layer(heads, size, spot, keep, head, got, pos_table, type_row, vecs, b_qkv, b_in, weights, sizes):
-    batch, seq = keep.shape
+def layer(heads, size, batch, spot, head, got, pos_table, type_row, vecs, b_qkv, b_in, weights, sizes):
+    seq = spot.shape[0] // batch
     width = head.shape[1]
     ffn = b_in.shape[0]
-    pos = jnp.concatenate([jnp.broadcast_to(pos_table[1:2], (8, width)), pos_table[2:2 + seq]], axis=0)
-    keep = keep.astype(jnp.float32)
     n_dev = weights.shape[0]
 
     def whole(*shape):
@@ -106,20 +103,22 @@
         functools.partial(layer_kernel, (heads, size)),
         out_shape=jax.ShapeDtypeStruct((batch, seq, width), jnp.bfloat16),
         grid=(batch,),
-        in_specs=[each(seq, 1), each(seq, 1), each(1, seq), whole(*head.shape), whole(*got.shape), whole(*pos.shape),
+        in_specs=[each(seq, 1), each(1, seq), whole(*head.shape), whole(*got.shape), whole(*pos_table.shape),
                   whole(1, width), whole(8, width), whole(1, 3 * width), whole(1, ffn)] + pieces,
         out_specs=each(seq, width),
         scratch_shapes=[pltpu.VMEM((seq, 3 * width), jnp.bfloat16), pltpu.VMEM((seq, width), jnp.bfloat16),
                         pltpu.VMEM((seq, width), jnp.bfloat16)],
         compiler_params=pltpu.CompilerParams(vmem_limit_bytes=60 << 20),
         cost_estimate=pl.CostEstimate(flops=40 * 10 ** 9, bytes_accessed=30 * 10 ** 6, transcendentals=10 ** 7))(
-            spot.reshape(batch, seq, 1), keep[:, :, None], keep[:, None, :], head, got, pos, type_row[None, :], vecs,
+            spot.reshape(batch, seq, 1), spot.reshape(batch, 1, seq), head, got, pos_table, type_row[None, :], vecs,
             b_qkv[None, :], b_in[None, :], *([weights] * len(sizes)))
 
 
 HEAD = 2048
-CAPS = ((0, 1, 192), (1, 2, 96), (2, 4, 80), (4, 32, 48))
+CAPS = ((0, 1, 176), (1, 2, 96), (2, 4, 72), (4, 8, 56), (8, 32, 48))
+HOT = 2
 EXTRA = 48
+PLANE = 8
 MESH = pl.DeviceIdType.MESH
 
 
@@ -137,17 +136,24 @@
     pl.semaphore_wait(barrier, n - 1)
 
 
-def tell_kernel(n, part, msg_ref, table_ref, told_ref, piece_ref, send_sem, recv_sem, out_sem, in_sem, own_sem):
+def tell_kernel(n, part, msg_ref, table_ref, told_ref, piece_ref, relay_ref, send_sem, recv_sem, out_sem, in_sem, relay_sem,
+                own_sem):
     me = lax.axis_index('fsdp')
+    planes = n // PLANE
+    group = part * planes
     meet(n, me)
 
     def note(k, dev, slot):
         return pltpu.make_async_remote_copy(msg_ref, told_ref.at[slot], send_sem.at[k], recv_sem.at[slot],
                                             device_id=(dev,), device_id_type=MESH)
 
-    def head(dev):
-        return pltpu.make_async_remote_copy(table_ref.at[pl.ds(pl.multiple_of(dev * part, 8), part)], piece_ref,
-                                            out_sem.at[dev], in_sem, device_id=(dev,), device_id_type=MESH)
+    def lend(p):
+        return pltpu.make_async_remote_copy(table_ref.at[pl.ds(p * group, group)], relay_ref, out_sem.at[p], relay_sem,
+                                            device_id=(p,), device_id_type=MESH)
+
+    def part_of(ref, z, dev):
+        return pltpu.make_async_remote_copy(ref.at[pl.ds(z * part, part)], piece_ref, out_sem.at[PLANE + z], in_sem,
+                                            device_id=(dev,), device_id_type=MESH)
 
     def own():
         return pltpu.make_async_copy(table_ref.at[pl.ds(0, part)], piece_ref, own_sem)
@@ -156,21 +162,40 @@
 
     @pl.when(me == 0)
     def _():
-        others(n, me, lambda k, dev: head(dev).start())
+        for p in range(PLANE - 1, 0, -1):
+            lend(p).start()
+        for z in range(1, planes):
+            part_of(table_ref, z, z * PLANE).start()
         own().start()
 
     told_ref[me] = msg_ref[...]
+
+    @pl.when((me > 0) & (me < PLANE))
+    def _():
+        lend(0).wait_recv()
+        for z in range(planes - 1, 0, -1):
+            part_of(relay_ref, z, z * PLANE + me).start()
+        piece_ref[...] = relay_ref[0:part, :]
+
     others(n, me, lambda k, dev: note(k, dev, dev).wait_recv())
     others(n, me, lambda k, dev: note(k, dev, me).wait_send())
 
     @pl.when(me == 0)
     def _():
         own().wait()
-        others(n, me, lambda k, dev: head(dev).wait_send())
-
-    @pl.when(me != 0)
+        for p in range(1, PLANE):
+            lend(p).wait_send()
+        for z in range(1, planes):
+            part_of(table_ref, z, z * PLANE).wait_send()
+
+    @pl.when((me > 0) & (me < PLANE))
     def _():
-        head(me).wait_recv()
+        for z in range(1, planes):
+            part_of(relay_ref, z, z * PLANE + me).wait_send()
+
+    @pl.when(me >= PLANE)
+    def _():
+        part_of(relay_ref, 0, me).wait_recv()
 
 
 def tell(n, msg, table):
@@ -181,9 +206,18 @@
                    jax.ShapeDtypeStruct((part, table.shape[1]), table.dtype)),
         in_specs=[pl.BlockSpec(memory_space=pltpu.VMEM), pl.BlockSpec(memory_space=pl.ANY)],
         out_specs=(pl.BlockSpec(memory_space=pltpu.VMEM), pl.BlockSpec(memory_space=pltpu.VMEM)),
-        scratch_shapes=[pltpu.SemaphoreType.DMA((n,)), pltpu.SemaphoreType.DMA((n,)), pltpu.SemaphoreType.DMA((n,)),
-                        pltpu.SemaphoreType.DMA, pltpu.SemaphoreType.DMA],
+        scratch_shapes=[pltpu.VMEM((part * (n // PLANE), table.shape[1]), table.dtype),
+                        pltpu.SemaphoreType.DMA((n,)), pltpu.SemaphoreType.DMA((n,)),
+                        pltpu.SemaphoreType.DMA((PLANE + n // PLANE,)), pltpu.SemaphoreType.DMA, pltpu.SemaphoreType.DMA,
+                        pltpu.SemaphoreType.DMA],
         compiler_params=pltpu.CompilerParams(collective_id=0, has_side_effects=True))(msg, table)
+
+
+def head_spot(n, ids):
+    part = HEAD // n
+    planes = n // PLANE
+    at = ids // part
+    return ((at % planes) * PLANE + at // planes) * part + ids % part
 
 
 def bases():
@@ -194,8 +228,13 @@
     return out, at
 
 
-def swap_kernel(n, send_ref, recv_ref, send_sem, recv_sem, own_sem):
+def relayed(p, z):
+    return z > 0 and 2 <= p and p < PLANE - 1 and (p, z) != (PLANE - 2, 3)
+
+
+def swap_kernel(n, send_ref, recv_ref, relay_ref, send_sem, recv_sem, lend_sem, pass_sem, own_sem):
     me = lax.axis_index('fsdp')
+    planes = n // PLANE
     meet(n, me)
     starts, _ = bases()
 
@@ -203,18 +242,60 @@
         lo, _, cap = CAPS[c]
         return recv_ref.at[pl.ds(pl.multiple_of(starts[c] + (dev - lo) * cap, 8), cap)]
 
+    def block(c, dev):
+        return send_ref.at[lax.rem(dev, PLANE) * planes + lax.div(dev, PLANE), pl.ds(0, CAPS[c][2])]
+
     def row(c, k, dev, owner):
-        return pltpu.make_async_remote_copy(send_ref.at[dev, pl.ds(0, CAPS[c][2])], spot(c, owner), send_sem.at[k],
-                                            recv_sem.at[owner], device_id=(dev,), device_id_type=MESH)
+        return pltpu.make_async_remote_copy(block(c, dev), spot(c, owner), send_sem.at[k], recv_sem.at[owner],
+                                            device_id=(dev,), device_id_type=MESH)
+
+    def held(c, z):
+        return relay_ref.at[c, z - 1, pl.ds(0, CAPS[c][2])]
+
+    def lend(c, p, z):
+        return pltpu.make_async_remote_copy(send_ref.at[p * planes + z, pl.ds(0, CAPS[c][2])], held(c, z),
+                                            send_sem.at[z * PLANE + p], lend_sem.at[c, z - 1], device_id=(p,),
+                                            device_id_type=MESH)
+
+    def hand_on(c, z):
+        return pltpu.make_async_remote_copy(held(c, z), spot(c, c), pass_sem.at[c, z - 1], recv_sem.at[c],
+                                            device_id=(z * PLANE + me,), device_id_type=MESH)
 
     def own(c):
-        return pltpu.make_async_copy(send_ref.at[me, pl.ds(0, CAPS[c][2])], spot(c, me), own_sem)
+        return pltpu.make_async_copy(block(c, me), spot(c, me), own_sem)
+
+    def hot_sends(c):
+        for z in range(planes - 1, -1, -1):
+            for p in range(PLANE):
+                dev = z * PLANE + p
+                if relayed(p, z):
+                    yield lend(c, p, z)
+                elif dev != c:
+                    yield row(c, dev, jnp.int32(dev), c)
+
+    def relays():
+        for p in range(PLANE):
+            zs = [z for z in range(planes - 1, 0, -1) if relayed(p, z)]
+            if zs:
+                yield p, zs
 
     for c, (lo, hi, cap) in enumerate(CAPS):
         @pl.when((me >= lo) & (me < hi))
         def _(c=c):
-            others(n, me, lambda k, dev: row(c, k, dev, me).start())
             own(c).start()
+            if c < HOT:
+                for copy in hot_sends(c):
+                    copy.start()
+            else:
+                others(n, me, lambda k, dev: row(c, k, dev, me).start())
+
+    for p, zs in relays():
+        @pl.when(me == p)
+        def _(zs=zs):
+            for z in zs:
+                for c in range(HOT):
+                    lend(c, 0, z).wait_recv()
+                    hand_on(c, z).start()
 
     for c, (lo, hi, cap) in enumerate(CAPS):
         def one(dev, carry, c=c):
@@ -229,16 +310,31 @@
     for c, (lo, hi, cap) in enumerate(CAPS):
         @pl.when((me >= lo) & (me < hi))
         def _(c=c):
-            others(n, me, lambda k, dev: row(c, k, dev, me).wait_send())
             own(c).wait()
+            if c < HOT:
+                for copy in hot_sends(c):
+                    copy.wait_send()
+            else:
+                others(n, me, lambda k, dev: row(c, k, dev, me).wait_send())
+
+    for p, zs in relays():
+        @pl.when(me == p)
+        def _(zs=zs):
+            for z in zs:
+                for c in range(HOT):
+                    hand_on(c, z).wait_send()
 
 
 def swap(n, rows):
+    planes = n // PLANE
+    most = max(cap for _, _, cap in CAPS[:HOT])
     return pl.pallas_call(
         lambda *refs: swap_kernel(n, *refs),
         out_shape=jax.ShapeDtypeStruct((bases()[1], rows.shape[2]), rows.dtype),
         in_specs=[pl.BlockSpec(memory_space=pl.ANY)], out_specs=pl.BlockSpec(memory_space=pl.ANY),
-        scratch_shapes=[pltpu.SemaphoreType.DMA((n,)), pltpu.SemaphoreType.DMA((n,)), pltpu.SemaphoreType.DMA],
+        scratch_shapes=[pltpu.VMEM((HOT, planes - 1, most, rows.shape[2]), rows.dtype), pltpu.SemaphoreType.DMA((n,)),
+                        pltpu.SemaphoreType.DMA((n,)), pltpu.SemaphoreType.DMA((HOT, planes - 1)),
+                        pltpu.SemaphoreType.DMA((HOT, planes - 1)), pltpu.SemaphoreType.DMA],
         compiler_params=pltpu.CompilerParams(collective_id=1, has_side_effects=True))(rows)
 
 
@@ -297,9 +393,10 @@
         most = max(c for _, _, c in CAPS)
         wanted = lax.dynamic_slice(told, (0, my_base), (n_dev, most)).astype(jnp.int32) - me * shard_rows
         wanted = jnp.clip(wanted, 0, shard_rows - 1)
+        wanted = wanted.reshape(n_dev // PLANE, PLANE, most).transpose(1, 0, 2)
         rows = jnp.take(tok_shard, wanted.reshape(-1), axis=0, mode='clip').reshape(n_dev, most, width)
         got = swap(n_dev, rows)
-        spot = jnp.where(ids < HEAD, ids, HEAD + jnp.maximum(slot, 0))
+        spot = jnp.where(ids < HEAD, head_spot(n_dev, ids), HEAD + jnp.maximum(slot, 0))
 
         caps = jnp.concatenate([jnp.full((hi - lo,), c, jnp.float32) for lo, hi, c in CAPS])
         left = jnp.max(told[:, wide:wide + n_dev] - caps[None, :])
@@ -321,11 +418,11 @@
         def slow(got_now, spot_now):
             rows_now = jnp.take(jnp.concatenate([head, got_now], axis=0), spot_now, axis=0, mode='clip')
             _, rows_now = lax.while_loop(lambda state: state[0] < rounds, again, (jnp.int32(0), rows_now))
-            return jnp.pad(rows_now, ((0, slots - n_tok), (0, 0))), HEAD + place
+            return jnp.pad(rows_now, ((0, slots - n_tok), (0, 0))), jnp.where(ids == PAD_ID, spot_now, HEAD + place)
 
         got, spot = lax.cond(rounds > 0, slow, lambda g, p: (g, p), got, spot)
         vecs = jnp.stack([emb_g, emb_b, ln1_g, ln1_b, ln2_g, ln2_b, b_out_f, b_back_f])
-        return layer(num_heads, head_dim, spot, token_ids != PAD_ID, head, got, pos_table, type_row, vecs, b_qkv_f, b_in_f,
+        return layer(num_heads, head_dim, batch_dev, spot, head, got, pos_table, type_row, vecs, b_qkv_f, b_in_f,
                      weights, sizes)
 
     vec_spec = P('fsdp')

time: 380 us -> 353 us (0.929)
  Pallas kernels: 309 us -> 195 us
  waiting for transfers between devices: 0.04 us -> 98 us
  local copies, waits for them, and re-layouts: 50.8 us -> 40.6 us
    pallas_call x1, Pallas kernels: 194 us -> 91.1 us  [swap(): pl.pallas_call(lambda *refs: swap_kernel(n, *refs), out_shape=jax.ShapeDt...]
    all_gather x1, waiting for transfers between devices: 0.01 us -> 97.9 us  [local_step(): lax.all_gather(jnp.concatenate(pieces, axis=0), 'fsdp', axis=0, tiled=False)]
    pallas_call x1, Pallas kernels: 41.7 us -> 31.1 us  [tell(): pl.pallas_call(lambda *refs: tell_kernel(n, part, *refs), out_shape=(jax....]
    gather x1, local copies, waits for them, and re-layouts: 39.2 us -> 32.1 us  [local_step(): jnp.take(tok_shard, wanted.reshape(-1), axis=0, mode='clip')]
  transfers between devices with their start and end apart: 2 -> 2, of which waited for: 0 -> 1; matrix products, arithmetic and copies ran while one was open for 14% -> 12% of each run, Pallas kernels for 51% -> 26%
where the time goes in v3:
time: 353 us
  Pallas kernels  195 us (55%)
  waiting for transfers between devices  98 us (28%)
  local copies, waits for them, and re-layouts  40.6 us (12%)
  between operations  14.5 us (4%)
    all_gather x1, waiting for transfers between devices, local_step(): lax.all_gather(jnp.concatenate(pieces, axis=0), 'fsdp', axis=0, tiled=False)  97.9 us
    pallas_call x1, Pallas kernels, swap(): pl.pallas_call(lambda *refs: swap_kernel(n, *refs), out_shape=jax.ShapeDt...  91.1 us
    pallas_call x1, Pallas kernels, layer(): pl.pallas_call(functools.partial(layer_kernel, (heads, size)), out_shape=...  72.8 us
    gather x1, local copies, waits for them, and re-layouts, local_step(): jnp.take(tok_shard, wanted.reshape(-1), axis=0, mode='clip')  32.1 us
    pallas_call x1, Pallas kernels, tell(): pl.pallas_call(lambda *refs: tell_kernel(n, part, *refs), out_shape=(jax....  31.1 us
  transfers between devices with their start and end apart: 2, of which 1 were waited for; matrix products, arithmetic and copies ran while one was open for 12% of the time, Pallas kernels for 26%

profile of v3, /device:TPU:0, one launch (start us, length us, event | category | flops | bytes accessed | tf_op | source)
XLA Modules:
  0.0 352.9 jit_solution(1470881104707414776)
XLA Ops:
  6.5 0.7 reshape.276
  7.3 0.0 copy-start.5
  7.3 0.0 copy-start.6
  7.3 0.0 copy-start.7
  7.3 0.0 copy-start.8
  7.3 0.0 copy-start.9
  7.3 0.0 copy-start.10
  7.3 0.0 copy-start.11
  7.4 0.0 copy-start.12
  7.4 0.0 copy-start.14
  7.4 1.3 fusion.5
  8.7 0.3 convert_reduce_fusion
  9.0 1.5 select_reduce_fusion.1
  10.6 0.1 concatenate.9
  10.7 0.6 pad_bitcast_fusion.refs_0_
  11.3 0.0 copy-start.15
  11.3 31.1 %shard_map.172 = (f32[32,24,128]{2,1,0:T(8,128)}, bf16[64,768]{1,0:T(8,128)(2,1)}) custom-call(f32[24,128]{1,0:T(8,128)} %pad_bitcast_fusion.refs_0_, bf16[15664,768]{1,0:T(8,128)(2,1)} %refs_1_.1), custom_call_target="tpu_custom_call" | custom-call | tf_op jit(solution)/shard_map/pallas_call | solution.py:203
  42.5 0.0 all-gather.4.cloned.1.call-update
  42.5 0.0 all-gather.6.cloned.1.call-start
  42.6 0.1 reshape.283
  42.7 0.8 pad_maximum_fusion.1
  43.6 0.0 all-gather.6.cloned.1.call-update
  43.6 1.1 copy.29
  44.7 0.6 fusion.10
  46.0 0.1 slice.69
  46.0 0.1 slice.68
  46.1 0.1 clamp_bitcast_fusion
  46.2 0.1 reshape.314
  46.3 32.1 %gather_fusion.3 = bf16[5632,768]{1,0:T(8,128)(2,1)} fusion(bf16[15664,768]{1,0:T(8,128)(2,1)} %refs_1_.1, s32[6144]{0:T(1024)S(1)} %pad_clamp_fusion.3), kind=kCustom, calls=%fused_computation.3 | custom fusion | bytes 17324032 | tf_op jit(solution)/shard_map/jit(_take)/gather | solution.py:397
  78.4 91.1 %shard_map.173 = bf16[1792,768]{1,0:T(8,128)(2,1)S(1)} custom-call(bf16[32,176,768]{2,1,0:T(8,128)(2,1)} %bitcast.29), custom_call_target="tpu_custom_call" | custom-call | tf_op jit(solution)/shard_map/pallas_call | solution.py:331
  169.6 0.1 fusion.24
  169.7 0.1 stack_reshape.24
  169.8 0.1 stack_reshape.25
  169.9 0.1 stack_reshape.26
  170.0 0.1 stack_reshape.27
  170.1 0.1 stack_reshape.28
  170.2 0.1 stack_reshape.29
  170.3 0.1 stack_reshape.30
  170.3 0.1 stack_reshape.31
  170.4 0.7 broadcast_in_dim_reshape.7.b_in_ref
  171.1 0.7 broadcast_in_dim_reshape.6.b_qkv_ref
  171.8 0.6 broadcast_in_dim.89.type_ref
  172.4 0.6 stack.3.vec_ref
  173.1 0.2 conditional.1
  173.3 1.5 reshape.334.spot_ref
  174.8 0.6 reshape.332.spot_row_ref
  175.4 97.9 %all-gather.6.cloned.1.call-done = bf16[9216,768]{1,0:T(8,128)(2,1)} async-done(((bf16[288,768]{1,0:T(8,128)(2,1)}), bf16[9216,768]{1,0:T(8,128)(2,1)}) %all-gather.6.cloned.1.call-update) | async-done | bytes 14155792 | tf_op jit(solution)/shard_map/all_gather | solution.py:352
  273.4 72.8 %shard_map.174 = bf16[4,384,768]{2,1,0:T(8,128)(2,1)} custom-call(s32[4,384,1]{2,1,0:T(8,128)} %reshape.334.spot_ref, s32[4,1,384]{2,1,0:T(1,128)} %reshape.332.spot_row_ref, bf16[2048,768]{1,0:T(8,128)(2,1)} %all-gather.4.cloned.1.call-done.head_ref, bf16[1792,768]{1,0:T(8,128)(2,1)S(1)} %get-tuple-element.217.got_ref, bf16[512,768]{1,0:T(8,128)(2,1)} %pos_ref.1, ...), custom_call_target="tpu_custom_call" | custom-call | flops 40000000000 | bytes 30000000 | tf_op jit(solution)/shard_map/pallas_call | solution.py:102
  (33 shorter events, 0.2 us)
Async XLA Ops:
  6.5 166.5 %all-gather.4.cloned.1.call-start = ((), (), s32[]{:S(2)}) async-start(), calls=%async_computation.2 | async-start | bytes 3244032 | tf_op jit(solution)/shard_map/all_gather | solution.py:382
  7.3 3.2 copy-start.5
  7.3 3.2 copy-start.6
  7.3 3.2 copy-start.7
  7.3 3.2 copy-start.8
  7.3 3.2 copy-start.9
  7.3 3.2 copy-start.10
  7.3 3.2 copy-start.11
  7.4 3.2 copy-start.12
  7.4 3.2 copy-start.13
  7.4 3.2 copy-start.14
  11.3 31.2 %copy-start.3 = (bf16[12,64,24]{1,2,0:T(8,128)(2,1)S(1)}, bf16[12,64,24]{1,2,0:T(8,128)(2,1)}, u32[]{:S(2)}) copy-start(bf16[12,64,24]{1,2,0:T(8,128)(2,1)} %param.30) | copy-start | bytes 110596
  11.3 31.4 %copy-start = (bf16[96,768]{1,0:T(8,128)(2,1)S(1)}, bf16[96,768]{1,0:T(8,128)(2,1)}, u32[]{:S(2)}) copy-start(bf16[96,768]{1,0:T(8,128)(2,1)} %param.36) | copy-start | bytes 442372
  11.3 31.4 %copy-start.1 = (bf16[768,96]{0,1:T(8,128)(2,1)S(1)}, bf16[768,96]{0,1:T(8,128)(2,1)}, u32[]{:S(2)}) copy-start(bf16[768,96]{0,1:T(8,128)(2,1)} %param.34) | copy-start | bytes 442372
  11.3 31.4 %copy-start.2 = (bf16[768,72]{0,1:T(8,128)(2,1)S(1)}, bf16[768,72]{0,1:T(8,128)(2,1)}, u32[]{:S(2)}) copy-start(bf16[768,72]{0,1:T(8,128)(2,1)} %param.28) | copy-start | bytes 331780
  11.3 33.3 %copy-start.15 = (f32[32]{0:T(128)S(1)}, f32[32]{0:T(128)}, u32[]{:S(2)}) copy-start(f32[32]{0:T(128)} %constant.169.clone.1) | copy-start | bytes 388
  42.5 230.9 %all-gather.6.cloned.1.call-start = ((), (), s32[]{:S(2)}) async-start(), calls=%async_computation.3 | async-start | bytes 14598144 | tf_op jit(solution)/shard_map/all_gather | solution.py:352
  78.4 93.4 %copy-start.4 = (bf16[768]{0:T(1024)(128)(2,1)S(1)}, bf16[768]{0:T(1024)(128)(2,1)}, u32[]{:S(2)}) copy-start(bf16[768]{0:T(1024)(128)(2,1)} %param.25) | copy-start | bytes 4612
Sparse Core Ops, SparseCore 0:
  42.6 88.4 all-gather.3
  134.0 139.3 all-gather.5

commit v4 on v3

--- a/solution.py
+++ b/solution.py
@@ -6,7 +6,6 @@
 from jax.experimental import pallas as pl
 from jax.experimental.pallas import tpu as pltpu
 from jax.sharding import PartitionSpec as P
-
 
 PAD_ID = 1
 LN_EPS = 1e-5
@@ -115,7 +114,7 @@
 
 
 HEAD = 2048
-CAPS = ((0, 1, 176), (1, 2, 96), (2, 4, 72), (4, 8, 56), (8, 32, 48))
+CAPS = ((0, 1, 160), (1, 2, 80), (2, 4, 72), (4, 8, 48), (8, 32, 40))
 HOT = 2
 EXTRA = 48
 PLANE = 8
@@ -136,11 +135,9 @@
     pl.semaphore_wait(barrier, n - 1)
 
 
-def tell_kernel(n, part, msg_ref, table_ref, told_ref, piece_ref, relay_ref, send_sem, recv_sem, out_sem, in_sem, relay_sem,
-                own_sem):
+def tell_kernel(n, msg_ref, table_ref, told_ref, group_ref, send_sem, recv_sem, out_sem, in_sem, own_sem):
     me = lax.axis_index('fsdp')
-    planes = n // PLANE
-    group = part * planes
+    group = HEAD // PLANE
     meet(n, me)
 
     def note(k, dev, slot):
@@ -148,15 +145,11 @@
                                             device_id=(dev,), device_id_type=MESH)
 
     def lend(p):
-        return pltpu.make_async_remote_copy(table_ref.at[pl.ds(p * group, group)], relay_ref, out_sem.at[p], relay_sem,
+        return pltpu.make_async_remote_copy(table_ref.at[pl.ds(p * group, group)], group_ref, out_sem.at[p], in_sem,
                                             device_id=(p,), device_id_type=MESH)
 
-    def part_of(ref, z, dev):
-        return pltpu.make_async_remote_copy(ref.at[pl.ds(z * part, part)], piece_ref, out_sem.at[PLANE + z], in_sem,
-                                            device_id=(dev,), device_id_type=MESH)
-
     def own():
-        return pltpu.make_async_copy(table_ref.at[pl.ds(0, part)], piece_ref, own_sem)
+        return pltpu.make_async_copy(table_ref.at[pl.ds(0, group)], group_ref, own_sem)
 
     others(n, me, lambda k, dev: note(k, dev, me).start())
 
@@ -164,19 +157,9 @@
     def _():
         for p in range(PLANE - 1, 0, -1):
             lend(p).start()
-        for z in range(1, planes):
-            part_of(table_ref, z, z * PLANE).start()
         own().start()
 
     told_ref[me] = msg_ref[...]
-
-    @pl.when((me > 0) & (me < PLANE))
-    def _():
-        lend(0).wait_recv()
-        for z in range(planes - 1, 0, -1):
-            part_of(relay_ref, z, z * PLANE + me).start()
-        piece_ref[...] = relay_ref[0:part, :]
-
     others(n, me, lambda k, dev: note(k, dev, dev).wait_recv())
     others(n, me, lambda k, dev: note(k, dev, me).wait_send())
 
@@ -185,39 +168,22 @@
         own().wait()
         for p in range(1, PLANE):
             lend(p).wait_send()
-        for z in range(1, planes):
-            part_of(table_ref, z, z * PLANE).wait_send()
 
     @pl.when((me > 0) & (me < PLANE))
     def _():
-        for z in range(1, planes):
-            part_of(relay_ref, z, z * PLANE + me).wait_send()
-
-    @pl.when(me >= PLANE)
-    def _():
-        part_of(relay_ref, 0, me).wait_recv()
+        lend(0).wait_recv()
 
 
 def tell(n, msg, table):
-    part = HEAD // n
+    vmem = pl.BlockSpec(memory_space=pltpu.VMEM)
     return pl.pallas_call(
-        lambda *refs: tell_kernel(n, part, *refs),
+        lambda *refs: tell_kernel(n, *refs),
         out_shape=(jax.ShapeDtypeStruct((n,) + msg.shape, msg.dtype),
-                   jax.ShapeDtypeStruct((part, table.shape[1]), table.dtype)),
-        in_specs=[pl.BlockSpec(memory_space=pltpu.VMEM), pl.BlockSpec(memory_space=pl.ANY)],
-        out_specs=(pl.BlockSpec(memory_space=pltpu.VMEM), pl.BlockSpec(memory_space=pltpu.VMEM)),
-        scratch_shapes=[pltpu.VMEM((part * (n // PLANE), table.shape[1]), table.dtype),
-                        pltpu.SemaphoreType.DMA((n,)), pltpu.SemaphoreType.DMA((n,)),
-                        pltpu.SemaphoreType.DMA((PLANE + n // PLANE,)), pltpu.SemaphoreType.DMA, pltpu.SemaphoreType.DMA,
-                        pltpu.SemaphoreType.DMA],
+                   jax.ShapeDtypeStruct((HEAD // PLANE, table.shape[1]), table.dtype)),
+        in_specs=[vmem, pl.BlockSpec(memory_space=pl.ANY)], out_specs=(vmem, vmem),
+        scratch_shapes=[pltpu.SemaphoreType.DMA((n,)), pltpu.SemaphoreType.DMA((n,)), pltpu.SemaphoreType.DMA((PLANE,)),
+                        pltpu.SemaphoreType.DMA, pltpu.SemaphoreType.DMA],
         compiler_params=pltpu.CompilerParams(collective_id=0, has_side_effects=True))(msg, table)
-
-
-def head_spot(n, ids):
-    part = HEAD // n
-    planes = n // PLANE
-    at = ids // part
-    return ((at % planes) * PLANE + at // planes) * part + ids % part
 
 
 def bases():
@@ -232,9 +198,36 @@
     return z > 0 and 2 <= p and p < PLANE - 1 and (p, z) != (PLANE - 2, 3)
 
 
-def swap_kernel(n, send_ref, recv_ref, relay_ref, send_sem, recv_sem, lend_sem, pass_sem, own_sem):
+def swap_kernel(n, send_ref, group_ref, recv_ref, head_ref, relay_ref, send_sem, recv_sem, lend_sem, pass_sem, own_sem,
+                up_send, up_recv, flat_send, head_recv, core_send):
     me = lax.axis_index('fsdp')
     planes = n // PLANE
+    group = HEAD // PLANE
+    place = lax.rem(me, PLANE)
+    level = lax.div(me, PLANE)
+    base = level * PLANE
+    partner = base + place + 1 - 2 * lax.rem(place, 2)
+
+    def slot(p):
+        return head_ref.at[pl.ds(pl.multiple_of(p * group, 8), group)]
+
+    def pass_up(dev):
+        return pltpu.make_async_remote_copy(slot(place), slot(place), up_send, up_recv, device_id=(dev,), device_id_type=MESH)
+
+    def across(k):
+        p = lax.rem(place + 2 * k, PLANE)
+        return pltpu.make_async_remote_copy(slot(place), slot(place), flat_send.at[k], head_recv.at[place],
+                                            device_id=(base + p,), device_id_type=MESH)
+
+    def arrival(p):
+        return pltpu.make_async_remote_copy(slot(p), slot(p), core_send.at[0], head_recv.at[p], device_id=(me,),
+                                            device_id_type=MESH)
+
+    def share(k):
+        p = lax.rem(place + 2 * k, PLANE)
+        return pltpu.make_async_remote_copy(slot(p), slot(p), core_send.at[k], head_recv.at[p], device_id=(partner,),
+                                            device_id_type=MESH)
+
     meet(n, me)
     starts, _ = bases()
 
@@ -289,6 +282,24 @@
             else:
                 others(n, me, lambda k, dev: row(c, k, dev, me).start())
 
+    @pl.when(level == 0)
+    def _():
+        keep = pltpu.make_async_copy(group_ref, slot(place), up_recv)
+        keep.start()
+        keep.wait()
+
+    @pl.when(level > 0)
+    def _():
+        pass_up(me).wait_recv()
+
+    @pl.when(level < planes - 1)
+    def _():
+        pass_up(me + PLANE).start()
+
+    for k in range(1, PLANE // 2):
+        across(k).start()
+    share(0).start()
+
     for p, zs in relays():
         @pl.when(me == p)
         def _(zs=zs):
@@ -296,6 +307,10 @@
                 for c in range(HOT):
                     lend(c, 0, z).wait_recv()
                     hand_on(c, z).start()
+
+    for k in range(PLANE // 2 - 1, 0, -1):
+        arrival(lax.rem(place + 2 * k, PLANE)).wait_recv()
+        share(k).start()
 
     for c, (lo, hi, cap) in enumerate(CAPS):
         def one(dev, carry, c=c):
@@ -324,18 +339,32 @@
                 for c in range(HOT):
                     hand_on(c, z).wait_send()
 
-
-def swap(n, rows):
+    for k in range(PLANE // 2):
+        arrival(lax.rem(partner + 2 * k, PLANE)).wait_recv()
+    for k in range(1, PLANE // 2):
+        across(k).wait_send()
+    for k in range(PLANE // 2):
+        share(k).wait_send()
+
+    @pl.when(level < planes - 1)
+    def _():
+        pass_up(me + PLANE).wait_send()
+
+
+def swap(n, rows, group):
     planes = n // PLANE
     most = max(cap for _, _, cap in CAPS[:HOT])
+    vmem = pl.BlockSpec(memory_space=pltpu.VMEM)
+    dma = pltpu.SemaphoreType.DMA
     return pl.pallas_call(
         lambda *refs: swap_kernel(n, *refs),
-        out_shape=jax.ShapeDtypeStruct((bases()[1], rows.shape[2]), rows.dtype),
-        in_specs=[pl.BlockSpec(memory_space=pl.ANY)], out_specs=pl.BlockSpec(memory_space=pl.ANY),
-        scratch_shapes=[pltpu.VMEM((HOT, planes - 1, most, rows.shape[2]), rows.dtype), pltpu.SemaphoreType.DMA((n,)),
-                        pltpu.SemaphoreType.DMA((n,)), pltpu.SemaphoreType.DMA((HOT, planes - 1)),
-                        pltpu.SemaphoreType.DMA((HOT, planes - 1)), pltpu.SemaphoreType.DMA],
-        compiler_params=pltpu.CompilerParams(collective_id=1, has_side_effects=True))(rows)
+        out_shape=(jax.ShapeDtypeStruct((bases()[1], rows.shape[2]), rows.dtype),
+                   jax.ShapeDtypeStruct((HEAD, rows.shape[2]), rows.dtype)),
+        in_specs=[pl.BlockSpec(memory_space=pl.ANY), vmem], out_specs=(pl.BlockSpec(memory_space=pl.ANY), vmem),
+        scratch_shapes=[pltpu.VMEM((HOT, planes - 1, most, rows.shape[2]), rows.dtype), dma((n,)), dma((n,)),
+                        dma((HOT, planes - 1)), dma((HOT, planes - 1)), dma, dma, dma, dma((PLANE // 2,)), dma((PLANE,)),
+                        dma((PLANE // 2,))],
+        compiler_params=pltpu.CompilerParams(collective_id=1, has_side_effects=True))(rows, group)
 
 
 def solution(mesh):
@@ -377,9 +406,8 @@
         small = [emb_gain, emb_bias, ln1_gain, ln1_bias, ln2_gain, ln2_bias, b_out, b_ffn_out, b_qkv, b_ffn_in]
         message = jnp.concatenate([slotted, count] + small)
         message = jnp.pad(message, (0, -message.shape[0] % 1024))
-        told, piece = tell(n_dev, message.reshape(-1, 128), tok_shard)
+        told, group = tell(n_dev, message.reshape(-1, 128), tok_shard)
         told = told.reshape(n_dev, -1)
-        head = lax.all_gather(piece, 'fsdp', axis=0, tiled=True)
         at = wide + 128
         vectors = []
         for v in small:
@@ -395,8 +423,8 @@
         wanted = jnp.clip(wanted, 0, shard_rows - 1)
         wanted = wanted.reshape(n_dev // PLANE, PLANE, most).transpose(1, 0, 2)
         rows = jnp.take(tok_shard, wanted.reshape(-1), axis=0, mode='clip').reshape(n_dev, most, width)
-        got = swap(n_dev, rows)
-        spot = jnp.where(ids < HEAD, head_spot(n_dev, ids), HEAD + jnp.maximum(slot, 0))
+        got, head = swap(n_dev, rows, group)
+        spot = jnp.where(ids < HEAD, ids, HEAD + jnp.maximum(slot, 0))
 
         caps = jnp.concatenate([jnp.full((hi - lo,), c, jnp.float32) for lo, hi, c in CAPS])
         left = jnp.max(told[:, wide:wide + n_dev] - caps[None, :])

time: 353 us -> 326 us (0.924)
  the two profiles are of different devices: /device:TPU:0 before, /device:TPU:25 now
where the time goes in v4:
time: 326 us
  Pallas kernels  262 us (80%)
  local copies, waits for them, and re-layouts  43.7 us (13%)
  between operations  14.5 us (4%)
  other arithmetic  4.16 us (1%)
    pallas_call x1, Pallas kernels, swap(): pl.pallas_call(lambda *refs: swap_kernel(n, *refs), out_shape=(jax.ShapeD...  174 us
    pallas_call x1, Pallas kernels, layer(): pl.pallas_call(functools.partial(layer_kernel, (heads, size)), out_shape=...  71.4 us
    gather x1, local copies, waits for them, and re-layouts, local_step(): jnp.take(tok_shard, wanted.reshape(-1), axis=0, mode='clip')  34.5 us
    pallas_call x1, Pallas kernels, tell(): pl.pallas_call(lambda *refs: tell_kernel(n, *refs), out_shape=(jax.ShapeD...  16.4 us
  transfers between devices with their start and end apart: 1, of which 0 were waited for; matrix products, arithmetic and copies ran while one was open for 14% of the time, Pallas kernels for 59%

profile of v4, /device:TPU:25, one launch (start us, length us, event | category | flops | bytes accessed | tf_op | source)
XLA Modules:
  0.0 325.9 jit_solution(1208699014059643856)
XLA Ops:
  6.5 0.0 all-gather.3.cloned.1.call-start
  6.5 0.9 copy.24
  7.4 0.1 reshape.283
  7.6 1.8 pad_maximum_fusion.1
  9.4 0.0 all-gather.3.cloned.1.call-update
  9.4 0.7 reshape.276
  10.2 0.3 convert_reduce_fusion
  10.5 0.0 copy-start.2
  10.5 0.0 copy-start.3
  10.5 0.0 copy-start.4
  10.5 0.0 copy-start.5
  10.5 0.0 copy-start.6
  10.6 0.0 copy-start.7
  10.6 0.0 copy-start.8
  10.6 0.0 copy-start.9
  10.6 0.0 copy-start.10
  10.6 1.3 fusion.5
  11.9 1.3 select_reduce_fusion.1
  13.3 0.1 concatenate.9
  13.3 0.6 pad_bitcast_fusion.refs_0_
  13.9 16.4 %shard_map.172 = (f32[32,16,128]{2,1,0:T(8,128)}, bf16[256,768]{1,0:T(8,128)(2,1)}) custom-call(f32[16,128]{1,0:T(8,128)} %pad_bitcast_fusion.refs_0_, bf16[15664,768]{1,0:T(8,128)(2,1)} %refs_1_.1), custom_call_target="tpu_custom_call" | custom-call | tf_op jit(solution)/shard_map/pallas_call | solution.py:179
  30.4 1.0 copy.29
  31.4 0.0 copy-done.11
  31.4 0.6 fusion.10
  32.7 0.1 clamp_bitcast_fusion
  32.9 0.1 reshape.314
  33.0 34.5 %gather_fusion.3 = bf16[5120,768]{1,0:T(8,128)(2,1)} fusion(bf16[15664,768]{1,0:T(8,128)(2,1)} %refs_1_.1, s32[5120]{0:T(1024)S(1)} %broadcast_clamp_fusion), kind=kCustom, calls=%fused_computation.3 | custom fusion | bytes 15749120 | tf_op jit(solution)/shard_map/jit(_take)/gather | solution.py:425
  67.5 174.2 %shard_map.173 = (bf16[1536,768]{1,0:T(8,128)(2,1)}, bf16[2048,768]{1,0:T(8,128)(2,1)}) custom-call(bf16[32,160,768]{2,1,0:T(8,128)(2,1)} %bitcast.29, bf16[256,768]{1,0:T(8,128)(2,1)} %get-tuple-element.212.refs_1_), custom_call_target="tpu_custom_call" | custom-call | tf_op jit(solution)/shard_map/pallas_call | solution.py:359
  241.7 0.0 copy-start
  241.7 0.2 conditional.1
  242.0 1.5 reshape.334.spot_ref
  243.5 0.6 reshape.332.spot_row_ref
  244.1 0.1 slice.69
  244.1 0.1 slice.68
  244.2 0.1 fusion.14
  244.3 0.1 stack_reshape.24
  244.4 0.1 stack_reshape.25
  244.5 0.1 stack_reshape.26
  244.6 0.1 stack_reshape.27
  244.7 0.1 stack_reshape.28
  244.8 0.1 stack_reshape.29
  244.9 0.1 stack_reshape.30
  244.9 0.1 stack_reshape.31
  245.0 0.7 broadcast_in_dim_reshape.7.b_in_ref
  245.7 0.7 broadcast_in_dim_reshape.6.b_qkv_ref
  246.4 0.6 broadcast_in_dim.89.type_ref
  247.0 0.6 stack.3.vec_ref
  247.7 71.4 %shard_map.174 = bf16[4,384,768]{2,1,0:T(8,128)(2,1)} custom-call(s32[4,384,1]{2,1,0:T(8,128)} %reshape.334.spot_ref, s32[4,1,384]{2,1,0:T(1,128)} %reshape.332.spot_row_ref, bf16[2048,768]{1,0:T(8,128)(2,1)} %get-tuple-element.214.head_ref, bf16[1536,768]{1,0:T(8,128)(2,1)} %get-tuple-element.221.got_ref, bf16[512,768]{1,0:T(8,128)(2,1)} %pos_ref.1, ...), custom_call_target="tpu_custom_call" | custom-call | flops 40000000000 | bytes 30000000 | tf_op jit(solution)/shard_map/pallas_call | solution.py:101
  (22 shorter events, 0.1 us)
Async XLA Ops:
  6.5 241.1 %all-gather.3.cloned.1.call-start = ((), (), s32[]{:S(2)}) async-start(), calls=%async_computation.2 | async-start | bytes 14598144 | tf_op jit(solution)/shard_map/all_gather | solution.py:381
  10.5 2.7 copy-start.1
  10.5 2.7 copy-start.2
  10.5 2.7 copy-start.3
  10.5 2.7 copy-start.4
  10.5 2.7 copy-start.5
  10.5 2.7 copy-start.6
  10.6 2.7 copy-start.7
  10.6 2.7 copy-start.8
  10.6 2.7 copy-start.9
  10.6 2.7 copy-start.10
  13.9 17.5 %copy-start.11 = (f32[32]{0:T(128)S(1)}, f32[32]{0:T(128)}, u32[]{:S(2)}) copy-start(f32[32]{0:T(128)} %constant.130.clone.1) | copy-start | bytes 388
  241.7 4.7 %copy-start = (bf16[768]{0:T(1024)(128)(2,1)S(1)}, bf16[768]{0:T(1024)(128)(2,1)}, u32[]{:S(2)}) copy-start(bf16[768]{0:T(1024)(128)(2,1)} %param.25) | copy-start | bytes 4612
Sparse Core Ops, SparseCore 0:
  10.2 148.0 all-gather.2

commit v5 on v3

--- a/solution.py
+++ b/solution.py
@@ -30,12 +30,15 @@
     return lax.dot_general(a, b, (((1,), (1,)), ((), ())), preferred_element_type=jnp.float32)
 
 
-def layer_kernel(dims, spot_ref, spot_row_ref, head_ref, got_ref, pos_ref, type_ref, vec_ref, b_qkv_ref, b_in_ref,
-                 w_qkv_ref, w_out_ref, w_in_ref, w_back_ref, out_ref, qkv_ref, ctx_ref, x_ref):
+def flat(ref):
+    return ref.reshape(ref.shape[0] * ref.shape[1], ref.shape[2])
+
+
+def attention_kernel(dims, spot_ref, spot_row_ref, head_ref, got_ref, pos_ref, type_ref, vec_ref, b_qkv_ref, w_qkv_ref, w_out_ref,
+                     out_ref, qkv_ref, ctx_ref, x_ref):
     heads, size = dims
     seq, width = out_ref.shape[1:]
-    w_qkv_ref, w_out_ref, w_in_ref, w_back_ref = (
-        r.reshape(r.shape[0] * r.shape[1], width) for r in (w_qkv_ref, w_out_ref, w_in_ref, w_back_ref))
+    w_qkv_ref, w_out_ref = flat(w_qkv_ref), flat(w_out_ref)
     spot = spot_ref[0]
     total = jnp.zeros((seq, width), jnp.float32)
     step = 256
@@ -70,52 +73,69 @@
 
     a = (times_t(ctx_ref[...], w_out_ref[...]) + vec_ref[6:7, :]).astype(jnp.bfloat16)
     z = x_ref[...].astype(jnp.float32) + a.astype(jnp.float32)
-    x_ref[...] = norm(z, vec_ref[2:3, :], vec_ref[3:4, :]).astype(jnp.bfloat16)
-
-    total = jnp.zeros((seq, width), jnp.float32)
+    out_ref[0] = norm(z, vec_ref[2:3, :], vec_ref[3:4, :]).astype(jnp.bfloat16)
+
+
+def ffn_kernel(x_ref, vec_ref, b_in_ref, w_in_ref, w_back_ref, out_ref):
+    w_in_ref, w_back_ref = flat(w_in_ref), flat(w_back_ref)
+    x = x_ref[0]
+    total = jnp.zeros(x.shape, jnp.float32)
     for at in range(0, b_in_ref.shape[1], FFN_PART):
-        h = times_t(x_ref[...], w_in_ref[at:at + FFN_PART, :]) + b_in_ref[:, at:at + FFN_PART]
+        h = times_t(x, w_in_ref[at:at + FFN_PART, :]) + b_in_ref[:, at:at + FFN_PART]
         h = (0.5 * h * (1.0 + lax.erf(h * SQRT_HALF))).astype(jnp.bfloat16)
         total += times(h, w_back_ref[at:at + FFN_PART, :])
-    z = x_ref[...].astype(jnp.float32) + (total + vec_ref[7:8, :])
+    z = x.astype(jnp.float32) + (total + vec_ref[7:8, :])
     out_ref[0] = norm(z, vec_ref[4:5, :], vec_ref[5:6, :]).astype(jnp.bfloat16)
 
 
-def layer(heads, size, batch, spot, head, got, pos_table, type_row, vecs, b_qkv, b_in, weights, sizes):
+def whole(*shape):
+    return pl.BlockSpec(shape, lambda b: (0,) * len(shape), pipeline_mode=pl.Buffered(1))
+
+
+def each(*shape):
+    return pl.BlockSpec((1,) + shape, lambda b: (b,) + (0,) * len(shape))
+
+
+def pieces(weights, sizes):
+    out, at = [], 0
+    for rows in sizes:
+        out.append(pl.BlockSpec((weights.shape[0], rows, weights.shape[2]),
+                                functools.partial(lambda i, b: (0, i, 0), at // rows), pipeline_mode=pl.Buffered(1)))
+        at += rows
+    return out
+
+
+def attend(heads, size, batch, spot, head, got, pos_table, type_row, vecs, b_qkv, weights, sizes):
     seq = spot.shape[0] // batch
     width = head.shape[1]
-    ffn = b_in.shape[0]
-    n_dev = weights.shape[0]
-
-    def whole(*shape):
-        return pl.BlockSpec(shape, lambda b: (0,) * len(shape), pipeline_mode=pl.Buffered(1))
-
-    def each(*shape):
-        return pl.BlockSpec((1,) + shape, lambda b: (b,) + (0,) * len(shape))
-
-    pieces, at = [], 0
-    for rows in sizes:
-        pieces.append(pl.BlockSpec((n_dev, rows, width), functools.partial(lambda i, b: (0, i, 0), at // rows),
-                                   pipeline_mode=pl.Buffered(1)))
-        at += rows
-
+    block = pltpu.VMEM((seq, width), jnp.bfloat16)
     return pl.pallas_call(
-        functools.partial(layer_kernel, (heads, size)),
+        functools.partial(attention_kernel, (heads, size)),
         out_shape=jax.ShapeDtypeStruct((batch, seq, width), jnp.bfloat16),
         grid=(batch,),
-        in_specs=[each(seq, 1), each(1, seq), whole(*head.shape), whole(*got.shape), whole(*pos_table.shape),
-                  whole(1, width), whole(8, width), whole(1, 3 * width), whole(1, ffn)] + pieces,
+        in_specs=[each(seq, 1), each(1, seq), whole(*head.shape), whole(*got.shape), whole(*pos_table.shape), whole(1, width),
+                  whole(8, width), whole(1, 3 * width)] + pieces(weights, sizes),
         out_specs=each(seq, width),
-        scratch_shapes=[pltpu.VMEM((seq, 3 * width), jnp.bfloat16), pltpu.VMEM((seq, width), jnp.bfloat16),
-                        pltpu.VMEM((seq, width), jnp.bfloat16)],
+        scratch_shapes=[pltpu.VMEM((seq, 3 * width), jnp.bfloat16), block, block],
         compiler_params=pltpu.CompilerParams(vmem_limit_bytes=60 << 20),
-        cost_estimate=pl.CostEstimate(flops=40 * 10 ** 9, bytes_accessed=30 * 10 ** 6, transcendentals=10 ** 7))(
+        cost_estimate=pl.CostEstimate(flops=20 * 10 ** 9, bytes_accessed=15 * 10 ** 6, transcendentals=7 * 10 ** 6))(
             spot.reshape(batch, seq, 1), spot.reshape(batch, 1, seq), head, got, pos_table, type_row[None, :], vecs,
-            b_qkv[None, :], b_in[None, :], *([weights] * len(sizes)))
+            b_qkv[None, :], *([weights] * len(sizes)))
+
+
+def feed(x, vecs, b_in, weights, sizes):
+    batch, seq, width = x.shape
+    return pl.pallas_call(
+        ffn_kernel, out_shape=jax.ShapeDtypeStruct(x.shape, jnp.bfloat16), grid=(batch,),
+        in_specs=[each(seq, width), whole(8, width), whole(1, b_in.shape[0])] + pieces(weights, sizes),
+        out_specs=each(seq, width),
+        compiler_params=pltpu.CompilerParams(vmem_limit_bytes=60 << 20),
+        cost_estimate=pl.CostEstimate(flops=15 * 10 ** 9, bytes_accessed=15 * 10 ** 6, transcendentals=5 * 10 ** 6))(
+            x, vecs, b_in[None, :], *([weights] * len(sizes)))
 
 
 HEAD = 2048
-CAPS = ((0, 1, 176), (1, 2, 96), (2, 4, 72), (4, 8, 56), (8, 32, 48))
+CAPS = ((0, 1, 160), (1, 2, 80), (2, 4, 72), (4, 8, 48), (8, 32, 40))
 HOT = 2
 EXTRA = 48
 PLANE = 8
@@ -347,9 +367,10 @@
         n_tok = batch_dev * seq_len
         shard_rows, width = tok_shard.shape
         num_heads, head_dim = w_out.shape[0], w_out.shape[1]
-        pieces = [w_qkv.T, w_out.reshape(num_heads * head_dim, -1).T, w_ffn_in.T, w_ffn_out]
-        sizes = [p.shape[0] for p in pieces]
-        weights = lax.all_gather(jnp.concatenate(pieces, axis=0), 'fsdp', axis=0, tiled=False)
+        first = [w_qkv.T, w_out.reshape(num_heads * head_dim, -1).T]
+        second = [w_ffn_in.T, w_ffn_out]
+        weights_a = lax.all_gather(jnp.concatenate(first, axis=0), 'fsdp', axis=0, tiled=False)
+        weights_b = lax.all_gather(jnp.concatenate(second, axis=0), 'fsdp', axis=0, tiled=False)
 
         ids = token_ids.reshape(n_tok)
         keep = ids != PAD_ID
@@ -422,8 +443,9 @@
 
         got, spot = lax.cond(rounds > 0, slow, lambda g, p: (g, p), got, spot)
         vecs = jnp.stack([emb_g, emb_b, ln1_g, ln1_b, ln2_g, ln2_b, b_out_f, b_back_f])
-        return layer(num_heads, head_dim, batch_dev, spot, head, got, pos_table, type_row, vecs, b_qkv_f, b_in_f,
-                     weights, sizes)
+        x = attend(num_heads, head_dim, batch_dev, spot, head, got, pos_table, type_row, vecs, b_qkv_f, weights_a,
+                   [w.shape[0] for w in first])
+        return feed(x, vecs, b_in_f, weights_b, [w.shape[0] for w in second])
 
     vec_spec = P('fsdp')
     in_specs = (P('fsdp', None), P('fsdp', None), P(None, None), P(None), vec_spec, vec_spec,

time: 353 us -> 338 us (0.958)
  Pallas kernels: 195 us -> 184 us
  waiting for transfers between devices: 98 us -> 91.5 us
    pallas_call x1, Pallas kernels: 91.1 us -> 78.5 us  [swap(): pl.pallas_call(lambda *refs: swap_kernel(n, *refs), out_shape=jax.ShapeDt...]
    all_gather x1 -> x2, waiting for transfers between devices: 97.9 us -> 91.4 us  [the longest x1 60.7 us: local_step(): lax.all_gather(jnp.concatenate(first, axis=0), 'fsdp', axis=0, tiled=False)]
    pallas_call x1 -> x2, Pallas kernels: 72.8 us -> 75.4 us  [the longest x1 52.1 us: attend(): pl.pallas_call(functools.partial(attention_kernel, (heads, size)), out_sh...]
  transfers between devices with their start and end apart: 2 -> 3, of which waited for: 1 -> 2; matrix products, arithmetic and copies ran while one was open for 12% -> 13% of each run, Pallas kernels for 26% -> 39%
where the time goes in v5:
time: 338 us
  Pallas kernels  184 us (54%)
  waiting for transfers between devices  91.5 us (27%)
  local copies, waits for them, and re-layouts  43.1 us (13%)
  between operations  14.2 us (4%)
  other arithmetic  3.72 us (1%)
    pallas_call x1, Pallas kernels, swap(): pl.pallas_call(lambda *refs: swap_kernel(n, *refs), out_shape=jax.ShapeDt...  78.5 us
    all_gather x1, waiting for transfers between devices, local_step(): lax.all_gather(jnp.concatenate(first, axis=0), 'fsdp', axis=0, tiled=False)  60.7 us
    pallas_call x1, Pallas kernels, attend(): pl.pallas_call(functools.partial(attention_kernel, (heads, size)), out_sh...  52.1 us
    gather x1, local copies, waits for them, and re-layouts, local_step(): jnp.take(tok_shard, wanted.reshape(-1), axis=0, mode='clip')  34.6 us
    all_gather x1, waiting for transfers between devices, local_step(): lax.all_gather(jnp.concatenate(second, axis=0), 'fsdp', axis=0, tiled=False)  30.7 us
    pallas_call x1, Pallas kernels, tell(): pl.pallas_call(lambda *refs: tell_kernel(n, part, *refs), out_shape=(jax....  29.6 us
    pallas_call x1, Pallas kernels, feed(): pl.pallas_call(ffn_kernel, out_shape=jax.ShapeDtypeStruct(x.shape, jnp.bf...  23.3 us
  transfers between devices with their start and end apart: 3, of which 2 were waited for; matrix products, arithmetic and copies ran while one was open for 13% of the time, Pallas kernels for 39%

profile of v5, /device:TPU:0, one launch (start us, length us, event | category | flops | bytes accessed | tf_op | source)
XLA Modules:
  0.0 337.5 jit_solution(8074541256907906373)
XLA Ops:
  6.5 0.7 reshape.276
  7.3 0.0 copy-start.6
  7.3 0.0 copy-start.7
  7.3 0.0 copy-start.10
  7.3 0.0 copy-start.11
  7.4 1.3 fusion.5
  8.7 0.3 convert_reduce_fusion
  9.0 1.3 select_reduce_fusion.1
  10.4 0.1 concatenate.12
  10.5 0.6 pad_bitcast_fusion.refs_0_
  11.1 0.0 copy-start.15
  11.1 29.6 %shard_map.172 = (f32[32,16,128]{2,1,0:T(8,128)}, bf16[64,768]{1,0:T(8,128)(2,1)}) custom-call(f32[16,128]{1,0:T(8,128)} %pad_bitcast_fusion.refs_0_, bf16[15664,768]{1,0:T(8,128)(2,1)} %refs_1_.1), custom_call_target="tpu_custom_call" | custom-call | tf_op jit(solution)/shard_map/pallas_call | solution.py:223
  40.7 0.0 all-gather.6.cloned.1.call-update
  40.7 0.0 all-gather.8.cloned.1.call-start
  40.8 0.1 reshape.283
  40.9 0.7 pad_maximum_fusion.2
  41.6 0.0 all-gather.8.cloned.1.call-update
  41.6 0.0 all-gather.10.cloned.1.call-start
  41.7 0.7 pad_maximum_fusion.1
  42.4 0.0 all-gather.10.cloned.1.call-update
  42.5 1.0 copy.28
  43.5 0.6 fusion.10
  44.8 0.1 slice.68
  44.9 0.1 slice.69
  44.9 0.1 clamp_bitcast_fusion
  45.0 0.1 reshape.314
  45.2 34.6 %gather_fusion.3 = bf16[5120,768]{1,0:T(8,128)(2,1)} fusion(bf16[15664,768]{1,0:T(8,128)(2,1)} %refs_1_.1, s32[5120]{0:T(1024)S(1)} %broadcast_clamp_fusion), kind=kCustom, calls=%fused_computation.3 | custom fusion | bytes 15749120 | tf_op jit(solution)/shard_map/jit(_take)/gather | solution.py:418
  79.8 78.5 %shard_map.173 = bf16[1536,768]{1,0:T(8,128)(2,1)} custom-call(bf16[32,160,768]{2,1,0:T(8,128)(2,1)} %bitcast.30), custom_call_target="tpu_custom_call" | custom-call | tf_op jit(solution)/shard_map/pallas_call | solution.py:351
  158.3 0.1 fusion.24
  158.4 0.1 stack_reshape.24
  158.5 0.1 stack_reshape.25
  158.6 0.1 stack_reshape.26
  158.7 0.1 stack_reshape.27
  158.8 0.1 stack_reshape.28
  158.9 0.1 stack_reshape.29
  159.0 0.1 stack_reshape.30
  159.1 0.1 stack_reshape.31
  159.2 0.7 broadcast_in_dim_reshape.6.b_qkv_ref
  159.9 0.6 broadcast_in_dim.89.type_ref
  160.5 0.7 broadcast_in_dim_reshape.7.b_in_ref
  161.2 0.7 stack.3.vec_ref
  161.8 0.2 conditional.1
  162.1 1.5 reshape.335.spot_ref
  163.6 0.6 reshape.333.spot_row_ref
  164.2 60.7 %all-gather.8.cloned.1.call-done = bf16[3072,768]{1,0:T(8,128)(2,1)} async-done(((bf16[96,768]{1,0:T(8,128)(2,1)}), bf16[3072,768]{1,0:T(8,128)(2,1)}) %all-gather.8.cloned.1.call-update) | async-done | bytes 4718608 | tf_op jit(solution)/shard_map/all_gather | solution.py:372
  224.9 52.1 %shard_map.174.x_ref = bf16[4,384,768]{2,1,0:T(8,128)(2,1)} custom-call(s32[4,384,1]{2,1,0:T(8,128)} %reshape.335.spot_ref, s32[4,1,384]{2,1,0:T(1,128)} %reshape.333.spot_row_ref, bf16[2048,768]{1,0:T(8,128)(2,1)} %all-gather.6.cloned.1.call-done.head_ref, bf16[1536,768]{1,0:T(8,128)(2,1)} %get-tuple-element.217.got_ref, bf16[512,768]{1,0:T(8,128)(2,1)} %pos_ref.1, ...), custom_call_target="tpu_custom_call" | custom-call | flops 20000000000 | bytes 15000000 | tf_op jit(solution)/shard_map/pallas_call | solution.py:112
  277.0 30.7 %all-gather.10.cloned.1.call-done = bf16[6144,768]{1,0:T(8,128)(2,1)} async-done(((bf16[192,768]{1,0:T(8,128)(2,1)}), bf16[6144,768]{1,0:T(8,128)(2,1)}) %all-gather.10.cloned.1.call-update) | async-done | bytes 9437200 | tf_op jit(solution)/shard_map/all_gather | solution.py:373
  307.7 23.3 %shard_map.175 = bf16[4,384,768]{2,1,0:T(8,128)(2,1)} custom-call(bf16[4,384,768]{2,1,0:T(8,128)(2,1)} %shard_map.174.x_ref, f32[8,768]{1,0:T(8,128)} %stack.3.vec_ref, f32[1,3072]{1,0:T(1,128)} %broadcast_in_dim_reshape.7.b_in_ref, bf16[32,192,768]{2,1,0:T(8,128)(2,1)} %bitcast.42, bf16[32,192,768]{2,1,0:T(8,128)(2,1)} %bitcast.43), custom_call_target="tpu_custom_call" | custom-call | flops 15000000512 | bytes 15000000 | tf_op jit(solution)/shard_map/pallas_call | solution.py:128
  (38 shorter events, 0.2 us)
Async XLA Ops:
  6.5 155.3 %all-gather.6.cloned.1.call-start = ((), (), s32[]{:S(2)}) async-start(), calls=%async_computation.2 | async-start | bytes 3244032 | tf_op jit(solution)/shard_map/all_gather | solution.py:403
  7.3 3.0 copy-start.5
  7.3 3.0 copy-start.6
  7.3 3.0 copy-start.7
  7.3 3.0 copy-start.8
  7.3 3.0 copy-start.9
  7.3 3.0 copy-start.10
  7.3 3.0 copy-start.11
  7.4 3.0 copy-start.12
  7.4 3.0 copy-start.13
  7.4 3.0 copy-start.14
  11.1 29.7 %copy-start.3 = (bf16[12,64,24]{1,2,0:T(8,128)(2,1)S(1)}, bf16[12,64,24]{1,2,0:T(8,128)(2,1)}, u32[]{:S(2)}) copy-start(bf16[12,64,24]{1,2,0:T(8,128)(2,1)} %param.30) | copy-start | bytes 110596
  11.1 29.9 %copy-start.2 = (bf16[768,72]{0,1:T(8,128)(2,1)S(1)}, bf16[768,72]{0,1:T(8,128)(2,1)}, u32[]{:S(2)}) copy-start(bf16[768,72]{0,1:T(8,128)(2,1)} %param.28) | copy-start | bytes 331780
  11.1 30.6 %copy-start = (bf16[96,768]{1,0:T(8,128)(2,1)S(1)}, bf16[96,768]{1,0:T(8,128)(2,1)}, u32[]{:S(2)}) copy-start(bf16[96,768]{1,0:T(8,128)(2,1)} %param.36) | copy-start | bytes 442372
  11.1 30.6 %copy-start.1 = (bf16[768,96]{0,1:T(8,128)(2,1)S(1)}, bf16[768,96]{0,1:T(8,128)(2,1)}, u32[]{:S(2)}) copy-start(bf16[768,96]{0,1:T(8,128)(2,1)} %param.34) | copy-start | bytes 442372
  11.1 32.4 %copy-start.15 = (f32[32]{0:T(128)S(1)}, f32[32]{0:T(128)}, u32[]{:S(2)}) copy-start(f32[32]{0:T(128)} %constant.167.clone.1) | copy-start | bytes 388
  40.7 184.2 %all-gather.8.cloned.1.call-start = ((), (), s32[]{:S(2)}) async-start(), calls=%async_computation.3 | async-start | bytes 4866048 | tf_op jit(solution)/shard_map/all_gather | solution.py:372
  41.6 266.1 %all-gather.10.cloned.1.call-start = ((), (), s32[]{:S(2)}) async-start(), calls=%async_computation.4 | async-start | bytes 9732096 | tf_op jit(solution)/shard_map/all_gather | solution.py:373
  79.8 80.1 %copy-start.4 = (bf16[768]{0:T(1024)(128)(2,1)S(1)}, bf16[768]{0:T(1024)(128)(2,1)}, u32[]{:S(2)}) copy-start(bf16[768]{0:T(1024)(128)(2,1)} %param.25) | copy-start | bytes 4612
Sparse Core Ops, SparseCore 0:
  40.8 84.8 all-gather.5
  128.7 96.1 all-gather.7
  227.8 79.8 all-gather.9

commit v6 on v5

--- a/solution.py
+++ b/solution.py
@@ -34,12 +34,12 @@
     return ref.reshape(ref.shape[0] * ref.shape[1], ref.shape[2])
 
 
-def attention_kernel(dims, spot_ref, spot_row_ref, head_ref, got_ref, pos_ref, type_ref, vec_ref, b_qkv_ref, w_qkv_ref, w_out_ref,
-                     out_ref, qkv_ref, ctx_ref, x_ref):
+def attention_kernel(dims, spot_row_ref, got_ref, pos_ref, type_ref, vec_ref, b_qkv_ref, head_ref, w_qkv_ref, w_out_ref, out_ref,
+                     qkv_ref, ctx_ref, x_ref):
     heads, size = dims
     seq, width = out_ref.shape[1:]
-    w_qkv_ref, w_out_ref = flat(w_qkv_ref), flat(w_out_ref)
-    spot = spot_ref[0]
+    head_ref, w_qkv_ref, w_out_ref = flat(head_ref), flat(w_qkv_ref), flat(w_out_ref)
+    spot = jnp.transpose(jnp.broadcast_to(spot_row_ref[0].astype(jnp.float32), (8, seq)))[:, 0:1].astype(jnp.int32)
     total = jnp.zeros((seq, width), jnp.float32)
     step = 256
     for ref, first in ((head_ref, 0), (got_ref, head_ref.shape[0])):
@@ -99,27 +99,27 @@
 def pieces(weights, sizes):
     out, at = [], 0
     for rows in sizes:
-        out.append(pl.BlockSpec((weights.shape[0], rows, weights.shape[2]),
-                                functools.partial(lambda i, b: (0, i, 0), at // rows), pipeline_mode=pl.Buffered(1)))
+        out.append(pl.BlockSpec((pl.Element(weights.shape[0]), pl.Element(rows), pl.Element(weights.shape[2])),
+                                functools.partial(lambda i, b: (0, i, 0), at), pipeline_mode=pl.Buffered(1)))
         at += rows
     return out
 
 
-def attend(heads, size, batch, spot, head, got, pos_table, type_row, vecs, b_qkv, weights, sizes):
+def attend(heads, size, batch, spot, got, pos_table, type_row, vecs, b_qkv, weights, sizes):
     seq = spot.shape[0] // batch
-    width = head.shape[1]
+    width = got.shape[1]
     block = pltpu.VMEM((seq, width), jnp.bfloat16)
     return pl.pallas_call(
         functools.partial(attention_kernel, (heads, size)),
         out_shape=jax.ShapeDtypeStruct((batch, seq, width), jnp.bfloat16),
         grid=(batch,),
-        in_specs=[each(seq, 1), each(1, seq), whole(*head.shape), whole(*got.shape), whole(*pos_table.shape), whole(1, width),
+        in_specs=[each(1, seq), whole(*got.shape), whole(*pos_table.shape), whole(1, width),
                   whole(8, width), whole(1, 3 * width)] + pieces(weights, sizes),
         out_specs=each(seq, width),
         scratch_shapes=[pltpu.VMEM((seq, 3 * width), jnp.bfloat16), block, block],
         compiler_params=pltpu.CompilerParams(vmem_limit_bytes=60 << 20),
         cost_estimate=pl.CostEstimate(flops=20 * 10 ** 9, bytes_accessed=15 * 10 ** 6, transcendentals=7 * 10 ** 6))(
-            spot.reshape(batch, seq, 1), spot.reshape(batch, 1, seq), head, got, pos_table, type_row[None, :], vecs,
+            spot.reshape(batch, 1, seq), got, pos_table, type_row[None, :], vecs,
             b_qkv[None, :], *([weights] * len(sizes)))
 
 
@@ -135,7 +135,7 @@
 
 
 HEAD = 2048
-CAPS = ((0, 1, 160), (1, 2, 80), (2, 4, 72), (4, 8, 48), (8, 32, 40))
+CAPS = ((0, 1, 168), (1, 2, 88), (2, 4, 64), (4, 8, 48), (8, 32, 40))
 HOT = 2
 EXTRA = 48
 PLANE = 8
@@ -367,11 +367,6 @@
         n_tok = batch_dev * seq_len
         shard_rows, width = tok_shard.shape
         num_heads, head_dim = w_out.shape[0], w_out.shape[1]
-        first = [w_qkv.T, w_out.reshape(num_heads * head_dim, -1).T]
-        second = [w_ffn_in.T, w_ffn_out]
-        weights_a = lax.all_gather(jnp.concatenate(first, axis=0), 'fsdp', axis=0, tiled=False)
-        weights_b = lax.all_gather(jnp.concatenate(second, axis=0), 'fsdp', axis=0, tiled=False)
-
         ids = token_ids.reshape(n_tok)
         keep = ids != PAD_ID
         asks = keep & (ids >= HEAD)
@@ -400,7 +395,11 @@
         message = jnp.pad(message, (0, -message.shape[0] % 1024))
         told, piece = tell(n_dev, message.reshape(-1, 128), tok_shard)
         told = told.reshape(n_dev, -1)
-        head = lax.all_gather(piece, 'fsdp', axis=0, tiled=True)
+        first = [piece, w_qkv.T, w_out.reshape(num_heads * head_dim, -1).T]
+        second = [w_ffn_in.T, w_ffn_out]
+        weights_a = lax.all_gather(jnp.concatenate(first, axis=0), 'fsdp', axis=0, tiled=False)
+        weights_b = lax.all_gather(jnp.concatenate(second, axis=0), 'fsdp', axis=0, tiled=False)
+
         at = wide + 128
         vectors = []
         for v in small:
@@ -437,13 +436,14 @@
             return r + 1, jnp.where(live[:, None], new, rows_now)
 
         def slow(got_now, spot_now):
+            head = weights_a[:, :piece.shape[0]].reshape(HEAD, width)
             rows_now = jnp.take(jnp.concatenate([head, got_now], axis=0), spot_now, axis=0, mode='clip')
             _, rows_now = lax.while_loop(lambda state: state[0] < rounds, again, (jnp.int32(0), rows_now))
             return jnp.pad(rows_now, ((0, slots - n_tok), (0, 0))), jnp.where(ids == PAD_ID, spot_now, HEAD + place)
 
         got, spot = lax.cond(rounds > 0, slow, lambda g, p: (g, p), got, spot)
         vecs = jnp.stack([emb_g, emb_b, ln1_g, ln1_b, ln2_g, ln2_b, b_out_f, b_back_f])
-        x = attend(num_heads, head_dim, batch_dev, spot, head, got, pos_table, type_row, vecs, b_qkv_f, weights_a,
+        x = attend(num_heads, head_dim, batch_dev, spot, got, pos_table, type_row, vecs, b_qkv_f, weights_a,
                    [w.shape[0] for w in first])
         return feed(x, vecs, b_in_f, weights_b, [w.shape[0] for w in second])
 

time: 338 us -> 296 us (0.88)
  waiting for transfers between devices: 91.5 us -> 38.2 us
  Pallas kernels: 184 us -> 199 us
  local copies, waits for them, and re-layouts: 43.1 us -> 38.1 us
    all_gather x1, waiting for transfers between devices: 60.7 us -> 0.01 us  [local_step(): lax.all_gather(jnp.concatenate(first, axis=0), 'fsdp', axis=0, tiled=False)]
    pallas_call x1, Pallas kernels: 78.5 us -> 92.4 us  [swap(): pl.pallas_call(lambda *refs: swap_kernel(n, *refs), out_shape=jax.ShapeDt...]
    all_gather x1, waiting for transfers between devices: 30.7 us -> 38.2 us  [local_step(): lax.all_gather(jnp.concatenate(second, axis=0), 'fsdp', axis=0, tiled=False)]
    gather x1, local copies, waits for them, and re-layouts: 34.6 us -> 31.2 us  [local_step(): jnp.take(tok_shard, wanted.reshape(-1), axis=0, mode='clip')]
  transfers between devices with their start and end apart: 3 -> 2, of which waited for: 2 -> 1; matrix products, arithmetic and copies ran while one was open for 13% -> 13% of each run, Pallas kernels for 39% -> 49%
where the time goes in v6:
time: 296 us; the launch traced here: 295 us
  Pallas kernels  199 us (67%)
  waiting for transfers between devices  38.2 us (13%)
  local copies, waits for them, and re-layouts  38.1 us (13%)
  between operations  14.3 us (5%)
  other arithmetic  4.65 us (2%)
    pallas_call x1, Pallas kernels, swap(): pl.pallas_call(lambda *refs: swap_kernel(n, *refs), out_shape=jax.ShapeDt...  92.4 us
    pallas_call x1, Pallas kernels, attend(): pl.pallas_call(functools.partial(attention_kernel, (heads, size)), out_sh...  53.3 us
    all_gather x1, waiting for transfers between devices, local_step(): lax.all_gather(jnp.concatenate(second, axis=0), 'fsdp', axis=0, tiled=False)  38.2 us
    gather x1, local copies, waits for them, and re-layouts, local_step(): jnp.take(tok_shard, wanted.reshape(-1), axis=0, mode='clip')  31.2 us
    pallas_call x1, Pallas kernels, tell(): pl.pallas_call(lambda *refs: tell_kernel(n, part, *refs), out_shape=(jax....  29.6 us
    pallas_call x1, Pallas kernels, feed(): pl.pallas_call(ffn_kernel, out_shape=jax.ShapeDtypeStruct(x.shape, jnp.bf...  23.3 us
  transfers between devices with their start and end apart: 2, of which 1 were waited for; matrix products, arithmetic and copies ran while one was open for 13% of the time, Pallas kernels for 49%

profile of v6, /device:TPU:0, one launch (start us, length us, event | category | flops | bytes accessed | tf_op | source)
XLA Modules:
  0.0 295.5 jit_solution(8264269548551099187)
XLA Ops:
  6.5 0.7 reshape.276
  7.3 0.0 copy-start.6
  7.3 0.0 copy-start.7
  7.3 0.0 copy-start.10
  7.3 0.0 copy-start.11
  7.4 0.0 copy-start.14
  7.4 0.0 copy-start.3
  7.4 1.3 fusion.5
  8.7 0.3 convert_reduce_fusion
  9.0 1.3 select_reduce_fusion.1
  10.4 0.1 concatenate.12
  10.5 0.6 pad_bitcast_fusion.refs_0_
  11.1 0.1 reshape.281
  11.2 0.0 copy-start
  11.2 0.0 copy-start.1
  11.2 0.0 copy-start.15
  11.3 29.6 %shard_map.172 = (f32[32,16,128]{2,1,0:T(8,128)}, bf16[64,768]{1,0:T(8,128)(2,1)}) custom-call(f32[16,128]{1,0:T(8,128)} %pad_bitcast_fusion.refs_0_, bf16[15664,768]{1,0:T(8,128)(2,1)} %refs_1_.1), custom_call_target="tpu_custom_call" | custom-call | tf_op jit(solution)/shard_map/pallas_call | solution.py:223
  40.9 1.6 pad_maximum_fusion.2
  42.5 0.0 all-gather.5.cloned.1.call-update
  42.5 0.0 all-gather.7.cloned.1.call-start
  42.6 0.7 pad_maximum_fusion.1
  43.3 0.0 all-gather.7.cloned.1.call-update
  43.3 1.0 copy.26
  44.4 0.6 fusion.10
  45.6 0.1 slice.71
  45.6 0.1 slice.72
  45.7 0.1 clamp_bitcast_fusion
  45.8 0.1 reshape.311
  46.0 31.2 %gather_fusion.3 = bf16[5376,768]{1,0:T(8,128)(2,1)} fusion(bf16[15664,768]{1,0:T(8,128)(2,1)} %refs_1_.1, s32[6144]{0:T(1024)S(1)} %pad_clamp_fusion.3), kind=kCustom, calls=%fused_computation.3 | custom fusion | bytes 16536576 | tf_op jit(solution)/shard_map/jit(_take)/gather | solution.py:417
  77.1 92.4 %shard_map.173 = bf16[1536,768]{1,0:T(8,128)(2,1)} custom-call(bf16[32,168,768]{2,1,0:T(8,128)(2,1)} %bitcast.31), custom_call_target="tpu_custom_call" | custom-call | tf_op jit(solution)/shard_map/pallas_call | solution.py:351
  169.6 0.6 broadcast_in_dim.89.type_ref
  170.1 0.1 fusion.24
  170.2 0.1 stack_reshape.24
  170.3 0.1 stack_reshape.25
  170.4 0.1 stack_reshape.26
  170.5 0.1 stack_reshape.27
  170.6 0.1 stack_reshape.28
  170.7 0.1 stack_reshape.29
  170.8 0.1 stack_reshape.30
  170.9 0.1 stack_reshape.31
  171.0 0.7 broadcast_in_dim_reshape.6.b_qkv_ref
  171.7 0.7 broadcast_in_dim_reshape.7.b_in_ref
  172.4 0.6 stack.3.vec_ref
  173.0 0.2 conditional.1
  173.3 0.6 reshape.330.spot_row_ref
  173.9 53.3 %shard_map.174.x_ref = bf16[4,384,768]{2,1,0:T(8,128)(2,1)} custom-call(s32[4,1,384]{2,1,0:T(1,128)} %reshape.330.spot_row_ref, bf16[1536,768]{1,0:T(8,128)(2,1)} %get-tuple-element.214.got_ref, bf16[512,768]{1,0:T(8,128)(2,1)} %pos_ref.1, bf16[1,768]{1,0:T(2,128)(2,1)} %broadcast_in_dim.89.type_ref, f32[8,768]{1,0:T(8,128)} %stack.3.vec_ref, ...), custom_call_target="tpu_custom_call" | custom-call | flops 20000000000 | bytes 15000000 | tf_op jit(solution)/shard_map/pallas_call | solution.py:112
  227.1 38.2 %all-gather.7.cloned.1.call-done = bf16[6144,768]{1,0:T(8,128)(2,1)} async-done(((bf16[192,768]{1,0:T(8,128)(2,1)}), bf16[6144,768]{1,0:T(8,128)(2,1)}) %all-gather.7.cloned.1.call-update) | async-done | bytes 9437200 | tf_op jit(solution)/shard_map/all_gather | solution.py:401
  265.3 23.3 %shard_map.175 = bf16[4,384,768]{2,1,0:T(8,128)(2,1)} custom-call(bf16[4,384,768]{2,1,0:T(8,128)(2,1)} %shard_map.174.x_ref, f32[8,768]{1,0:T(8,128)} %stack.3.vec_ref, f32[1,3072]{1,0:T(1,128)} %broadcast_in_dim_reshape.7.b_in_ref, bf16[32,192,768]{2,1,0:T(8,128)(2,1)} %bitcast.48, bf16[32,192,768]{2,1,0:T(8,128)(2,1)} %bitcast.49), custom_call_target="tpu_custom_call" | custom-call | flops 15000000512 | bytes 15000000 | tf_op jit(solution)/shard_map/pallas_call | solution.py:128
  (34 shorter events, 0.2 us)
Async XLA Ops:
  6.5 166.5 %all-gather.5.cloned.1.call-start = ((), (), s32[]{:S(2)}) async-start(), calls=%async_computation.2 | async-start | bytes 8110080 | tf_op jit(solution)/shard_map/all_gather | solution.py:400
  7.3 3.0 %copy-start.5 = (f32[24]{0:T(128)S(1)}, f32[24]{0:T(128)}, u32[]{:S(2)}) copy-start(f32[24]{0:T(128)} %param.26) | copy-start | bytes 292
  7.3 3.0 %copy-start.6 = (f32[24]{0:T(128)S(1)}, f32[24]{0:T(128)}, u32[]{:S(2)}) copy-start(f32[24]{0:T(128)} %param.27) | copy-start | bytes 292
  7.3 3.0 %copy-start.7 = (f32[24]{0:T(128)S(1)}, f32[24]{0:T(128)}, u32[]{:S(2)}) copy-start(f32[24]{0:T(128)} %param.32) | copy-start | bytes 292
  7.3 3.0 %copy-start.8 = (f32[24]{0:T(128)S(1)}, f32[24]{0:T(128)}, u32[]{:S(2)}) copy-start(f32[24]{0:T(128)} %param.33) | copy-start | bytes 292
  7.3 3.0 %copy-start.9 = (f32[24]{0:T(128)S(1)}, f32[24]{0:T(128)}, u32[]{:S(2)}) copy-start(f32[24]{0:T(128)} %param.38) | copy-start | bytes 292
  7.3 3.0 %copy-start.10 = (f32[24]{0:T(128)S(1)}, f32[24]{0:T(128)}, u32[]{:S(2)}) copy-start(f32[24]{0:T(128)} %param.39) | copy-start | bytes 292
  7.3 3.0 %copy-start.11 = (f32[24]{0:T(128)S(1)}, f32[24]{0:T(128)}, u32[]{:S(2)}) copy-start(f32[24]{0:T(128)} %param.31) | copy-start | bytes 292
  7.4 3.0 %copy-start.12 = (f32[24]{0:T(128)S(1)}, f32[24]{0:T(128)}, u32[]{:S(2)}) copy-start(f32[24]{0:T(128)} %param.37) | copy-start | bytes 292
  7.4 3.0 %copy-start.13 = (f32[72]{0:T(128)S(1)}, f32[72]{0:T(128)}, u32[]{:S(2)}) copy-start(f32[72]{0:T(128)} %param.29) | copy-start | bytes 868
  7.4 3.0 %copy-start.14 = (f32[96]{0:T(128)S(1)}, f32[96]{0:T(128)}, u32[]{:S(2)}) copy-start(f32[96]{0:T(128)} %param.35) | copy-start | bytes 1156
  7.4 3.7 %copy-start.3 = (bf16[12,64,24]{1,2,0:T(8,128)(2,1)S(1)}, bf16[12,64,24]{1,2,0:T(8,128)(2,1)}, u32[]{:S(2)}) copy-start(bf16[12,64,24]{1,2,0:T(8,128)(2,1)} %param.30) | copy-start | bytes 110596
  11.2 29.7 %copy-start.2 = (bf16[768,72]{0,1:T(8,128)(2,1)S(1)}, bf16[768,72]{0,1:T(8,128)(2,1)}, u32[]{:S(2)}) copy-start(bf16[768,72]{0,1:T(8,128)(2,1)} %param.28) | copy-start | bytes 331780
  11.2 31.3 %copy-start = (bf16[96,768]{1,0:T(8,128)(2,1)S(1)}, bf16[96,768]{1,0:T(8,128)(2,1)}, u32[]{:S(2)}) copy-start(bf16[96,768]{1,0:T(8,128)(2,1)} %param.36) | copy-start | bytes 442372
  11.2 31.3 %copy-start.1 = (bf16[768,96]{0,1:T(8,128)(2,1)S(1)}, bf16[768,96]{0,1:T(8,128)(2,1)}, u32[]{:S(2)}) copy-start(bf16[768,96]{0,1:T(8,128)(2,1)} %param.34) | copy-start | bytes 442372
  11.2 33.1 %copy-start.15 = (f32[32]{0:T(128)S(1)}, f32[32]{0:T(128)}, u32[]{:S(2)}) copy-start(f32[32]{0:T(128)} %constant.165.clone.1) | copy-start | bytes 388
  42.5 222.8 %all-gather.7.cloned.1.call-start = ((), (), s32[]{:S(2)}) async-start(), calls=%async_computation.3 | async-start | bytes 9732096 | tf_op jit(solution)/shard_map/all_gather | solution.py:401
  77.1 92.4 %copy-start.4 = (bf16[768]{0:T(1024)(128)(2,1)S(1)}, bf16[768]{0:T(1024)(128)(2,1)}, u32[]{:S(2)}) copy-start(bf16[768]{0:T(1024)(128)(2,1)} %param.25) | copy-start | bytes 4612
Sparse Core Ops, SparseCore 0:
  42.6 108.1 all-gather.4
  153.7 111.5 all-gather.6

commit v7 on v6

--- a/solution.py
+++ b/solution.py
@@ -13,6 +13,7 @@
 
 
 SQRT_HALF = 0.5 ** 0.5
+LOG2_E = 1.4426950408889634
 FFN_PART = 768
 
 
@@ -65,8 +66,8 @@
         zero = jnp.zeros_like(q)
         mixed = []
         for mine in (low, ~low):
-            s = times_t(jnp.where(mine, q, zero), k) * size ** -0.5 + masked
-            p = jnp.exp(s - jnp.max(s, axis=-1, keepdims=True))
+            s = times_t(jnp.where(mine, q, zero), k) + masked
+            p = jnp.exp2((s - jnp.max(s, axis=-1, keepdims=True)) * (size ** -0.5 * LOG2_E))
             p = p * (1.0 / jnp.sum(p, axis=-1, keepdims=True))
             mixed.append(times(p.astype(jnp.bfloat16), v))
         ctx_ref[:, at:at + 2 * size] = jnp.where(low, mixed[0], mixed[1]).astype(jnp.bfloat16)
@@ -77,7 +78,6 @@
 
 
 def ffn_kernel(x_ref, vec_ref, b_in_ref, w_in_ref, w_back_ref, out_ref):
-    w_in_ref, w_back_ref = flat(w_in_ref), flat(w_back_ref)
     x = x_ref[0]
     total = jnp.zeros(x.shape, jnp.float32)
     for at in range(0, b_in_ref.shape[1], FFN_PART):
@@ -123,19 +123,19 @@
             b_qkv[None, :], *([weights] * len(sizes)))
 
 
-def feed(x, vecs, b_in, weights, sizes):
+def feed(x, vecs, b_in, w_in, w_back):
     batch, seq, width = x.shape
     return pl.pallas_call(
         ffn_kernel, out_shape=jax.ShapeDtypeStruct(x.shape, jnp.bfloat16), grid=(batch,),
-        in_specs=[each(seq, width), whole(8, width), whole(1, b_in.shape[0])] + pieces(weights, sizes),
+        in_specs=[each(seq, width), whole(8, width), whole(1, b_in.shape[0]), whole(*w_in.shape), whole(*w_back.shape)],
         out_specs=each(seq, width),
         compiler_params=pltpu.CompilerParams(vmem_limit_bytes=60 << 20),
         cost_estimate=pl.CostEstimate(flops=15 * 10 ** 9, bytes_accessed=15 * 10 ** 6, transcendentals=5 * 10 ** 6))(
-            x, vecs, b_in[None, :], *([weights] * len(sizes)))
+            x, vecs, b_in[None, :], w_in, w_back)
 
 
 HEAD = 2048
-CAPS = ((0, 1, 168), (1, 2, 88), (2, 4, 64), (4, 8, 48), (8, 32, 40))
+CAPS = ((0, 1, 152), (1, 2, 88), (2, 4, 72), (4, 8, 48), (8, 32, 40))
 HOT = 2
 EXTRA = 48
 PLANE = 8
@@ -396,9 +396,9 @@
         told, piece = tell(n_dev, message.reshape(-1, 128), tok_shard)
         told = told.reshape(n_dev, -1)
         first = [piece, w_qkv.T, w_out.reshape(num_heads * head_dim, -1).T]
-        second = [w_ffn_in.T, w_ffn_out]
+        w_in_full = lax.all_gather(w_ffn_in.T, 'fsdp', axis=0, tiled=True)
         weights_a = lax.all_gather(jnp.concatenate(first, axis=0), 'fsdp', axis=0, tiled=False)
-        weights_b = lax.all_gather(jnp.concatenate(second, axis=0), 'fsdp', axis=0, tiled=False)
+        w_back_full = lax.all_gather(w_ffn_out, 'fsdp', axis=0, tiled=True)
 
         at = wide + 128
         vectors = []
@@ -445,7 +445,7 @@
         vecs = jnp.stack([emb_g, emb_b, ln1_g, ln1_b, ln2_g, ln2_b, b_out_f, b_back_f])
         x = attend(num_heads, head_dim, batch_dev, spot, got, pos_table, type_row, vecs, b_qkv_f, weights_a,
                    [w.shape[0] for w in first])
-        return feed(x, vecs, b_in_f, weights_b, [w.shape[0] for w in second])
+        return feed(x, vecs, b_in_f, w_in_full, w_back_full)
 
     vec_spec = P('fsdp')
     in_specs = (P('fsdp', None), P('fsdp', None), P(None, None), P(None), vec_spec, vec_spec,

time: 296 us -> 345 us (1.17)
  waiting for transfers between devices: 38.2 us -> 95.1 us
  Pallas kernels: 199 us -> 194 us
    all_gather x1 -> x2, waiting for transfers between devices: 38.2 us -> 93.7 us  [the longest x1 64.9 us: local_step(): w_back_full = lax.all_gather(w_ffn_out, 'fsdp', axis=0, tiled=True)]
    pallas_call x1, Pallas kernels: 92.4 us -> 87.7 us  [swap(): pl.pallas_call(lambda *refs: swap_kernel(n, *refs), out_shape=jax.ShapeDt...]
  transfers between devices with their start and end apart: 2 -> 3, of which waited for: 1 -> 2; matrix products, arithmetic and copies ran while one was open for 13% -> 10% of each run, Pallas kernels for 49% -> 41%
where the time goes in v7:
time: 345 us
  Pallas kernels  194 us (56%)
  waiting for transfers between devices  95.1 us (28%)
  local copies, waits for them, and re-layouts  36.3 us (11%)
  between operations  14.1 us (4%)
  other arithmetic  3.99 us (1%)
    pallas_call x1, Pallas kernels, swap(): pl.pallas_call(lambda *refs: swap_kernel(n, *refs), out_shape=jax.ShapeDt...  87.7 us
    all_gather x1, waiting for transfers between devices, local_step(): w_back_full = lax.all_gather(w_ffn_out, 'fsdp', axis=0, tiled=True)  64.9 us
    pallas_call x1, Pallas kernels, attend(): pl.pallas_call(functools.partial(attention_kernel, (heads, size)), out_sh...  53.1 us
    pallas_call x1, Pallas kernels, tell(): pl.pallas_call(lambda *refs: tell_kernel(n, part, *refs), out_shape=(jax....  29.6 us
    gather x1, local copies, waits for them, and re-layouts, local_step(): jnp.take(tok_shard, wanted.reshape(-1), axis=0, mode='clip')  29.4 us
    all_gather x1, waiting for transfers between devices, local_step(): w_in_full = lax.all_gather(w_ffn_in.T, 'fsdp', axis=0, tiled=True)  28.8 us
    pallas_call x1, Pallas kernels, feed(): pl.pallas_call(ffn_kernel, out_shape=jax.ShapeDtypeStruct(x.shape, jnp.bf...  23.3 us
  transfers between devices with their start and end apart: 3, of which 2 were waited for; matrix products, arithmetic and copies ran while one was open for 10% of the time, Pallas kernels for 41%

profile of v7, /device:TPU:0, one launch (start us, length us, event | category | flops | bytes accessed | tf_op | source)
XLA Modules:
  0.0 344.8 jit_solution(9610635406892582387)
XLA Ops:
  6.5 0.7 reshape.276
  7.3 0.0 copy-start.4
  7.3 0.0 copy-start.5
  7.3 0.0 copy-start.8
  7.3 0.0 copy-start.9
  7.4 0.0 copy-start.12
  7.4 0.0 copy-start.1
  7.4 1.3 fusion.5
  8.7 0.3 convert_reduce_fusion
  9.0 1.3 select_reduce_fusion.1
  10.4 0.1 concatenate.9
  10.5 0.6 pad_bitcast_fusion.refs_0_
  11.1 0.1 reshape.281
  11.2 0.0 copy-start.13
  11.2 29.6 %shard_map.172 = (f32[32,16,128]{2,1,0:T(8,128)}, bf16[64,768]{1,0:T(8,128)(2,1)}) custom-call(f32[16,128]{1,0:T(8,128)} %pad_bitcast_fusion.refs_0_, bf16[15664,768]{1,0:T(8,128)(2,1)} %refs_1_.1), custom_call_target="tpu_custom_call" | custom-call | tf_op jit(solution)/shard_map/pallas_call | solution.py:223
  40.8 1.6 pad_maximum_fusion.1
  42.4 0.0 all-gather.9.cloned.1.call-update
  42.5 0.0 all-gather.5.cloned.1.call-start
  42.5 0.7 all-gather.5.cloned.1.call-update
  43.2 0.0 all-gather.7.cloned.1.call-start
  43.3 0.7 all-gather.7.cloned.1.call-update
  43.9 1.0 copy.26
  45.0 0.7 fusion.10
  46.3 0.1 slice.71
  46.4 0.1 slice.72
  46.5 0.1 clamp_bitcast_fusion
  46.6 0.1 reshape.311
  46.7 29.4 %gather_fusion.3 = bf16[4864,768]{1,0:T(8,128)(2,1)} fusion(bf16[15664,768]{1,0:T(8,128)(2,1)} %refs_1_.1, s32[5120]{0:T(1024)S(1)} %pad_clamp_fusion.3), kind=kCustom, calls=%fused_computation.3 | custom fusion | bytes 14961664 | tf_op jit(solution)/shard_map/jit(_take)/gather | solution.py:417
  76.1 87.7 %shard_map.173 = bf16[1536,768]{1,0:T(8,128)(2,1)} custom-call(bf16[32,152,768]{2,1,0:T(8,128)(2,1)} %bitcast.30), custom_call_target="tpu_custom_call" | custom-call | tf_op jit(solution)/shard_map/pallas_call | solution.py:351
  163.8 0.6 broadcast_in_dim.89.type_ref
  164.4 0.1 fusion.24
  164.5 0.1 stack_reshape.24
  164.6 0.1 stack_reshape.25
  164.7 0.1 stack_reshape.26
  164.8 0.1 stack_reshape.27
  164.9 0.1 stack_reshape.28
  165.0 0.1 stack_reshape.29
  165.1 0.1 stack_reshape.30
  165.2 0.1 stack_reshape.31
  165.2 0.7 broadcast_in_dim_reshape.6.b_qkv_ref
  165.9 0.7 broadcast_in_dim_reshape.7.b_in_ref
  166.6 0.6 stack.3.vec_ref
  167.3 0.2 conditional.1
  167.5 0.6 reshape.329.spot_row_ref
  168.1 53.1 %shard_map.174.x_ref = bf16[4,384,768]{2,1,0:T(8,128)(2,1)} custom-call(s32[4,1,384]{2,1,0:T(1,128)} %reshape.329.spot_row_ref, bf16[1536,768]{1,0:T(8,128)(2,1)} %get-tuple-element.214.got_ref, bf16[512,768]{1,0:T(8,128)(2,1)} %pos_ref.1, bf16[1,768]{1,0:T(2,128)(2,1)} %broadcast_in_dim.89.type_ref, f32[8,768]{1,0:T(8,128)} %stack.3.vec_ref, ...), custom_call_target="tpu_custom_call" | custom-call | flops 20000000000 | bytes 15000000 | tf_op jit(solution)/shard_map/pallas_call | solution.py:112
  221.3 28.8 %all-gather.5.cloned.1.call-done.w_in_ref = bf16[3072,768]{1,0:T(8,128)(2,1)} async-done(((bf16[96,768]{1,0:T(8,128)(2,1)}), bf16[3072,768]{1,0:T(8,128)(2,1)}) %all-gather.5.cloned.1.call-update) | async-done | bytes 4718608 | tf_op jit(solution)/shard_map/all_gather | solution.py:399
  250.1 64.9 %all-gather.7.cloned.1.call-done.w_back_ref = bf16[3072,768]{1,0:T(8,128)(2,1)} async-done(((bf16[96,768]{1,0:T(8,128)(2,1)}), bf16[3072,768]{1,0:T(8,128)(2,1)}) %all-gather.7.cloned.1.call-update) | async-done | bytes 4718608 | tf_op jit(solution)/shard_map/all_gather | solution.py:401
  315.0 23.3 %shard_map.175 = bf16[4,384,768]{2,1,0:T(8,128)(2,1)} custom-call(bf16[4,384,768]{2,1,0:T(8,128)(2,1)} %shard_map.174.x_ref, f32[8,768]{1,0:T(8,128)} %stack.3.vec_ref, f32[1,3072]{1,0:T(1,128)} %broadcast_in_dim_reshape.7.b_in_ref, bf16[3072,768]{1,0:T(8,128)(2,1)} %all-gather.5.cloned.1.call-done.w_in_ref, ...), custom_call_target="tpu_custom_call" | custom-call | flops 15000000512 | bytes 15000000 | tf_op jit(solution)/shard_map/pallas_call | solution.py:128
  (32 shorter events, 0.2 us)
Async XLA Ops:
  6.5 160.7 %all-gather.9.cloned.1.call-start = ((), (), s32[]{:S(2)}) async-start(), calls=%async_computation.4 | async-start | bytes 8110080 | tf_op jit(solution)/shard_map/all_gather | solution.py:400
  7.3 3.0 copy-start.3
  7.3 3.0 copy-start.4
  7.3 3.0 copy-start.5
  7.3 3.0 copy-start.6
  7.3 3.0 copy-start.7
  7.3 3.0 copy-start.8
  7.3 3.0 copy-start.9
  7.4 3.0 copy-start.10
  7.4 3.0 copy-start.11
  7.4 3.0 copy-start.12
  7.4 3.7 %copy-start.1 = (bf16[12,64,24]{1,2,0:T(8,128)(2,1)S(1)}, bf16[12,64,24]{1,2,0:T(8,128)(2,1)}, u32[]{:S(2)}) copy-start(bf16[12,64,24]{1,2,0:T(8,128)(2,1)} %param.30) | copy-start | bytes 110596
  11.2 29.6 %copy-start = (bf16[768,72]{0,1:T(8,128)(2,1)S(1)}, bf16[768,72]{0,1:T(8,128)(2,1)}, u32[]{:S(2)}) copy-start(bf16[768,72]{0,1:T(8,128)(2,1)} %param.28) | copy-start | bytes 331780
  11.2 33.8 %copy-start.13 = (f32[32]{0:T(128)S(1)}, f32[32]{0:T(128)}, u32[]{:S(2)}) copy-start(f32[32]{0:T(128)} %constant.167.clone.1) | copy-start | bytes 388
  42.5 207.6 %all-gather.5.cloned.1.call-start = ((), (), s32[]{:S(2)}) async-start(), calls=%async_computation.2 | async-start | bytes 4866048 | tf_op jit(solution)/shard_map/all_gather | solution.py:399
  43.2 271.8 %all-gather.7.cloned.1.call-start = ((), (), s32[]{:S(2)}) async-start(), calls=%async_computation.3 | async-start | bytes 4866048 | tf_op jit(solution)/shard_map/all_gather | solution.py:401
  76.1 87.7 %copy-start.2 = (bf16[768]{0:T(1024)(128)(2,1)S(1)}, bf16[768]{0:T(1024)(128)(2,1)}, u32[]{:S(2)}) copy-start(bf16[768]{0:T(1024)(128)(2,1)} %param.25) | copy-start | bytes 4612
Sparse Core Ops, SparseCore 0:
  42.6 111.1 all-gather.8
  156.6 93.4 all-gather.4
  253.0 61.9 all-gather.6

commit v8 on v7

--- a/solution.py
+++ b/solution.py
@@ -7,7 +7,6 @@
 from jax.experimental.pallas import tpu as pltpu
 from jax.sharding import PartitionSpec as P
 
-
 PAD_ID = 1
 LN_EPS = 1e-5
 
@@ -35,11 +34,12 @@
     return ref.reshape(ref.shape[0] * ref.shape[1], ref.shape[2])
 
 
-def attention_kernel(dims, spot_row_ref, got_ref, pos_ref, type_ref, vec_ref, b_qkv_ref, head_ref, w_qkv_ref, w_out_ref, out_ref,
-                     qkv_ref, ctx_ref, x_ref):
+def layer_kernel(dims, spot_row_ref, got_ref, pos_ref, type_ref, vec_ref, b_qkv_ref, b_in_ref, head_ref, w_qkv_ref, w_out_ref,
+                 w_in_ref, w_back_ref, out_ref, qkv_ref, ctx_ref, x_ref):
     heads, size = dims
     seq, width = out_ref.shape[1:]
-    head_ref, w_qkv_ref, w_out_ref = flat(head_ref), flat(w_qkv_ref), flat(w_out_ref)
+    head_ref, w_qkv_ref, w_out_ref, w_in_ref, w_back_ref = (
+        flat(r) for r in (head_ref, w_qkv_ref, w_out_ref, w_in_ref, w_back_ref))
     spot = jnp.transpose(jnp.broadcast_to(spot_row_ref[0].astype(jnp.float32), (8, seq)))[:, 0:1].astype(jnp.int32)
     total = jnp.zeros((seq, width), jnp.float32)
     step = 256
@@ -74,17 +74,14 @@
 
     a = (times_t(ctx_ref[...], w_out_ref[...]) + vec_ref[6:7, :]).astype(jnp.bfloat16)
     z = x_ref[...].astype(jnp.float32) + a.astype(jnp.float32)
-    out_ref[0] = norm(z, vec_ref[2:3, :], vec_ref[3:4, :]).astype(jnp.bfloat16)
-
-
-def ffn_kernel(x_ref, vec_ref, b_in_ref, w_in_ref, w_back_ref, out_ref):
-    x = x_ref[0]
-    total = jnp.zeros(x.shape, jnp.float32)
+    x_ref[...] = norm(z, vec_ref[2:3, :], vec_ref[3:4, :]).astype(jnp.bfloat16)
+
+    total = jnp.zeros((seq, width), jnp.float32)
     for at in range(0, b_in_ref.shape[1], FFN_PART):
-        h = times_t(x, w_in_ref[at:at + FFN_PART, :]) + b_in_ref[:, at:at + FFN_PART]
+        h = times_t(x_ref[...], w_in_ref[at:at + FFN_PART, :]) + b_in_ref[:, at:at + FFN_PART]
         h = (0.5 * h * (1.0 + lax.erf(h * SQRT_HALF))).astype(jnp.bfloat16)
         total += times(h, w_back_ref[at:at + FFN_PART, :])
-    z = x.astype(jnp.float32) + (total + vec_ref[7:8, :])
+    z = x_ref[...].astype(jnp.float32) + (total + vec_ref[7:8, :])
     out_ref[0] = norm(z, vec_ref[4:5, :], vec_ref[5:6, :]).astype(jnp.bfloat16)
 
 
@@ -105,33 +102,22 @@
     return out
 
 
-def attend(heads, size, batch, spot, got, pos_table, type_row, vecs, b_qkv, weights, sizes):
+def layer(heads, size, batch, spot, got, pos_table, type_row, vecs, b_qkv, b_in, weights, sizes):
     seq = spot.shape[0] // batch
     width = got.shape[1]
     block = pltpu.VMEM((seq, width), jnp.bfloat16)
     return pl.pallas_call(
-        functools.partial(attention_kernel, (heads, size)),
+        functools.partial(layer_kernel, (heads, size)),
         out_shape=jax.ShapeDtypeStruct((batch, seq, width), jnp.bfloat16),
         grid=(batch,),
         in_specs=[each(1, seq), whole(*got.shape), whole(*pos_table.shape), whole(1, width),
-                  whole(8, width), whole(1, 3 * width)] + pieces(weights, sizes),
+                  whole(8, width), whole(1, 3 * width), whole(1, b_in.shape[0])] + pieces(weights, sizes),
         out_specs=each(seq, width),
         scratch_shapes=[pltpu.VMEM((seq, 3 * width), jnp.bfloat16), block, block],
         compiler_params=pltpu.CompilerParams(vmem_limit_bytes=60 << 20),
         cost_estimate=pl.CostEstimate(flops=20 * 10 ** 9, bytes_accessed=15 * 10 ** 6, transcendentals=7 * 10 ** 6))(
             spot.reshape(batch, 1, seq), got, pos_table, type_row[None, :], vecs,
-            b_qkv[None, :], *([weights] * len(sizes)))
-
-
-def feed(x, vecs, b_in, w_in, w_back):
-    batch, seq, width = x.shape
-    return pl.pallas_call(
-        ffn_kernel, out_shape=jax.ShapeDtypeStruct(x.shape, jnp.bfloat16), grid=(batch,),
-        in_specs=[each(seq, width), whole(8, width), whole(1, b_in.shape[0]), whole(*w_in.shape), whole(*w_back.shape)],
-        out_specs=each(seq, width),
-        compiler_params=pltpu.CompilerParams(vmem_limit_bytes=60 << 20),
-        cost_estimate=pl.CostEstimate(flops=15 * 10 ** 9, bytes_accessed=15 * 10 ** 6, transcendentals=5 * 10 ** 6))(
-            x, vecs, b_in[None, :], w_in, w_back)
+            b_qkv[None, :], b_in[None, :], *([weights] * len(sizes)))
 
 
 HEAD = 2048
@@ -395,10 +381,8 @@
         message = jnp.pad(message, (0, -message.shape[0] % 1024))
         told, piece = tell(n_dev, message.reshape(-1, 128), tok_shard)
         told = told.reshape(n_dev, -1)
-        first = [piece, w_qkv.T, w_out.reshape(num_heads * head_dim, -1).T]
-        w_in_full = lax.all_gather(w_ffn_in.T, 'fsdp', axis=0, tiled=True)
-        weights_a = lax.all_gather(jnp.concatenate(first, axis=0), 'fsdp', axis=0, tiled=False)
-        w_back_full = lax.all_gather(w_ffn_out, 'fsdp', axis=0, tiled=True)
+        parts = [piece, w_qkv.T, w_out.reshape(num_heads * head_dim, -1).T, w_ffn_in.T, w_ffn_out]
+        weights = lax.all_gather(jnp.concatenate(parts, axis=0), 'fsdp', axis=0, tiled=False)
 
         at = wide + 128
         vectors = []
@@ -436,16 +420,15 @@
             return r + 1, jnp.where(live[:, None], new, rows_now)
 
         def slow(got_now, spot_now):
-            head = weights_a[:, :piece.shape[0]].reshape(HEAD, width)
+            head = weights[:, :piece.shape[0]].reshape(HEAD, width)
             rows_now = jnp.take(jnp.concatenate([head, got_now], axis=0), spot_now, axis=0, mode='clip')
             _, rows_now = lax.while_loop(lambda state: state[0] < rounds, again, (jnp.int32(0), rows_now))
             return jnp.pad(rows_now, ((0, slots - n_tok), (0, 0))), jnp.where(ids == PAD_ID, spot_now, HEAD + place)
 
         got, spot = lax.cond(rounds > 0, slow, lambda g, p: (g, p), got, spot)
         vecs = jnp.stack([emb_g, emb_b, ln1_g, ln1_b, ln2_g, ln2_b, b_out_f, b_back_f])
-        x = attend(num_heads, head_dim, batch_dev, spot, got, pos_table, type_row, vecs, b_qkv_f, weights_a,
-                   [w.shape[0] for w in first])
-        return feed(x, vecs, b_in_f, w_in_full, w_back_full)
+        return layer(num_heads, head_dim, batch_dev, spot, got, pos_table, type_row, vecs, b_qkv_f, b_in_f, weights,
+                     [w.shape[0] for w in parts])
 
     vec_spec = P('fsdp')
     in_specs = (P('fsdp', None), P('fsdp', None), P(None, None), P(None), vec_spec, vec_spec,

time: 345 us -> 316 us (0.916)
  the two profiles are of different devices: /device:TPU:0 before, /device:TPU:11 now
where the time goes in v8:
time: 316 us; the launch traced here: 315 us
  Pallas kernels  258 us (82%)
  local copies, waits for them, and re-layouts  38 us (12%)
  between operations  14.5 us (5%)
    pallas_call x1, Pallas kernels, swap(): pl.pallas_call(lambda *refs: swap_kernel(n, *refs), out_shape=jax.ShapeDt...  156 us
    pallas_call x1, Pallas kernels, layer(): pl.pallas_call(functools.partial(layer_kernel, (heads, size)), out_shape=...  71.9 us
    pallas_call x1, Pallas kernels, tell(): pl.pallas_call(lambda *refs: tell_kernel(n, part, *refs), out_shape=(jax....  30 us
    gather x1, local copies, waits for them, and re-layouts, local_step(): jnp.take(tok_shard, wanted.reshape(-1), axis=0, mode='clip')  29.4 us
  transfers between devices with their start and end apart: 1, of which 1 were waited for; matrix products, arithmetic and copies ran while one was open for 11% of the time, Pallas kernels for 50%

profile of v8, /device:TPU:11, one launch (start us, length us, event | category | flops | bytes accessed | tf_op | source)
XLA Modules:
  0.0 315.5 jit_solution(11363167247880987055)
XLA Ops:
  6.5 0.7 reshape.276
  7.3 0.3 convert_reduce_fusion
  7.6 0.0 copy-start.7
  7.6 0.0 copy-start.8
  7.6 0.0 copy-start.9
  7.6 0.0 copy-start.10
  7.6 0.0 copy-start.11
  7.6 0.0 copy-start.12
  7.7 0.0 copy-start.13
  7.7 0.0 copy-start.14
  7.7 0.0 copy-start.15
  7.7 0.0 copy-start.4
  7.7 1.3 fusion.5
  9.0 1.3 select_reduce_fusion.1
  10.4 0.1 concatenate.9
  10.5 0.6 pad_bitcast_fusion.refs_0_
  11.1 0.1 reshape.281
  11.2 0.0 copy-start.1
  11.2 0.0 copy-start.2
  11.2 0.0 copy-start.16
  11.3 30.0 %shard_map.172 = (f32[32,16,128]{2,1,0:T(8,128)}, bf16[64,768]{1,0:T(8,128)(2,1)}) custom-call(f32[16,128]{1,0:T(8,128)} %pad_bitcast_fusion.refs_0_, bf16[15664,768]{1,0:T(8,128)(2,1)} %refs_1_.1), custom_call_target="tpu_custom_call" | custom-call | tf_op jit(solution)/shard_map/pallas_call | solution.py:209
  41.3 0.9 constant_dynamic-update-slice_fusion.1
  42.3 0.8 copy-done
  43.1 0.0 all-gather.3.cloned.1.call-update
  43.1 1.0 copy.27
  44.2 0.7 fusion.10
  45.6 0.1 slice.71
  45.6 0.1 slice.72
  45.7 0.6 broadcast_in_dim.89.type_ref
  46.3 0.7 broadcast_in_dim_reshape.6.b_qkv_ref
  47.0 0.7 broadcast_in_dim_reshape.7.b_in_ref
  47.7 0.1 fusion.24
  47.8 0.1 stack_reshape.31
  47.9 0.1 clamp_bitcast_fusion
  48.0 0.1 reshape.311
  48.1 0.1 stack_reshape.30
  48.2 0.1 stack_reshape.29
  48.3 0.1 stack_reshape.28
  48.4 0.1 stack_reshape.27
  48.5 0.1 stack_reshape.26
  48.6 0.1 stack_reshape.25
  48.7 0.1 stack_reshape.24
  48.8 29.4 %gather_fusion.3 = bf16[4864,768]{1,0:T(8,128)(2,1)} fusion(bf16[15664,768]{1,0:T(8,128)(2,1)} %refs_1_.1, s32[5120]{0:T(1024)S(1)} %pad_clamp_fusion.3), kind=kCustom, calls=%fused_computation.3 | custom fusion | bytes 14961664 | tf_op jit(solution)/shard_map/jit(_take)/gather | solution.py:401
  78.1 156.3 %shard_map.173 = bf16[1536,768]{1,0:T(8,128)(2,1)} custom-call(bf16[32,152,768]{2,1,0:T(8,128)(2,1)} %bitcast.40), custom_call_target="tpu_custom_call" | custom-call | tf_op jit(solution)/shard_map/pallas_call | solution.py:337
  234.4 0.6 stack.3.vec_ref
  235.1 1.1 all-gather.3.cloned.1.call-done
  236.1 0.6 reshape.329.spot_row_ref
  236.7 71.9 %shard_map.174 = bf16[4,384,768]{2,1,0:T(8,128)(2,1)} custom-call(s32[4,1,384]{2,1,0:T(1,128)} %reshape.329.spot_row_ref, bf16[1536,768]{1,0:T(8,128)(2,1)} %get-tuple-element.214.got_ref, bf16[512,768]{1,0:T(8,128)(2,1)} %pos_ref.1, bf16[1,768]{1,0:T(2,128)(2,1)} %broadcast_in_dim.89.type_ref, f32[8,768]{1,0:T(8,128)} %stack.3.vec_ref, ...), custom_call_target="tpu_custom_call" | custom-call | flops 20000000000 | bytes 15000000 | tf_op jit(solution)/shard_map/pallas_call | solution.py:109
  (35 shorter events, 0.2 us)
Async XLA Ops:
  6.5 229.6 %all-gather.3.cloned.1.call-start = ((), (), s32[]{:S(2)}) async-start(), calls=%async_computation.2 | async-start | bytes 17842176 | tf_op jit(solution)/shard_map/all_gather | solution.py:385
  7.6 2.7 copy-start.6
  7.6 2.7 copy-start.7
  7.6 2.7 copy-start.8
  7.6 2.7 copy-start.9
  7.6 2.7 copy-start.10
  7.6 2.7 copy-start.11
  7.6 2.7 copy-start.12
  7.7 2.7 copy-start.13
  7.7 2.7 copy-start.14
  7.7 2.7 copy-start.15
  7.7 3.4 %copy-start.4 = (bf16[12,64,24]{1,2,0:T(8,128)(2,1)S(1)}, bf16[12,64,24]{1,2,0:T(8,128)(2,1)}, u32[]{:S(2)}) copy-start(bf16[12,64,24]{1,2,0:T(8,128)(2,1)} %param.30) | copy-start | bytes 110596
  11.2 31.0 %copy-start.3 = (bf16[768,72]{0,1:T(8,128)(2,1)S(1)}, bf16[768,72]{0,1:T(8,128)(2,1)}, u32[]{:S(2)}) copy-start(bf16[768,72]{0,1:T(8,128)(2,1)} %param.28) | copy-start | bytes 331780
  11.2 31.0 %copy-start.1 = (bf16[768,96]{0,1:T(8,128)(2,1)S(1)}, bf16[768,96]{0,1:T(8,128)(2,1)}, u32[]{:S(2)}) copy-start(bf16[768,96]{0,1:T(8,128)(2,1)} %param.34) | copy-start | bytes 442372
  11.2 31.0 %copy-start.2 = (bf16[96,768]{1,0:T(8,128)(2,1)S(1)}, bf16[96,768]{1,0:T(8,128)(2,1)}, u32[]{:S(2)}) copy-start(bf16[96,768]{1,0:T(8,128)(2,1)} %param.36) | copy-start | bytes 442372
  11.2 32.9 %copy-start.16 = (f32[32]{0:T(128)S(1)}, f32[32]{0:T(128)}, u32[]{:S(2)}) copy-start(f32[32]{0:T(128)} %constant.167.clone.1) | copy-start | bytes 388
  11.3 34.5 %copy-start.5 = (bf16[768]{0:T(1024)(128)(2,1)S(1)}, bf16[768]{0:T(1024)(128)(2,1)}, u32[]{:S(2)}) copy-start(bf16[768]{0:T(1024)(128)(2,1)} %param.25) | copy-start | bytes 4612
  42.3 0.8 copy-start
Sparse Core Ops, SparseCore 0:
  43.2 192.8 all-gather.2

commit v9 on v8

--- a/solution.py
+++ b/solution.py
@@ -235,7 +235,7 @@
 
 
 def relayed(p, z):
-    return z > 0 and 2 <= p and p < PLANE - 1 and (p, z) != (PLANE - 2, 3)
+    return z > 0 and p >= PLANE // 2
 
 
 def swap_kernel(n, send_ref, recv_ref, relay_ref, send_sem, recv_sem, lend_sem, pass_sem, own_sem):

time: 316 us -> 296 us (0.937)
  the two profiles are of different devices: /device:TPU:11 before, /device:TPU:15 now
where the time goes in v9:
time: 296 us
  Pallas kernels  212 us (72%)
  local copies, waits for them, and re-layouts  38 us (13%)
  waiting for transfers between devices  28.3 us (10%)
  between operations  14.5 us (5%)
    pallas_call x1, Pallas kernels, swap(): pl.pallas_call(lambda *refs: swap_kernel(n, *refs), out_shape=jax.ShapeDt...  118 us
    pallas_call x1, Pallas kernels, layer(): pl.pallas_call(functools.partial(layer_kernel, (heads, size)), out_shape=...  71.9 us
    gather x1, local copies, waits for them, and re-layouts, local_step(): jnp.take(tok_shard, wanted.reshape(-1), axis=0, mode='clip')  29.4 us
    all_gather x1, waiting for transfers between devices, local_step(): lax.all_gather(jnp.concatenate(parts, axis=0), 'fsdp', axis=0, tiled=False)  28.3 us
    pallas_call x1, Pallas kernels, tell(): pl.pallas_call(lambda *refs: tell_kernel(n, part, *refs), out_shape=(jax....  21.5 us
  transfers between devices with their start and end apart: 1, of which 1 were waited for; matrix products, arithmetic and copies ran while one was open for 12% of the time, Pallas kernels for 40%

profile of v9, /device:TPU:15, one launch (start us, length us, event | category | flops | bytes accessed | tf_op | source)
XLA Modules:
  0.0 296.0 jit_solution(14454938757002847053)
XLA Ops:
  6.5 0.7 reshape.276
  7.3 0.3 convert_reduce_fusion
  7.6 0.0 copy-start.7
  7.6 0.0 copy-start.8
  7.6 0.0 copy-start.9
  7.6 0.0 copy-start.10
  7.6 0.0 copy-start.11
  7.6 0.0 copy-start.12
  7.7 0.0 copy-start.13
  7.7 0.0 copy-start.14
  7.7 0.0 copy-start.15
  7.7 0.0 copy-start.4
  7.7 1.3 fusion.5
  9.0 1.3 select_reduce_fusion.1
  10.4 0.1 concatenate.9
  10.5 0.6 pad_bitcast_fusion.refs_0_
  11.1 0.1 reshape.281
  11.2 0.0 copy-start.1
  11.2 0.0 copy-start.2
  11.2 0.0 copy-start.16
  11.3 21.5 %shard_map.172 = (f32[32,16,128]{2,1,0:T(8,128)}, bf16[64,768]{1,0:T(8,128)(2,1)}) custom-call(f32[16,128]{1,0:T(8,128)} %pad_bitcast_fusion.refs_0_, bf16[15664,768]{1,0:T(8,128)(2,1)} %refs_1_.1), custom_call_target="tpu_custom_call" | custom-call | tf_op jit(solution)/shard_map/pallas_call | solution.py:209
  32.8 0.9 constant_dynamic-update-slice_fusion.1
  33.8 0.8 copy-done
  34.6 0.0 all-gather.3.cloned.1.call-update
  34.7 1.0 copy.27
  35.7 0.7 fusion.10
  37.1 0.1 slice.71
  37.1 0.1 slice.72
  37.2 0.6 broadcast_in_dim.89.type_ref
  37.8 0.7 broadcast_in_dim_reshape.6.b_qkv_ref
  38.5 0.7 broadcast_in_dim_reshape.7.b_in_ref
  39.2 0.1 fusion.24
  39.3 0.1 stack_reshape.31
  39.4 0.1 clamp_bitcast_fusion
  39.5 0.1 reshape.311
  39.6 0.1 stack_reshape.30
  39.7 0.1 stack_reshape.29
  39.8 0.1 stack_reshape.28
  39.9 0.1 stack_reshape.27
  40.0 0.1 stack_reshape.26
  40.1 0.1 stack_reshape.25
  40.2 0.1 stack_reshape.24
  40.3 29.4 %gather_fusion.3 = bf16[4864,768]{1,0:T(8,128)(2,1)} fusion(bf16[15664,768]{1,0:T(8,128)(2,1)} %refs_1_.1, s32[5120]{0:T(1024)S(1)} %pad_clamp_fusion.3), kind=kCustom, calls=%fused_computation.3 | custom fusion | bytes 14961664 | tf_op jit(solution)/shard_map/jit(_take)/gather | solution.py:401
  69.6 118.1 %shard_map.173 = bf16[1536,768]{1,0:T(8,128)(2,1)} custom-call(bf16[32,152,768]{2,1,0:T(8,128)(2,1)} %bitcast.40), custom_call_target="tpu_custom_call" | custom-call | tf_op jit(solution)/shard_map/pallas_call | solution.py:337
  187.7 0.6 stack.3.vec_ref
  188.4 28.3 %all-gather.3.cloned.1.call-done = bf16[11264,768]{1,0:T(8,128)(2,1)} async-done(((bf16[352,768]{1,0:T(8,128)(2,1)}), bf16[11264,768]{1,0:T(8,128)(2,1)}) %all-gather.3.cloned.1.call-update) | async-done | bytes 17301520 | tf_op jit(solution)/shard_map/all_gather | solution.py:385
  216.7 0.6 reshape.329.spot_row_ref
  217.3 71.9 %shard_map.174 = bf16[4,384,768]{2,1,0:T(8,128)(2,1)} custom-call(s32[4,1,384]{2,1,0:T(1,128)} %reshape.329.spot_row_ref, bf16[1536,768]{1,0:T(8,128)(2,1)} %get-tuple-element.214.got_ref, bf16[512,768]{1,0:T(8,128)(2,1)} %pos_ref.1, bf16[1,768]{1,0:T(2,128)(2,1)} %broadcast_in_dim.89.type_ref, f32[8,768]{1,0:T(8,128)} %stack.3.vec_ref, ...), custom_call_target="tpu_custom_call" | custom-call | flops 20000000000 | bytes 15000000 | tf_op jit(solution)/shard_map/pallas_call | solution.py:109
  (35 shorter events, 0.2 us)
Async XLA Ops:
  6.5 210.1 %all-gather.3.cloned.1.call-start = ((), (), s32[]{:S(2)}) async-start(), calls=%async_computation.2 | async-start | bytes 17842176 | tf_op jit(solution)/shard_map/all_gather | solution.py:385
  7.6 2.7 copy-start.6
  7.6 2.7 copy-start.7
  7.6 2.7 copy-start.8
  7.6 2.7 copy-start.9
  7.6 2.7 copy-start.10
  7.6 2.7 copy-start.11
  7.6 2.7 copy-start.12
  7.7 2.7 copy-start.13
  7.7 2.7 copy-start.14
  7.7 2.7 copy-start.15
  7.7 3.4 %copy-start.4 = (bf16[12,64,24]{1,2,0:T(8,128)(2,1)S(1)}, bf16[12,64,24]{1,2,0:T(8,128)(2,1)}, u32[]{:S(2)}) copy-start(bf16[12,64,24]{1,2,0:T(8,128)(2,1)} %param.30) | copy-start | bytes 110596
  11.2 22.5 %copy-start.3 = (bf16[768,72]{0,1:T(8,128)(2,1)S(1)}, bf16[768,72]{0,1:T(8,128)(2,1)}, u32[]{:S(2)}) copy-start(bf16[768,72]{0,1:T(8,128)(2,1)} %param.28) | copy-start | bytes 331780
  11.2 22.5 %copy-start.1 = (bf16[768,96]{0,1:T(8,128)(2,1)S(1)}, bf16[768,96]{0,1:T(8,128)(2,1)}, u32[]{:S(2)}) copy-start(bf16[768,96]{0,1:T(8,128)(2,1)} %param.34) | copy-start | bytes 442372
  11.2 22.5 %copy-start.2 = (bf16[96,768]{1,0:T(8,128)(2,1)S(1)}, bf16[96,768]{1,0:T(8,128)(2,1)}, u32[]{:S(2)}) copy-start(bf16[96,768]{1,0:T(8,128)(2,1)} %param.36) | copy-start | bytes 442372
  11.2 24.5 %copy-start.16 = (f32[32]{0:T(128)S(1)}, f32[32]{0:T(128)}, u32[]{:S(2)}) copy-start(f32[32]{0:T(128)} %constant.167.clone.1) | copy-start | bytes 388
  11.3 26.0 %copy-start.5 = (bf16[768]{0:T(1024)(128)(2,1)S(1)}, bf16[768]{0:T(1024)(128)(2,1)}, u32[]{:S(2)}) copy-start(bf16[768]{0:T(1024)(128)(2,1)} %param.25) | copy-start | bytes 4612
  33.8 0.8 copy-start
Sparse Core Ops, SparseCore 0:
  34.7 181.8 all-gather.2

commit v10 on v9

--- a/solution.py
+++ b/solution.py
@@ -34,19 +34,18 @@
     return ref.reshape(ref.shape[0] * ref.shape[1], ref.shape[2])
 
 
-def layer_kernel(dims, spot_row_ref, got_ref, pos_ref, type_ref, vec_ref, b_qkv_ref, b_in_ref, head_ref, w_qkv_ref, w_out_ref,
+def layer_kernel(dims, spot_row_ref, rows_ref, pos_ref, type_ref, vec_ref, b_qkv_ref, b_in_ref, head_ref, w_qkv_ref, w_out_ref,
                  w_in_ref, w_back_ref, out_ref, qkv_ref, ctx_ref, x_ref):
     heads, size = dims
     seq, width = out_ref.shape[1:]
     head_ref, w_qkv_ref, w_out_ref, w_in_ref, w_back_ref = (
         flat(r) for r in (head_ref, w_qkv_ref, w_out_ref, w_in_ref, w_back_ref))
     spot = jnp.transpose(jnp.broadcast_to(spot_row_ref[0].astype(jnp.float32), (8, seq)))[:, 0:1].astype(jnp.int32)
-    total = jnp.zeros((seq, width), jnp.float32)
+    total = jnp.where(spot < head_ref.shape[0], 0.0, rows_ref[0].astype(jnp.float32))
     step = 256
-    for ref, first in ((head_ref, 0), (got_ref, head_ref.shape[0])):
-        for at in range(0, ref.shape[0], step):
-            hit = spot == lax.broadcasted_iota(jnp.int32, (seq, step), 1) + (first + at)
-            total += times(jnp.where(hit, 1.0, 0.0).astype(jnp.bfloat16), ref[at:at + step, :])
+    for at in range(0, head_ref.shape[0], step):
+        hit = spot == lax.broadcasted_iota(jnp.int32, (seq, step), 1) + at
+        total += times(jnp.where(hit, 1.0, 0.0).astype(jnp.bfloat16), head_ref[at:at + step, :])
     pos = jnp.where(spot != PAD_ID, pos_ref[2:2 + seq, :].astype(jnp.float32), pos_ref[1:2, :].astype(jnp.float32))
     embedded = total + pos + type_ref[...].astype(jnp.float32)
     x_ref[...] = norm(embedded, vec_ref[0:1, :], vec_ref[1:2, :]).astype(jnp.bfloat16)
@@ -102,21 +101,21 @@
     return out
 
 
-def layer(heads, size, batch, spot, got, pos_table, type_row, vecs, b_qkv, b_in, weights, sizes):
+def layer(heads, size, batch, spot, rows, pos_table, type_row, vecs, b_qkv, b_in, weights, sizes):
     seq = spot.shape[0] // batch
-    width = got.shape[1]
+    width = rows.shape[1]
     block = pltpu.VMEM((seq, width), jnp.bfloat16)
     return pl.pallas_call(
         functools.partial(layer_kernel, (heads, size)),
         out_shape=jax.ShapeDtypeStruct((batch, seq, width), jnp.bfloat16),
         grid=(batch,),
-        in_specs=[each(1, seq), whole(*got.shape), whole(*pos_table.shape), whole(1, width),
+        in_specs=[each(1, seq), each(seq, width), whole(*pos_table.shape), whole(1, width),
                   whole(8, width), whole(1, 3 * width), whole(1, b_in.shape[0])] + pieces(weights, sizes),
         out_specs=each(seq, width),
         scratch_shapes=[pltpu.VMEM((seq, 3 * width), jnp.bfloat16), block, block],
         compiler_params=pltpu.CompilerParams(vmem_limit_bytes=60 << 20),
         cost_estimate=pl.CostEstimate(flops=20 * 10 ** 9, bytes_accessed=15 * 10 ** 6, transcendentals=7 * 10 ** 6))(
-            spot.reshape(batch, 1, seq), got, pos_table, type_row[None, :], vecs,
+            spot.reshape(batch, 1, seq), rows.reshape(batch, seq, width), pos_table, type_row[None, :], vecs,
             b_qkv[None, :], b_in[None, :], *([weights] * len(sizes)))
 
 
@@ -419,15 +418,13 @@
             new = jnp.take(back, jnp.where(live, at_slot, 0), axis=0, mode='clip')
             return r + 1, jnp.where(live[:, None], new, rows_now)
 
-        def slow(got_now, spot_now):
-            head = weights[:, :piece.shape[0]].reshape(HEAD, width)
-            rows_now = jnp.take(jnp.concatenate([head, got_now], axis=0), spot_now, axis=0, mode='clip')
-            _, rows_now = lax.while_loop(lambda state: state[0] < rounds, again, (jnp.int32(0), rows_now))
-            return jnp.pad(rows_now, ((0, slots - n_tok), (0, 0))), jnp.where(ids == PAD_ID, spot_now, HEAD + place)
-
-        got, spot = lax.cond(rounds > 0, slow, lambda g, p: (g, p), got, spot)
+        def slow(rows_now):
+            return lax.while_loop(lambda state: state[0] < rounds, again, (jnp.int32(0), rows_now))[1]
+
+        rows = jnp.take(got, jnp.maximum(slot, 0), axis=0, mode='clip')
+        rows = lax.cond(rounds > 0, slow, lambda r: r, rows)
         vecs = jnp.stack([emb_g, emb_b, ln1_g, ln1_b, ln2_g, ln2_b, b_out_f, b_back_f])
-        return layer(num_heads, head_dim, batch_dev, spot, got, pos_table, type_row, vecs, b_qkv_f, b_in_f, weights,
+        return layer(num_heads, head_dim, batch_dev, spot, rows, pos_table, type_row, vecs, b_qkv_f, b_in_f, weights,
                      [w.shape[0] for w in parts])
 
     vec_spec = P('fsdp')

time: 296 us -> 289 us (0.976)
  the two profiles are of different devices: /device:TPU:15 before, /device:TPU:13 now
where the time goes in v10:
time: 289 us
  Pallas kernels  210 us (73%)
  local copies, waits for them, and re-layouts  46.8 us (16%)
  between operations  14.6 us (5%)
  waiting for transfers between devices  13.7 us (5%)
    pallas_call x1, Pallas kernels, swap(): pl.pallas_call(lambda *refs: swap_kernel(n, *refs), out_shape=jax.ShapeDt...  124 us
    pallas_call x1, Pallas kernels, layer(): pl.pallas_call(functools.partial(layer_kernel, (heads, size)), out_shape=...  65.7 us
    gather x1, local copies, waits for them, and re-layouts, local_step(): jnp.take(tok_shard, wanted.reshape(-1), axis=0, mode='clip')  29.3 us
    pallas_call x1, Pallas kernels, tell(): pl.pallas_call(lambda *refs: tell_kernel(n, part, *refs), out_shape=(jax....  20.4 us
    all_gather x1, waiting for transfers between devices, local_step(): lax.all_gather(jnp.concatenate(parts, axis=0), 'fsdp', axis=0, tiled=False)  13.7 us
    gather x1, local copies, waits for them, and re-layouts, local_step(): rows = jnp.take(got, jnp.maximum(slot, 0), axis=0, mode='clip')  8.68 us
  transfers between devices with their start and end apart: 1, of which 1 were waited for; matrix products, arithmetic and copies ran while one was open for 15% of the time, Pallas kernels for 43%

profile of v10, /device:TPU:13, one launch (start us, length us, event | category | flops | bytes accessed | tf_op | source)
XLA Modules:
  0.0 289.1 jit_solution(7254072088643641454)
XLA Ops:
  6.5 0.7 reshape.547
  7.3 0.0 copy-start.7
  7.3 0.0 copy-start.8
  7.3 0.0 copy-start.9
  7.3 0.0 copy-start.10
  7.3 0.0 copy-start.11
  7.3 0.0 copy-start.12
  7.4 0.0 copy-start.15
  7.4 0.0 copy-start.16
  7.4 1.3 fusion.5
  8.6 0.3 convert_reduce_fusion
  9.0 1.3 select_reduce_fusion.1
  10.3 0.1 concatenate.6
  10.4 0.6 pad_bitcast_fusion.refs_0_
  11.1 20.4 %shard_map.172 = (f32[32,16,128]{2,1,0:T(8,128)}, bf16[64,768]{1,0:T(8,128)(2,1)}) custom-call(f32[16,128]{1,0:T(8,128)} %pad_bitcast_fusion.refs_0_, bf16[15664,768]{1,0:T(8,128)(2,1)} %refs_1_.1), custom_call_target="tpu_custom_call" | custom-call | tf_op jit(solution)/shard_map/pallas_call | solution.py:208
  31.5 0.0 copy-start.17
  31.5 0.9 constant_dynamic-update-slice_fusion.1
  32.4 0.1 reshape.553
  32.6 0.8 copy-done
  33.5 0.0 all-gather.3.cloned.1.call-update
  33.5 1.0 copy.30
  34.6 0.6 fusion.10
  35.8 0.1 slice.69
  35.9 0.1 slice.68
  36.0 0.1 clamp_bitcast_fusion
  36.1 0.1 reshape.574
  36.2 29.3 %gather_fusion.2 = bf16[4864,768]{1,0:T(8,128)(2,1)} fusion(bf16[15664,768]{1,0:T(8,128)(2,1)} %refs_1_.1, s32[5120]{0:T(1024)S(1)} %pad_clamp_fusion.2), kind=kCustom, calls=%fused_computation.2 | custom fusion | bytes 14961664 | tf_op jit(solution)/shard_map/jit(_take)/gather | solution.py:400
  65.6 124.0 %shard_map.173 = bf16[1536,768]{1,0:T(8,128)(2,1)} custom-call(bf16[32,152,768]{2,1,0:T(8,128)(2,1)} %bitcast.54), custom_call_target="tpu_custom_call" | custom-call | tf_op jit(solution)/shard_map/pallas_call | solution.py:336
  189.6 0.1 fusion.25
  189.8 0.1 fusion.24
  189.9 8.7 %gather_fusion.3 = bf16[1536,768]{1,0:T(8,128)(2,1)} fusion(bf16[1536,768]{1,0:T(8,128)(2,1)} %shard_map.173, s32[2048]{0:T(1024)S(1)} %pad_clamp_fusion.3), kind=kCustom, calls=%fused_computation.3 | custom fusion | bytes 4724736 | tf_op jit(solution)/shard_map/jit(_take)/gather | solution.py:424
  198.6 0.1 fusion.28
  198.7 0.1 stack_reshape.24
  198.8 0.1 stack_reshape.25
  198.8 0.1 stack_reshape.26
  198.9 0.1 stack_reshape.27
  199.0 0.1 stack_reshape.28
  199.1 0.1 stack_reshape.29
  199.2 0.1 stack_reshape.30
  199.3 0.1 stack_reshape.31
  199.4 0.7 broadcast_in_dim_reshape.7.b_in_ref
  200.1 0.7 broadcast_in_dim_reshape.6.b_qkv_ref
  200.8 0.6 select_n.410.spot_row_ref
  201.4 0.6 broadcast_in_dim.138.type_ref
  202.0 0.2 conditional.1
  202.3 0.6 stack.3.vec_ref
  202.9 13.7 %all-gather.3.cloned.1.call-done = bf16[11264,768]{1,0:T(8,128)(2,1)} async-done(((bf16[352,768]{1,0:T(8,128)(2,1)}), bf16[11264,768]{1,0:T(8,128)(2,1)}) %all-gather.3.cloned.1.call-update) | async-done | bytes 17301520 | tf_op jit(solution)/shard_map/all_gather | solution.py:384
  216.6 65.7 %shard_map.174 = bf16[4,384,768]{2,1,0:T(8,128)(2,1)} custom-call(s32[4,1,384]{2,1,0:T(1,128)} %select_n.410.spot_row_ref, bf16[4,384,768]{2,1,0:T(8,128)(2,1)} %get-tuple-element.254.rows_ref, bf16[512,768]{1,0:T(8,128)(2,1)} %pos_ref.1, bf16[1,768]{1,0:T(2,128)(2,1)} %broadcast_in_dim.138.type_ref, f32[8,768]{1,0:T(8,128)} %stack.3.vec_ref, ...), custom_call_target="tpu_custom_call" | custom-call | flops 20000000000 | bytes 15000000 | tf_op jit(solution)/shard_map/pallas_call | solution.py:108
  (51 shorter events, 0.3 us)
Async XLA Ops:
  6.5 210.1 %all-gather.3.cloned.1.call-start = ((), (), s32[]{:S(2)}) async-start(), calls=%async_computation.2 | async-start | bytes 17842176 | tf_op jit(solution)/shard_map/all_gather | solution.py:384
  7.3 3.0 %copy-start.7 = (f32[24]{0:T(128)S(1)}, f32[24]{0:T(128)}, u32[]{:S(2)}) copy-start(f32[24]{0:T(128)} %param.26) | copy-start | bytes 292
  7.3 3.0 %copy-start.8 = (f32[24]{0:T(128)S(1)}, f32[24]{0:T(128)}, u32[]{:S(2)}) copy-start(f32[24]{0:T(128)} %param.27) | copy-start | bytes 292
  7.3 3.0 %copy-start.9 = (f32[24]{0:T(128)S(1)}, f32[24]{0:T(128)}, u32[]{:S(2)}) copy-start(f32[24]{0:T(128)} %param.32) | copy-start | bytes 292
  7.3 3.0 %copy-start.10 = (f32[24]{0:T(128)S(1)}, f32[24]{0:T(128)}, u32[]{:S(2)}) copy-start(f32[24]{0:T(128)} %param.33) | copy-start | bytes 292
  7.3 3.0 %copy-start.11 = (f32[24]{0:T(128)S(1)}, f32[24]{0:T(128)}, u32[]{:S(2)}) copy-start(f32[24]{0:T(128)} %param.38) | copy-start | bytes 292
  7.3 3.0 %copy-start.12 = (f32[24]{0:T(128)S(1)}, f32[24]{0:T(128)}, u32[]{:S(2)}) copy-start(f32[24]{0:T(128)} %param.39) | copy-start | bytes 292
  7.3 3.0 %copy-start.13 = (f32[24]{0:T(128)S(1)}, f32[24]{0:T(128)}, u32[]{:S(2)}) copy-start(f32[24]{0:T(128)} %param.31) | copy-start | bytes 292
  7.3 3.0 %copy-start.14 = (f32[24]{0:T(128)S(1)}, f32[24]{0:T(128)}, u32[]{:S(2)}) copy-start(f32[24]{0:T(128)} %param.37) | copy-start | bytes 292
  7.4 3.0 %copy-start.15 = (f32[72]{0:T(128)S(1)}, f32[72]{0:T(128)}, u32[]{:S(2)}) copy-start(f32[72]{0:T(128)} %param.29) | copy-start | bytes 868
  7.4 3.0 %copy-start.16 = (f32[96]{0:T(128)S(1)}, f32[96]{0:T(128)}, u32[]{:S(2)}) copy-start(f32[96]{0:T(128)} %param.35) | copy-start | bytes 1156
  11.0 21.3 %copy-start.4 = (bf16[12,64,24]{1,2,0:T(8,128)(2,1)S(1)}, bf16[12,64,24]{1,2,0:T(8,128)(2,1)}, u32[]{:S(2)}) copy-start(bf16[12,64,24]{1,2,0:T(8,128)(2,1)} %param.30) | copy-start | bytes 110596
  11.0 21.5 %copy-start.3 = (bf16[768,72]{0,1:T(8,128)(2,1)S(1)}, bf16[768,72]{0,1:T(8,128)(2,1)}, u32[]{:S(2)}) copy-start(bf16[768,72]{0,1:T(8,128)(2,1)} %param.28) | copy-start | bytes 331780
  11.0 21.5 %copy-start.1 = (bf16[768,96]{0,1:T(8,128)(2,1)S(1)}, bf16[768,96]{0,1:T(8,128)(2,1)}, u32[]{:S(2)}) copy-start(bf16[768,96]{0,1:T(8,128)(2,1)} %param.34) | copy-start | bytes 442372
  11.0 21.5 %copy-start.2 = (bf16[96,768]{1,0:T(8,128)(2,1)S(1)}, bf16[96,768]{1,0:T(8,128)(2,1)}, u32[]{:S(2)}) copy-start(bf16[96,768]{1,0:T(8,128)(2,1)} %param.36) | copy-start | bytes 442372
  31.5 3.1 %copy-start.17 = (f32[32]{0:T(128)S(1)}, f32[32]{0:T(128)}, u32[]{:S(2)}) copy-start(f32[32]{0:T(128)} %constant.172.clone.1) | copy-start | bytes 388
  32.6 0.8 copy-start
  65.6 124.0 %copy-start.5 = (s32[4,384]{1,0:T(4,128)S(1)}, s32[4,384]{1,0:T(4,128)}, u32[]{:S(2)}) copy-start(s32[4,384]{1,0:T(4,128)} %param.22) | copy-start | bytes 18436
  189.9 11.5 %copy-start.6 = (bf16[768]{0:T(1024)(128)(2,1)S(1)}, bf16[768]{0:T(1024)(128)(2,1)}, u32[]{:S(2)}) copy-start(bf16[768]{0:T(1024)(128)(2,1)} %param.25) | copy-start | bytes 4612
Sparse Core Ops, SparseCore 0:
  33.6 182.9 all-gather.2
